TPU v7x, 512 devices: a whole 4x8x8 slice. The times are simulated.
512 devices in a mesh: group: 32 (over z, y_hi), proc: 16 (over y_lo, x, core).
Axes of the slice: x: 4, y: 8 (y_hi: 4, y_lo: 2; y = y_hi * 2 + y_lo), z: 8, core: 2. Of those that a mesh axis runs over, the one named last changes fastest.
Arguments:
- ancestor_rows: bfloat16 [32, 256, 8192], P('group', 'proc'), may hold values from -6 to 6
- piece_owner: int32 [32], replicated, may hold values from 0 to 31, each once
- structure: int32 [32, 8], replicated, may hold values from 0 to 15, as said below
- kept_blocks: int32 [32, 7], replicated, may hold values from 0 to 7, as said below
- panel_parent: bfloat16 [32, 8, 2, 256, 512], P('group', None, None, 'proc'), may hold values from -0.09375 to 0.09375
- panel_child: bfloat16 [32, 8, 2, 256, 512], P('group', None, None, 'proc'), may hold values from -0.09375 to 0.09375
- pivot_parent: bfloat16 [32, 2, 256, 512], P('group', None, 'proc'), may hold values from -4 to 6, as said below
- pivot_child: bfloat16 [32, 2, 256, 512], P('group', None, 'proc'), may hold values from -4 to 6, as said below
Outputs:
- column_parent: bfloat16 [32, 8, 2, 256, 512], P('group', None, None, 'proc')
- block_parent: bfloat16 [32, 2, 256, 512], P('group', None, 'proc')
- column_child: bfloat16 [32, 8, 2, 256, 512], P('group', None, None, 'proc')
- block_child: bfloat16 [32, 2, 256, 512], P('group', None, 'proc')
Inputs may be any that keep to these rules, and one draw needn't show every extreme that they name: `structure`: each row names 8 different top supernodes in increasing order. `kept_blocks`: each row names 7 different positions in increasing order. `piece_owner`: a permutation. `pivot_parent`: each group's block, read as a 512 x 512 matrix, is symmetric. `pivot_child`: each group's block, read as a 512 x 512 matrix, is symmetric.
All inputs are finite; a program needn't handle non-finite values.
Results may differ from a plain program's by a relative error of at most 0.018.
Values may be sent and summed in bfloat16 or wider, within the bound.
No kernel may reach another device: no remote copies, remote signals or barrier semaphores. Data moves between devices by JAX's collectives and lax.ppermute only.
A program may use at most 64 MiB of HBM per device.

v0:
```python
import jax
import jax.numpy as jnp
from jax import lax
from jax.sharding import PartitionSpec as P


def sent_together(arrays, axis, dim, along):
    both = jnp.concatenate(arrays, axis=along)
    result, at, gathered = (lax.all_gather(both, axis, axis=dim, tiled=True), 0, [])
    for a in arrays:
        gathered.append(lax.slice_in_dim(result, at, at + a.shape[along], axis=along))
        at += a.shape[along]
    return tuple(gathered)


def split_up(shard, dim, peers):
    shape = shard.shape
    blocks = shard.reshape(*shape[:dim], peers, shape[dim] // peers, *shape[dim + 1 :])
    return jnp.moveaxis(blocks, dim, 0)


def summed_on_arrival(shard, axis, dim):
    blocks = split_up(shard, dim, lax.axis_size(axis))
    arrived = lax.all_to_all(blocks, axis, split_axis=0, concat_axis=0, tiled=True)
    return arrived.astype(jnp.float32).sum(axis=0)


def column_sums(factor, column, pieces):
    row_count = factor.shape[0]
    window = factor.reshape(row_count, pieces, -1)
    return jnp.einsum("nht,nd->thd", window, column, preferred_element_type=jnp.float32)


def per_device(
    ancestor_rows,
    piece_owner,
    structure,
    kept_blocks,
    panel_parent,
    panel_child,
    pivot_parent,
    pivot_child,
):
    group_index = lax.axis_index("group")
    owned_count, strip_rows, top_width = ancestor_rows.shape
    groups, blocks = structure.shape
    pieces = panel_parent.shape[2]
    block_width = panel_parent.shape[-1]
    top_count = top_width // block_width
    own_structure = structure[group_index]
    kept_positions = kept_blocks[group_index]
    outgoing = ancestor_rows.reshape(owned_count, strip_rows, top_count, block_width)[
        :, :, structure, :
    ]
    outgoing = outgoing.reshape(owned_count, strip_rows, groups, blocks * block_width)
    received = lax.all_to_all(outgoing, "group", split_axis=2, concat_axis=2, tiled=True)
    wanted = own_structure[:, None] * pieces + jnp.arange(pieces, dtype=jnp.int32)[None, :]
    slab_index = piece_owner[wanted]
    source = slab_index // owned_count
    within = slab_index % owned_count
    upper_left = received[within, :, source, :]
    left_parent = upper_left.reshape(blocks * pieces * strip_rows, blocks * block_width)
    local_first = panel_parent[0]
    local_second = panel_child[0]
    flat_first = local_first.reshape(-1, block_width)
    flat_second = local_second.reshape(-1, block_width)
    whole_first, whole_second = sent_together((local_first, local_second), "proc", 2, 0)
    product_parent = jnp.dot(
        left_parent, whole_first.reshape(-1, block_width), preferred_element_type=jnp.float32
    )
    column_parent = (-product_parent).astype(jnp.bfloat16)
    summed_parent = summed_on_arrival(
        column_sums(flat_first, column_parent, pieces).astype(jnp.bfloat16), "proc", 0
    )
    block_parent = (pivot_parent[0].astype(jnp.float32) - jnp.swapaxes(summed_parent, 0, 1)).astype(
        jnp.bfloat16
    )
    column_blocks = column_parent.reshape(blocks, pieces, strip_rows, block_width)
    stacked = jnp.concatenate([block_parent[None], column_blocks[kept_positions]], axis=0)
    flat_stacked = stacked.reshape(-1, block_width)
    summed_head = summed_on_arrival(
        column_sums(flat_stacked, flat_second, pieces).astype(jnp.bfloat16), "proc", 0
    )
    first_rows = jnp.swapaxes(summed_head, 0, 1)
    inner = upper_left.reshape(blocks, pieces, strip_rows, blocks, block_width)[kept_positions][
        :, :, :, kept_positions, :
    ]
    inner = inner.reshape((blocks - 1) * pieces * strip_rows, (blocks - 1) * block_width)
    left_child = jnp.concatenate([stacked[1:].reshape(-1, block_width), inner], axis=1)
    product_child = jnp.dot(
        left_child, whole_second.reshape(-1, block_width), preferred_element_type=jnp.float32
    )
    other_rows = product_child.reshape(blocks - 1, pieces, strip_rows, block_width)
    column_child = (-jnp.concatenate([first_rows[None], other_rows], axis=0)).astype(jnp.bfloat16)
    flat_child = column_child.reshape(-1, block_width)
    summed_child = summed_on_arrival(
        column_sums(flat_second, flat_child, pieces).astype(jnp.bfloat16), "proc", 0
    )
    block_child = (pivot_child[0].astype(jnp.float32) - jnp.swapaxes(summed_child, 0, 1)).astype(
        jnp.bfloat16
    )
    return (
        column_parent.reshape(1, blocks, pieces, strip_rows, block_width),
        block_parent[None],
        column_child[None],
        block_child[None],
    )


def solution(mesh):
    in_specs = (
        P("group", "proc", None),
        P(),
        P(),
        P(),
        P("group", None, None, "proc", None),
        P("group", None, None, "proc", None),
        P("group", None, "proc", None),
        P("group", None, "proc", None),
    )
    out_specs = (
        P("group", None, None, "proc", None),
        P("group", None, "proc", None),
        P("group", None, None, "proc", None),
        P("group", None, "proc", None),
    )
    return jax.shard_map(
        per_device, mesh=mesh, in_specs=in_specs, out_specs=out_specs, check_vma=False
    )
```

profile of v0, /device:TPU:1, one launch (start us, length us, event | category | flops | bytes accessed | tf_op | source)
XLA Modules:
  0.0 254.5 jit_solution(15650943294794945064)
XLA Ops:
  7.2 1.9 pad_maximum_fusion
  10.0 1.0 copy.43
  11.2 2.8 %gather_fusion = bf16[256,16,512]{2,1,0:T(8,128)(2,1)} fusion(bf16[16,16,512]{2,0,1:T(8,128)(2,1)S(1)} %copy.30, s32[1024]{0:T(1024)S(1)} %pad_clamp_fusion.2), kind=kCustom, calls=%fused_computation | custom fusion | bytes 8389632 | tf_op jit(solution)/shard_map/gather | solution.py:52
  14.0 8.5 %copy.31 = bf16[16,32,8,512]{3,2,0,1:T(8,128)(2,1)} copy(bf16[16,32,8,512]{3,0,2,1:T(8,128)(2,1)} %bitcast.90) | data formatting | bytes 8388608 | tf_op jit(solution)/shard_map/gather | solution.py:52
  22.4 7.4 %reshape.186 = bf16[1,16,32,4096]{3,1,0,2:T(8,128)(2,1)} reshape(bf16[16,32,8,512]{3,2,0,1:T(8,128)(2,1)} %copy.31) | data formatting | bytes 8388608 | tf_op jit(solution)/shard_map/reshape | solution.py:55
  29.8 16.8 %all-to-all-start = ((bf16[1,16,32,4096]{3,1,0,2:T(8,128)(2,1)}), bf16[1,16,32,4096]{3,1,0,2:T(8,128)(2,1)}, u32[]{:S(2)}, u32[]{:S(2)}) async-start(bf16[1,16,32,4096]{3,1,0,2:T(8,128)(2,1)} %reshape.186), calls=%async_computation | async-start | bytes 8388608 | tf_op jit(solution)/shard_map/all_to_all | solution.py:56
  48.1 136.0 %all-to-all-done = bf16[1,16,32,4096]{3,1,0,2:T(8,128)(2,1)} async-done(((bf16[1,16,32,4096]{3,1,0,2:T(8,128)(2,1)}), bf16[1,16,32,4096]{3,1,0,2:T(8,128)(2,1)}, u32[]{:S(2)}, u32[]{:S(2)}) %all-to-all-start) | async-done | bytes 4194336 | tf_op jit(solution)/shard_map/all_to_all | solution.py:56
  184.1 2.9 %gather_fusion.2 = bf16[16,16,4096]{2,1,0:T(8,128)(2,1)S(1)} fusion(bf16[1,16,32,4096]{3,1,2,0:T(8,128)(2,1)} %bitcast.2, s32[16]{0:T(128)S(1)} %reshape.216), kind=kCustom, calls=%fused_computation.2 | custom fusion | bytes 4194432 | tf_op jit(solution)/shard_map/gather | solution.py:61
  187.0 5.1 %fusion.19 = (bf16[8,2,256,512]{3,2,1,0:T(8,128)(2,1)}, bf16[8,2,256,512]{3,2,1,0:T(8,128)(2,1)S(1)}) fusion(bf16[16,2,256,512]{3,2,1,0:T(8,128)(2,1)} %all-gather.2.cloned.1.call-done), kind=kLoop, calls=%fused_computation.47 | loop fusion | bytes 16777216 | tf_op jit(solution)/shard_map/slice | solution.py:11
  192.1 1.3 fusion.4
  193.8 0.8 copy.34
  194.6 4.4 %all-to-all-start.1 = ((bf16[16,16,2,512]{3,1,2,0:T(8,128)(2,1)}), bf16[16,16,2,512]{3,1,2,0:T(8,128)(2,1)S(1)}, u32[]{:S(2)}, u32[]{:S(2)}) async-start(bf16[16,16,2,512]{3,1,2,0:T(8,128)(2,1)} %copy.34), calls=%async_computation.1 | async-start | bytes 1048576 | tf_op jit(solution)/shard_map/all_to_all | solution.py:24
  199.8 9.0 %all-to-all-done.1 = bf16[16,16,2,512]{3,1,2,0:T(8,128)(2,1)S(1)} async-done(((bf16[16,16,2,512]{3,1,2,0:T(8,128)(2,1)}), bf16[16,16,2,512]{3,1,2,0:T(8,128)(2,1)S(1)}, u32[]{:S(2)}, u32[]{:S(2)}) %all-to-all-start.1) | async-done | bytes 524320 | tf_op jit(solution)/shard_map/all_to_all | solution.py:24
  209.4 0.8 copy.36
  210.2 5.2 %all-to-all-start.2 = ((bf16[16,16,2,512]{3,1,2,0:T(8,128)(2,1)}), bf16[16,16,2,512]{3,1,2,0:T(8,128)(2,1)}, u32[]{:S(2)}, u32[]{:S(2)}) async-start(bf16[16,16,2,512]{3,1,2,0:T(8,128)(2,1)} %copy.36), calls=%async_computation.2 | async-start | bytes 1048576 | tf_op jit(solution)/shard_map/all_to_all | solution.py:24
  216.2 2.3 copy.44
  218.5 3.5 %gather_fusion.4 = bf16[7,2,16,8,512]{4,3,2,1,0:T(8,128)(2,1)} fusion(bf16[8,2,16,8,512]{4,3,2,1,0:T(8,128)(2,1)} %bitcast.93, s32[1024]{0:T(1024)S(1)} %pad_clamp_fusion), kind=kCustom, calls=%fused_computation.4 | custom fusion | bytes 3670044 | tf_op jit(solution)/shard_map/gather | solution.py:85
  222.0 2.2 copy.37
  225.0 0.8 copy-done.7
  225.8 3.3 %fusion = f32[7,2,16,512]{3,2,1,0:T(8,128)S(1)} fusion(bf16[4096,512,1,1]{1,0,3,2:T(8,128)(2,1)} %bitcast.95, bf16[7,2,16,3584]{3,2,1,0:T(8,128)(2,1)S(1)} %bitcast.103, bf16[7,2,16,512]{3,2,1,0:T(8,128)(2,1)S(1)} %copy-done.7), kind=kOutput, calls=%fused_computation.6 | convolution fusion | flops 943194112 | bytes 6488064 | tf_op jit(solution)/shard_map/dot_general | solution.py:90
  229.1 1.1 convert_reduce_fusion.1
  230.7 0.8 copy.40
  231.5 5.8 %all-to-all-start.3 = ((bf16[16,16,2,512]{3,1,2,0:T(8,128)(2,1)}), bf16[16,16,2,512]{3,1,2,0:T(8,128)(2,1)S(1)}, u32[]{:S(2)}, u32[]{:S(2)}) async-start(bf16[16,16,2,512]{3,1,2,0:T(8,128)(2,1)} %copy.40), calls=%async_computation.3 | async-start | bytes 1048576 | tf_op jit(solution)/shard_map/all_to_all | solution.py:24
  238.0 8.9 %all-to-all-done.3 = bf16[16,16,2,512]{3,1,2,0:T(8,128)(2,1)S(1)} async-done(((bf16[16,16,2,512]{3,1,2,0:T(8,128)(2,1)}), bf16[16,16,2,512]{3,1,2,0:T(8,128)(2,1)S(1)}, u32[]{:S(2)}, u32[]{:S(2)}) %all-to-all-start.3) | async-done | bytes 524320 | tf_op jit(solution)/shard_map/all_to_all | solution.py:24
  (59 shorter events, 7.6 us)
Async XLA Ops:
  7.2 191.9 %copy-start = (s32[32,7]{0,1:T(8,128)S(1)}, s32[32,7]{0,1:T(8,128)}, u32[]{:S(2)}) copy-start(s32[32,7]{0,1:T(8,128)} %param.11) | copy-start | bytes 2692
  7.2 179.8 %all-gather.2.cloned.1.call-start = ((), (), s32[]{:S(2)}) async-start(), calls=%async_computation.4 | async-start | bytes 8912896 | tf_op jit(solution)/shard_map/all_gather | solution.py:9
  29.8 16.8 %copy-start.3 = (bf16[1,8,2,16,512]{4,3,2,1,0:T(8,128)(2,1)S(1)}, bf16[1,8,2,16,512]{4,3,2,1,0:T(8,128)(2,1)}, u32[]{:S(2)}) copy-start(bf16[1,8,2,16,512]{4,3,2,1,0:T(8,128)(2,1)} %param.12) | copy-start | bytes 786436
  29.8 16.9 %copy-start.11 = (s32[32,8]{0,1:T(8,128)S(1)}, s32[32,8]{0,1:T(8,128)}, u32[]{:S(2)}) copy-start(s32[32,8]{0,1:T(8,128)} %param.10) | copy-start | bytes 3076
  29.8 154.3 %all-to-all-start = ((bf16[1,16,32,4096]{3,1,0,2:T(8,128)(2,1)}), bf16[1,16,32,4096]{3,1,0,2:T(8,128)(2,1)}, u32[]{:S(2)}, u32[]{:S(2)}) async-start(bf16[1,16,32,4096]{3,1,0,2:T(8,128)(2,1)} %reshape.186), calls=%async_computation | async-start | bytes 8388608 | tf_op jit(solution)/shard_map/all_to_all | solution.py:56
  46.6 0.7 copy-start.1
  193.4 15.5 %copy-start.5 = (bf16[256,512]{1,0:T(8,128)(2,1)}, bf16[256,512]{1,0:T(8,128)(2,1)S(1)}, u32[]{:S(2)}) copy-start(bf16[256,512]{1,0:T(8,128)(2,1)S(1)} %fusion.4) | copy-start | bytes 786436
  193.4 15.5 %copy-start.9 = (bf16[1,2,16,512]{3,2,1,0:T(8,128)(2,1)S(1)}, bf16[1,2,16,512]{3,2,1,0:T(8,128)(2,1)}, u32[]{:S(2)}) copy-start(bf16[1,2,16,512]{3,2,1,0:T(8,128)(2,1)} %param.14) | copy-start | bytes 98308
  193.8 15.3 %copy-start.2 = (bf16[1,8,2,16,512]{4,3,2,1,0:T(8,128)(2,1)S(1)}, bf16[1,8,2,16,512]{4,3,2,1,0:T(8,128)(2,1)}, u32[]{:S(2)}) copy-start(bf16[1,8,2,16,512]{4,3,2,1,0:T(8,128)(2,1)} %param.13) | copy-start | bytes 786436
  194.6 14.2 %all-to-all-start.1 = ((bf16[16,16,2,512]{3,1,2,0:T(8,128)(2,1)}), bf16[16,16,2,512]{3,1,2,0:T(8,128)(2,1)S(1)}, u32[]{:S(2)}, u32[]{:S(2)}) async-start(bf16[16,16,2,512]{3,1,2,0:T(8,128)(2,1)} %copy.34), calls=%async_computation.1 | async-start | bytes 1048576 | tf_op jit(solution)/shard_map/all_to_all | solution.py:24
  199.8 10.4 %copy-start.6 = (bf16[7,2,16,512]{3,2,1,0:T(8,128)(2,1)}, bf16[7,2,16,512]{3,2,1,0:T(8,128)(2,1)S(1)}, u32[]{:S(2)}) copy-start(bf16[7,2,16,512]{3,2,1,0:T(8,128)(2,1)S(1)} %gather_fusion.3) | copy-start | bytes 688132
  208.9 1.3 copy-start.8
  210.2 18.9 %all-to-all-start.2 = ((bf16[16,16,2,512]{3,1,2,0:T(8,128)(2,1)}), bf16[16,16,2,512]{3,1,2,0:T(8,128)(2,1)}, u32[]{:S(2)}, u32[]{:S(2)}) async-start(bf16[16,16,2,512]{3,1,2,0:T(8,128)(2,1)} %copy.36), calls=%async_computation.2 | async-start | bytes 1048576 | tf_op jit(solution)/shard_map/all_to_all | solution.py:24
  224.8 0.9 copy-start.7
  225.8 4.5 %copy-start.4 = (bf16[256,2,256]{2,1,0:T(2,128)(2,1)S(1)}, bf16[256,2,256]{2,1,0:T(2,128)(2,1)}, u32[]{:S(2)}) copy-start(bf16[256,2,256]{2,1,0:T(2,128)(2,1)} %reshape_reshape_squeeze.7) | copy-start | bytes 786436
  230.3 16.7 %copy-start.10 = (bf16[1,2,16,512]{3,2,1,0:T(8,128)(2,1)S(1)}, bf16[1,2,16,512]{3,2,1,0:T(8,128)(2,1)}, u32[]{:S(2)}) copy-start(bf16[1,2,16,512]{3,2,1,0:T(8,128)(2,1)} %param.15) | copy-start | bytes 98308
  231.5 15.5 %all-to-all-start.3 = ((bf16[16,16,2,512]{3,1,2,0:T(8,128)(2,1)}), bf16[16,16,2,512]{3,1,2,0:T(8,128)(2,1)S(1)}, u32[]{:S(2)}, u32[]{:S(2)}) async-start(bf16[16,16,2,512]{3,1,2,0:T(8,128)(2,1)} %copy.40), calls=%async_computation.3 | async-start | bytes 1048576 | tf_op jit(solution)/shard_map/all_to_all | solution.py:24
Sparse Core Ops, SparseCore 0:
  10.1 121.0 all-gather.1
where the time goes:
time: 258 us; the launch traced here: 255 us
  waiting for transfers between devices  154 us (60%)
  local copies, waits for them, and re-layouts  42.7 us (17%)
  starting transfers between devices  32.3 us (13%)
  between operations  14.3 us (6%)
  matrix products  5.64 us (2%)
  other arithmetic  5.61 us (2%)
    all_to_all x1, waiting for transfers between devices, per_device(): lax.all_to_all(outgoing, 'group', split_axis=2, concat_axis=2, tiled=True)  136 us
    all_to_all x3, waiting for transfers between devices, summed_on_arrival(): lax.all_to_all(blocks, axis, split_axis=0, concat_axis=0, tiled=True)  17.9 us
    all_to_all x1, starting transfers between devices, per_device(): lax.all_to_all(outgoing, 'group', split_axis=2, concat_axis=2, tiled=True)  16.8 us
    all_to_all x3, starting transfers between devices, summed_on_arrival(): lax.all_to_all(blocks, axis, split_axis=0, concat_axis=0, tiled=True)  15.5 us
    gather x2, local copies, waits for them, and re-layouts, per_device(): ancestor_rows.reshape(owned_count, strip_rows, top_count, block_width)  11.2 us
    reshape x1, local copies, waits for them, and re-layouts, per_device(): outgoing.reshape(owned_count, strip_rows, groups, blocks * block_width)  7.39 us
    gather x3, local copies, waits for them, and re-layouts, per_device(): upper_left.reshape(blocks, pieces, strip_rows, blocks, block_width)  6.34 us
  transfers between devices with their start and end apart: 5, of which 3 were waited for; matrix products, arithmetic and copies ran while one was open for 15% of the time, Pallas kernels for 0%

commit v1 on v0

v1 whole, which is shorter than its diff:
```python
import jax
import jax.numpy as jnp
from jax import lax
from jax.experimental import pallas as pl
from jax.experimental.pallas import tpu as pltpu
from jax.sharding import PartitionSpec as P

INTERPRET = False
F32 = jnp.float32
BF16 = jnp.bfloat16


def dot(a, b):
    return jnp.dot(a, b, preferred_element_type=F32)


def dot_rows(a, b):
    return lax.dot_general(a, b, (((0,), (0,)), ((), ())), preferred_element_type=F32)


def products_kernel(kept, upper, panels, own_first, own_second, pivot, column_out, child_out, sums_out):
    strip, pieces, blocks, slabs, half = upper.shape
    procs, width = panels.shape[0], panels.shape[-1]
    rows = strip * slabs

    def left(h, b):
        return upper[:, h, b].reshape(rows, half)

    def right(n, b, h):
        return panels[:, n, b, h].reshape(half, width)

    total = jnp.zeros((rows, width), F32)
    for b in range(blocks):
        for h in range(pieces):
            total += dot(left(h, b), right(0, b, h))
    column = (-total).astype(BF16)
    at = lax.broadcasted_iota(jnp.int32, (rows, rows), 0)
    of = lax.broadcasted_iota(jnp.int32, (rows, rows), 1)
    same_row = (at % strip == of // slabs) & ((at // strip) % pieces == of % pieces)
    to_block = at // (strip * pieces)
    of_block = (of % slabs) // pieces
    wanted = jnp.full((rows, rows), -1, jnp.int32)
    for b in range(1, blocks):
        wanted = jnp.where(to_block == b, kept[b - 1], wanted)
    in_order = (same_row & (to_block == of_block)).astype(F32).astype(BF16)
    in_child = (same_row & (wanted == of_block)).astype(F32).astype(BF16)
    column_natural = dot(in_order, column).astype(BF16)
    column_kept = dot(in_child, column).astype(BF16)
    column_out[...] = column_natural.reshape(column_out.shape)

    top = [right(1, 0, h) for h in range(pieces)]
    total = jnp.zeros((rows, width), F32)
    for b in range(1, blocks):
        for h in range(pieces):
            total += dot(left(h, kept[b - 1]), right(1, b, h))
    for h in range(pieces):
        total += dot(column[:, h * half : (h + 1) * half], top[h])
    child = dot(in_child, (-total).astype(BF16)).astype(BF16)
    child_out[...] = child.reshape(child_out.shape)

    first = own_first[...].reshape(rows, width)
    second = own_second[...].reshape(rows, width)
    diagonal = pivot[...].reshape(strip * pieces, width)
    parent_sum = dot_rows(first, column_natural)
    cross = jnp.zeros((rows, width), F32)
    for h in range(pieces):
        cross += dot(first[:, h * half : (h + 1) * half], top[h])
    head_sum = (
        dot_rows(column_kept, second)
        - dot_rows(column_natural, cross.astype(BF16))
        + dot_rows(diagonal, second[: strip * pieces])
    ).astype(BF16)
    child_sum = -dot_rows(second, child)
    for h in range(pieces):
        child_sum += dot_rows(top[h], head_sum[h * half : (h + 1) * half])
    for n, value in enumerate((parent_sum.astype(BF16), head_sum, child_sum.astype(BF16))):
        for h in range(pieces):
            for p in range(procs):
                start = h * half + p * strip
                sums_out[p, n, h] = value[start : start + strip]


def final_kernel(arrived, pivot_first, pivot_second, child_in, block_first, child_out, block_second):
    del child_in
    sums = [arrived[0, n].astype(F32) for n in range(3)]
    for p in range(1, arrived.shape[0]):
        for n in range(3):
            sums[n] += arrived[p, n].astype(F32)
    block_first[...] = (pivot_first[...].astype(F32) - sums[0]).astype(BF16)
    child_out[0] = (-sums[1]).astype(BF16)
    block_second[...] = (pivot_second[...].astype(F32) + sums[2]).astype(BF16)


def per_device(
    ancestor_rows,
    piece_owner,
    structure,
    kept_blocks,
    panel_parent,
    panel_child,
    pivot_parent,
    pivot_child,
):
    group_index = lax.axis_index("group")
    strip = ancestor_rows.shape[1]
    groups, blocks = structure.shape
    procs = lax.axis_size("proc")
    pieces = panel_parent.shape[2]
    width = panel_parent.shape[-1]
    half = width // pieces
    tops = ancestor_rows.shape[2] // width
    slabs = blocks * pieces

    panels = lax.all_gather(jnp.stack([panel_parent[0], panel_child[0]]), "proc", axis=0)

    spread = ancestor_rows.reshape(strip, tops, pieces, half).transpose(0, 2, 1, 3)
    spread = lax.all_to_all(
        spread.reshape(groups, tops, half), "group", split_axis=0, concat_axis=0, tiled=True
    )
    wanted = structure[:, :, None] * pieces + jnp.arange(pieces, dtype=jnp.int32)
    owner = piece_owner[wanted.reshape(groups, slabs)]
    index = owner[:, None, :] * tops + structure[:, :, None]
    choice = jax.nn.one_hot(index.reshape(-1), groups * tops, dtype=BF16)
    outgoing = jnp.dot(choice, spread.reshape(groups * tops, half), preferred_element_type=BF16)
    upper = lax.all_to_all(
        outgoing.reshape(groups, blocks, slabs, half), "group", split_axis=0, concat_axis=0, tiled=True
    ).reshape(strip, pieces, blocks, slabs, half)

    vmem = pl.BlockSpec(memory_space=pltpu.VMEM)
    column_parent, column_child, sums = pl.pallas_call(
        products_kernel,
        out_shape=(
            jax.ShapeDtypeStruct((blocks, pieces, strip, width), BF16),
            jax.ShapeDtypeStruct((blocks, pieces, strip, width), BF16),
            jax.ShapeDtypeStruct((procs, 3, pieces, strip, width), BF16),
        ),
        in_specs=[pl.BlockSpec(memory_space=pltpu.SMEM)] + [vmem] * 5,
        out_specs=(vmem, vmem, vmem),
        interpret=INTERPRET,
        name="products",
    )(kept_blocks[group_index], upper, panels, panel_parent[0], panel_child[0], pivot_parent[0])
    arrived = lax.all_to_all(sums, "proc", split_axis=0, concat_axis=0, tiled=True)
    whole = pl.BlockSpec((pieces, strip, width), lambda i: (0, 0, 0))
    block_parent, column_child, block_child = pl.pallas_call(
        final_kernel,
        grid=(1,),
        out_shape=(
            jax.ShapeDtypeStruct((pieces, strip, width), BF16),
            jax.ShapeDtypeStruct((blocks, pieces, strip, width), BF16),
            jax.ShapeDtypeStruct((pieces, strip, width), BF16),
        ),
        in_specs=[
            pl.BlockSpec(arrived.shape, lambda i: (0, 0, 0, 0, 0)),
            whole,
            whole,
            pl.BlockSpec(memory_space=pl.ANY),
        ],
        out_specs=(whole, pl.BlockSpec((1, pieces, strip, width), lambda i: (0, 0, 0, 0)), whole),
        input_output_aliases={3: 1},
        interpret=INTERPRET,
        name="final",
    )(arrived, pivot_parent[0], pivot_child[0], column_child)
    return column_parent[None], block_parent[None], column_child[None], block_child[None]


def solution(mesh):
    in_specs = (
        P("group", "proc", None),
        P(),
        P(),
        P(),
        P("group", None, None, "proc", None),
        P("group", None, None, "proc", None),
        P("group", None, "proc", None),
        P("group", None, "proc", None),
    )
    out_specs = (
        P("group", None, None, "proc", None),
        P("group", None, "proc", None),
        P("group", None, None, "proc", None),
        P("group", None, "proc", None),
    )
    return jax.shard_map(
        per_device, mesh=mesh, in_specs=in_specs, out_specs=out_specs, check_vma=False
    )
```

time: 258 us -> 169 us (0.66); the launches traced: 255 us -> 169 us
  waiting for transfers between devices: 154 us -> 81.1 us
  local copies, waits for them, and re-layouts: 42.7 us -> 7.7 us
  blocking collectives: 0 us -> 27.1 us
  Pallas kernels: 0 us -> 11.4 us
  starting transfers between devices: 32.3 us -> 22.7 us
  other arithmetic: 5.61 us -> 2.08 us
  matrix products: 5.64 us -> 2.71 us
    all_to_all x4 -> x2, waiting for transfers between devices: 154 us -> 81.1 us  [the longest x1 72.8 us: per_device(): lax.all_to_all(outgoing.reshape(groups, blocks, slabs, half), 'group', sp...]
    all_to_all x0 -> x1, blocking collectives: none -> 27.1 us  [per_device(): lax.all_to_all(sums, 'proc', split_axis=0, concat_axis=0, tiled=True)]
    gather x9 -> x1, local copies, waits for them, and re-layouts: 21.7 us -> 3.34 us  [per_device(): owner = piece_owner[wanted.reshape(groups, slabs)]]
    pallas_call x0 -> x2, Pallas kernels: none -> 11.4 us  [the longest x1 9.14 us: per_device(): pl.pallas_call(products_kernel, out_shape=(jax.ShapeDtypeStruct((blocks,...]
    all_to_all x4 -> x2, starting transfers between devices: 32.3 us -> 22.6 us  [the longest x1 16.5 us: per_device(): lax.all_to_all(spread.reshape(groups, tops, half), 'group', split_axis=0,...]
    reshape x5 -> x1, local copies, waits for them, and re-layouts: 10 us -> 1.15 us  [per_device(): ancestor_rows.reshape(strip, tops, pieces, half).transpose(0, 2, 1, 3)]
    slice x1 -> x0, local copies, waits for them, and re-layouts: 5.09 us -> none  [sent_together(): lax.slice_in_dim(result, at, at + a.shape[along], axis=along)]
    dot_general x5 -> x1, matrix products: 5.64 us -> 2.71 us  [per_device(): jnp.dot(choice, spread.reshape(groups * tops, half), preferred_element_ty...]
  transfers between devices with their start and end apart: 5 -> 3, of which waited for: 3 -> 2; matrix products, arithmetic and copies ran while one was open for 15% -> 5% of each run, Pallas kernels for 0% -> 0%
where the time goes in v1:
time: 169 us
  waiting for transfers between devices  81.1 us (48%)
  blocking collectives  27.1 us (16%)
  starting transfers between devices  22.7 us (13%)
  between operations  14.1 us (8%)
  Pallas kernels  11.4 us (7%)
  local copies, waits for them, and re-layouts  7.7 us (5%)
  matrix products  2.71 us (2%)
  other arithmetic  2.08 us (1%)
    all_to_all x1, waiting for transfers between devices, per_device(): lax.all_to_all(outgoing.reshape(groups, blocks, slabs, half), 'group', sp...  72.8 us
    all_to_all x1, blocking collectives, per_device(): lax.all_to_all(sums, 'proc', split_axis=0, concat_axis=0, tiled=True)  27.1 us
    all_to_all x1, starting transfers between devices, per_device(): lax.all_to_all(spread.reshape(groups, tops, half), 'group', split_axis=0,...  16.5 us
    pallas_call x1, Pallas kernels, per_device(): pl.pallas_call(products_kernel, out_shape=(jax.ShapeDtypeStruct((blocks,...  9.14 us
    all_to_all x1, waiting for transfers between devices, per_device(): lax.all_to_all(spread.reshape(groups, tops, half), 'group', split_axis=0,...  8.25 us
    all_to_all x1, starting transfers between devices, per_device(): lax.all_to_all(outgoing.reshape(groups, blocks, slabs, half), 'group', sp...  6.11 us
  transfers between devices with their start and end apart: 3, of which 2 were waited for; matrix products, arithmetic and copies ran while one was open for 5% of the time, Pallas kernels for 0%

profile of v1, /device:TPU:1, one launch (start us, length us, event | category | flops | bytes accessed | tf_op | source)
XLA Modules:
  0.0 168.9 jit_solution(15092534639762023906)
XLA Ops:
  7.2 0.0 copy-start
  7.2 0.0 all-gather.3.cloned.1.call-start
  7.2 1.9 %pad_maximum_fusion = bf16[2,8,2,16,512]{4,3,2,1,0:T(8,128)(2,1)} fusion(bf16[1,8,2,16,512]{4,3,2,1,0:T(8,128)(2,1)} %param.13, bf16[1,8,2,16,512]{4,3,2,1,0:T(8,128)(2,1)} %param.12), kind=kLoop, calls=%fused_computation.5 | loop fusion | flops 262144 | bytes 1048576 | tf_op jit(solution)/shard_map/stack | solution.py:114
  9.1 0.0 all-gather.3.cloned.1.call-update
  9.2 1.1 reshape.114
  10.3 0.7 copy.21
  11.1 16.5 %all-to-all-start = ((bf16[32,16,256]{2,1,0:T(8,128)(2,1)}), bf16[32,16,256]{2,1,0:T(8,128)(2,1)S(1)}, u32[]{:S(2)}, u32[]{:S(2)}) async-start(bf16[32,16,256]{2,1,0:T(8,128)(2,1)} %bitcast.3), calls=%async_computation | async-start | bytes 524288 | tf_op jit(solution)/shard_map/all_to_all | solution.py:117
  27.6 0.1 add.64
  27.7 0.1 compare_select_fusion
  27.8 0.1 copy.19
  27.8 0.1 reshape.120
  27.9 0.1 copy.20
  28.0 3.3 %gather_fusion = s32[512]{0:T(512)S(1)} fusion(s32[32]{0:T(128)S(1)} %copy-done.1, s32[1024]{0:T(1024)S(1)} %pad_clamp_fusion), kind=kCustom, calls=%fused_computation | custom fusion | bytes 6144 | tf_op jit(solution)/shard_map/gather | solution.py:121
  31.4 0.1 reshape.129
  31.4 0.1 broadcast_add_fusion
  31.5 8.2 %all-to-all-done = bf16[32,16,256]{2,1,0:T(8,128)(2,1)S(1)} async-done(((bf16[32,16,256]{2,1,0:T(8,128)(2,1)}), bf16[32,16,256]{2,1,0:T(8,128)(2,1)S(1)}, u32[]{:S(2)}, u32[]{:S(2)}) %all-to-all-start) | async-done | bytes 262176 | tf_op jit(solution)/shard_map/all_to_all | solution.py:117
  39.8 2.7 %fusion.1 = bf16[32,8,16,256]{3,2,1,0:T(8,128)(2,1)} fusion(bf16[512,256,1,1]{1,0,3,2:T(8,128)(2,1)S(1)} %bitcast.29, s32[32,8,16]{2,1,0:T(8,128)S(1)} %broadcast_add_fusion), kind=kOutput, calls=%fused_computation.3 | convolution fusion | flops 1075838976 | bytes 2375680 | tf_op jit(solution)/shard_map/dot_general | solution.py:124
  42.5 6.1 %all-to-all-start.1 = ((bf16[32,8,16,256]{3,2,1,0:T(8,128)(2,1)}), bf16[32,8,16,256]{3,2,1,0:T(8,128)(2,1)S(1)}, u32[]{:S(2)}, u32[]{:S(2)}) async-start(bf16[32,8,16,256]{3,2,1,0:T(8,128)(2,1)} %fusion.1), calls=%async_computation.1 | async-start | bytes 4194304 | tf_op jit(solution)/shard_map/all_to_all | solution.py:125
  48.6 0.7 dynamic-slice_reduce_fusion.kept
  49.3 72.8 %all-to-all-done.1 = bf16[32,8,16,256]{3,2,1,0:T(8,128)(2,1)S(1)} async-done(((bf16[32,8,16,256]{3,2,1,0:T(8,128)(2,1)}), bf16[32,8,16,256]{3,2,1,0:T(8,128)(2,1)S(1)}, u32[]{:S(2)}, u32[]{:S(2)}) %all-to-all-start.1) | async-done | bytes 2097184 | tf_op jit(solution)/shard_map/all_to_all | solution.py:125
  122.2 1.4 copy-done.2
  123.5 9.1 %products.1 = (bf16[8,2,16,512]{3,2,1,0:T(8,128)(2,1)}, bf16[8,2,16,512]{3,2,1,0:T(8,128)(2,1)}, bf16[16,3,2,16,512]{4,3,2,1,0:T(8,128)(2,1)}) custom-call(s32[7]{0:T(128)} %dynamic-slice_reduce_fusion.kept, bf16[16,2,8,16,256]{4,3,2,1,0:T(8,128)(2,1)} %bitcast.25, bf16[16,2,8,2,16,512]{5,4,3,2,1,0:T(8,128)(2,1)} %bitcast.24, ...), custom_call_target="tpu_custom_call" | custom-call | tf_op jit(solution)/shard_map/products/pallas_call | solution.py:130
  132.6 27.1 %all_to_all.15.arrived = bf16[16,3,2,16,512]{4,3,2,1,0:T(8,128)(2,1)} all-to-all(bf16[16,3,2,16,512]{4,3,2,1,0:T(8,128)(2,1)} %get-tuple-element.11), channel_id=1, replica_groups=mesh['group'=32,'proc'=16] {'proc'}, dimensions={0} | all-to-all | bytes 3145728 | tf_op jit(solution)/shard_map/all_to_all | solution.py:142
  159.8 2.3 %final.1 = (bf16[2,16,512]{2,1,0:T(8,128)(2,1)}, bf16[8,2,16,512]{3,2,1,0:T(8,128)(2,1)}, bf16[2,16,512]{2,1,0:T(8,128)(2,1)}) custom-call(bf16[16,3,2,16,512]{4,3,2,1,0:T(8,128)(2,1)} %all_to_all.15.arrived, bf16[2,16,512]{2,1,0:T(8,128)(2,1)} %bitcast.32, bf16[2,16,512]{2,1,0:T(8,128)(2,1)} %bitcast.34, ...), custom_call_target="tpu_custom_call", output_to_operand_aliasing={{1}: (3, {})} | custom-call | tf_op jit(solution)/shard_map/final/pallas_call | solution.py:144
  (12 shorter events, 0.0 us)
Async XLA Ops:
  7.2 41.5 %copy-start = (s32[32,7]{0,1:T(8,128)S(1)}, s32[32,7]{0,1:T(8,128)}, u32[]{:S(2)}) copy-start(s32[32,7]{0,1:T(8,128)} %param.11) | copy-start | bytes 2692
  7.2 20.5 %copy-start.3 = (s32[32,8]{0,1:T(8,128)S(1)}, s32[32,8]{0,1:T(8,128)}, u32[]{:S(2)}) copy-start(s32[32,8]{0,1:T(8,128)} %param.10) | copy-start | bytes 3076
  7.2 20.8 %copy-start.1 = (s32[32]{0:T(128)S(1)}, s32[32]{0:T(128)}, u32[]{:S(2)}) copy-start(s32[32]{0:T(128)} %param.9) | copy-start | bytes 388
  7.2 115.0 %all-gather.3.cloned.1.call-start = ((), (), s32[]{:S(2)}) async-start(), calls=%async_computation.3 | async-start | bytes 8912896 | tf_op jit(solution)/shard_map/all_gather | solution.py:114
  11.1 28.7 %all-to-all-start = ((bf16[32,16,256]{2,1,0:T(8,128)(2,1)}), bf16[32,16,256]{2,1,0:T(8,128)(2,1)S(1)}, u32[]{:S(2)}, u32[]{:S(2)}) async-start(bf16[32,16,256]{2,1,0:T(8,128)(2,1)} %bitcast.3), calls=%async_computation | async-start | bytes 524288 | tf_op jit(solution)/shard_map/all_to_all | solution.py:117
  42.5 79.6 %all-to-all-start.1 = ((bf16[32,8,16,256]{3,2,1,0:T(8,128)(2,1)}), bf16[32,8,16,256]{3,2,1,0:T(8,128)(2,1)S(1)}, u32[]{:S(2)}, u32[]{:S(2)}) async-start(bf16[32,8,16,256]{3,2,1,0:T(8,128)(2,1)} %fusion.1), calls=%async_computation.1 | async-start | bytes 4194304 | tf_op jit(solution)/shard_map/all_to_all | solution.py:125
  122.1 1.4 copy-start.2
Sparse Core Ops, SparseCore 0:
  10.1 110.5 all-gather.2

commit v2 on v1

--- a/solution.py
+++ b/solution.py
@@ -5,7 +5,10 @@
 from jax.experimental.pallas import tpu as pltpu
 from jax.sharding import PartitionSpec as P
 
+
 INTERPRET = False
+YS, XS, CORES = 2, 4, 2
+PROCS = YS * XS * CORES
 F32 = jnp.float32
 BF16 = jnp.bfloat16
 
@@ -18,16 +21,19 @@
     return lax.dot_general(a, b, (((0,), (0,)), ((), ())), preferred_element_type=F32)
 
 
-def products_kernel(kept, upper, panels, own_first, own_second, pivot, column_out, child_out, sums_out):
+def products_kernel(kept, upper, mine, theirs, own_first, own_second, pivot, column_out, child_out, sums_out):
     strip, pieces, blocks, slabs, half = upper.shape
-    procs, width = panels.shape[0], panels.shape[-1]
+    procs, width = CORES * mine.shape[0], mine.shape[-1]
+    first_core = kept[blocks - 1] == 0
     rows = strip * slabs
 
     def left(h, b):
         return upper[:, h, b].reshape(rows, half)
 
     def right(n, b, h):
-        return panels[:, n, b, h].reshape(half, width)
+        a, b = mine[:, n, b, h], theirs[:, n, b, h]
+        pair = jnp.stack([jnp.where(first_core, a, b), jnp.where(first_core, b, a)], axis=1)
+        return pair.reshape(half, width)
 
     total = jnp.zeros((rows, width), F32)
     for b in range(blocks):
@@ -91,6 +97,39 @@
     block_second[...] = (pivot_second[...].astype(F32) + sums[2]).astype(BF16)
 
 
+def moved(value, step):
+    pairs = []
+    for p in range(PROCS):
+        y, x, core = p // (XS * CORES), p // CORES % XS, p % CORES
+        y, x, core = (y + step[0]) % YS, (x + step[1]) % XS, (core + step[2]) % CORES
+        pairs.append((p, (y * XS + x) * CORES + core))
+    return lax.ppermute(value, "proc", pairs)
+
+
+def placed(buffer, value, where):
+    return lax.dynamic_update_slice(buffer, value, tuple(where) + (0,) * (buffer.ndim - len(where)))
+
+
+def shifted(shard):
+    here = lax.axis_index("proc")
+    y, x = here >> 3, (here >> 1) & (XS - 1)
+    other = moved(shard, (1, 0, 0))
+    parts = []
+    for dy, part in ((0, shard), (1, other)):
+        for dx in range(XS):
+            arrived = moved(part, (0, dx, 0)) if dx else part
+            parts.append((arrived, ((y + dy) & (YS - 1), (x - dx) & (XS - 1))))
+    return parts
+
+
+def gathered(parts, start):
+    for part, where in parts:
+        start = placed(start, part[None, None], where)
+    other_core = moved(start, (0, 0, 1))
+    shape = (YS * XS,) + start.shape[2:]
+    return start.reshape(shape), other_core.reshape(shape)
+
+
 def per_device(
     ancestor_rows,
     piece_owner,
@@ -111,7 +150,7 @@
     tops = ancestor_rows.shape[2] // width
     slabs = blocks * pieces
 
-    panels = lax.all_gather(jnp.stack([panel_parent[0], panel_child[0]]), "proc", axis=0)
+    parts = shifted(jnp.stack([panel_parent[0], panel_child[0]]))
 
     spread = ancestor_rows.reshape(strip, tops, pieces, half).transpose(0, 2, 1, 3)
     spread = lax.all_to_all(
@@ -122,10 +161,16 @@
     index = owner[:, None, :] * tops + structure[:, :, None]
     choice = jax.nn.one_hot(index.reshape(-1), groups * tops, dtype=BF16)
     outgoing = jnp.dot(choice, spread.reshape(groups * tops, half), preferred_element_type=BF16)
+    start = jnp.zeros((YS, XS) + parts[0][0].shape, BF16)
+    outgoing, start = lax.optimization_barrier((outgoing, start))
+    mine, theirs = gathered(parts, start)
     upper = lax.all_to_all(
         outgoing.reshape(groups, blocks, slabs, half), "group", split_axis=0, concat_axis=0, tiled=True
-    ).reshape(strip, pieces, blocks, slabs, half)
-
+    )
+    upper = upper.reshape(strip, pieces, blocks, slabs, half)
+
+    core = lax.axis_index("proc") & (CORES - 1)
+    scalars = jnp.concatenate([kept_blocks[group_index], core[None].astype(jnp.int32)])
     vmem = pl.BlockSpec(memory_space=pltpu.VMEM)
     column_parent, column_child, sums = pl.pallas_call(
         products_kernel,
@@ -134,11 +179,12 @@
             jax.ShapeDtypeStruct((blocks, pieces, strip, width), BF16),
             jax.ShapeDtypeStruct((procs, 3, pieces, strip, width), BF16),
         ),
-        in_specs=[pl.BlockSpec(memory_space=pltpu.SMEM)] + [vmem] * 5,
+        in_specs=[pl.BlockSpec(memory_space=pltpu.SMEM)] + [vmem] * 6,
         out_specs=(vmem, vmem, vmem),
+        compiler_params=pltpu.CompilerParams(vmem_limit_bytes=32 * 1024 * 1024),
         interpret=INTERPRET,
         name="products",
-    )(kept_blocks[group_index], upper, panels, panel_parent[0], panel_child[0], pivot_parent[0])
+    )(scalars, upper, mine, theirs, panel_parent[0], panel_child[0], pivot_parent[0])
     arrived = lax.all_to_all(sums, "proc", split_axis=0, concat_axis=0, tiled=True)
     whole = pl.BlockSpec((pieces, strip, width), lambda i: (0, 0, 0))
     block_parent, column_child, block_child = pl.pallas_call(
@@ -180,6 +226,5 @@
         P("group", None, None, "proc", None),
         P("group", None, "proc", None),
     )
-    return jax.shard_map(
-        per_device, mesh=mesh, in_specs=in_specs, out_specs=out_specs, check_vma=False
-    )
+
+    return jax.shard_map(per_device, mesh=mesh, in_specs=in_specs, out_specs=out_specs, check_vma=False)

time: 169 us -> 198 us (1.17); the launches traced: 169 us -> 195 us
  starting transfers between devices: 22.7 us -> 48.4 us
  between operations: 14.1 us -> 0.83 us
  local copies, waits for them, and re-layouts: 7.7 us -> 17.9 us
  waiting for transfers between devices: 81.1 us -> 85.2 us
  blocking collectives: 27.1 us -> 29.2 us
    ppermute x0 -> x8, starting transfers between devices: none -> 26.4 us  [moved(): return lax.ppermute(value, 'proc', pairs)]
    ppermute x0 -> x8, waiting for transfers between devices: none -> 16.1 us  [moved(): return lax.ppermute(value, 'proc', pairs)]
    all_to_all x1, waiting for transfers between devices: 72.8 us -> 62.8 us  [per_device(): lax.all_to_all(outgoing.reshape(groups, blocks, slabs, half), 'group', sp...]
    dynamic_update_slice x0 -> x8, local copies, waits for them, and re-layouts: none -> 6.79 us  [placed(): lax.dynamic_update_slice(buffer, value, tuple(where) + (0,) * (buffer.ndi...]
    broadcast_in_dim x0 -> x1, local copies, waits for them, and re-layouts: none -> 2.51 us  [per_device(): start = jnp.zeros((YS, XS) + parts[0][0].shape, BF16)]
    all_to_all x1, blocking collectives: 27.1 us -> 29.2 us  [per_device(): lax.all_to_all(sums, 'proc', split_axis=0, concat_axis=0, tiled=True)]
  transfers between devices with their start and end apart: 3 -> 10, of which waited for: 2 -> 5; matrix products, arithmetic and copies ran while one was open for 5% -> 10% of each run, Pallas kernels for 0% -> 0%
where the time goes in v2:
time: 198 us; the launch traced here: 195 us
  waiting for transfers between devices  85.2 us (43%)
  starting transfers between devices  48.4 us (24%)
  blocking collectives  29.2 us (15%)
  local copies, waits for them, and re-layouts  17.9 us (9%)
  Pallas kernels  9.74 us (5%)
  matrix products  3.32 us (2%)
    all_to_all x1, waiting for transfers between devices, per_device(): lax.all_to_all(outgoing.reshape(groups, blocks, slabs, half), 'group', sp...  62.8 us
    all_to_all x1, blocking collectives, per_device(): lax.all_to_all(sums, 'proc', split_axis=0, concat_axis=0, tiled=True)  29.2 us
    ppermute x8, starting transfers between devices, moved(): return lax.ppermute(value, 'proc', pairs)  26.4 us
    ppermute x8, waiting for transfers between devices, moved(): return lax.ppermute(value, 'proc', pairs)  16.1 us
    all_to_all x1, starting transfers between devices, per_device(): lax.all_to_all(spread.reshape(groups, tops, half), 'group', split_axis=0,...  14.8 us
    pallas_call x1, Pallas kernels, per_device(): pl.pallas_call(products_kernel, out_shape=(jax.ShapeDtypeStruct((blocks,...  7.48 us
    all_to_all x1, starting transfers between devices, per_device(): lax.all_to_all(outgoing.reshape(groups, blocks, slabs, half), 'group', sp...  7.14 us
    dynamic_update_slice x8, local copies, waits for them, and re-layouts, placed(): lax.dynamic_update_slice(buffer, value, tuple(where) + (0,) * (buffer.ndi...  6.79 us
  transfers between devices with their start and end apart: 10, of which 5 were waited for; matrix products, arithmetic and copies ran while one was open for 10% of the time, Pallas kernels for 0%

profile of v2, /device:TPU:1, one launch (start us, length us, event | category | flops | bytes accessed | tf_op | source)
XLA Modules:
  0.0 195.4 jit_solution(2294982493994436940)
XLA Ops:
  0.7 1.0 constant_dynamic-update-slice_fusion.1
  1.6 1.0 constant_dynamic-update-slice_fusion
  2.6 3.9 %collective-permute-start = (bf16[2,8,2,16,512]{4,3,2,1,0:T(8,128)(2,1)S(1)}, bf16[2,8,2,16,512]{4,3,2,1,0:T(8,128)(2,1)S(1)}, u32[]{:S(2)}, u32[]{:S(2)}) collective-permute-start(bf16[2,8,2,16,512]{4,3,2,1,0:T(8,128)(2,1)S(1)} %constant_dynamic-update-slice_fusion), channel_id=1, source_target_pairs={{0,2},{1,3},{2,4},{3,5},{4,6},{5,7},{6,0},{7,1},{8,10},{9,11},{10,... | collective-permute-start | bytes 1572872 | tf_op jit(solution)/shard_map/ppermute | solution.py:106
  6.6 4.4 %collective-permute-start.1 = (bf16[2,8,2,16,512]{4,3,2,1,0:T(8,128)(2,1)S(1)}, bf16[2,8,2,16,512]{4,3,2,1,0:T(8,128)(2,1)S(1)}, u32[]{:S(2)}, u32[]{:S(2)}) collective-permute-start(bf16[2,8,2,16,512]{4,3,2,1,0:T(8,128)(2,1)S(1)} %constant_dynamic-update-slice_fusion), channel_id=1, source_target_pairs={{0,4},{1,5},{2,6},{3,7},{4,0},{5,1},{6,2},{7,3},{8,12},{9,13},{10,... | collective-permute-start | bytes 1572872 | tf_op jit(solution)/shard_map/ppermute | solution.py:106
  10.9 3.1 %collective-permute-start.2 = (bf16[2,8,2,16,512]{4,3,2,1,0:T(8,128)(2,1)S(1)}, bf16[2,8,2,16,512]{4,3,2,1,0:T(8,128)(2,1)S(1)}, u32[]{:S(2)}, u32[]{:S(2)}) collective-permute-start(bf16[2,8,2,16,512]{4,3,2,1,0:T(8,128)(2,1)S(1)} %constant_dynamic-update-slice_fusion), channel_id=1, source_target_pairs={{0,6},{1,7},{2,0},{3,1},{4,2},{5,3},{6,4},{7,5},{8,14},{9,15},{10,... | collective-permute-start | bytes 1572872 | tf_op jit(solution)/shard_map/ppermute | solution.py:106
  14.0 3.2 %collective-permute-start.3 = (bf16[2,8,2,16,512]{4,3,2,1,0:T(8,128)(2,1)S(1)}, bf16[2,8,2,16,512]{4,3,2,1,0:T(8,128)(2,1)S(1)}, u32[]{:S(2)}, u32[]{:S(2)}) collective-permute-start(bf16[2,8,2,16,512]{4,3,2,1,0:T(8,128)(2,1)S(1)} %constant_dynamic-update-slice_fusion), channel_id=1, source_target_pairs={{0,8},{1,9},{2,10},{3,11},{4,12},{5,13},{6,14},{7,15},{8,0},{9,1},... | collective-permute-start | bytes 1572872 | tf_op jit(solution)/shard_map/ppermute | solution.py:106
  17.2 1.1 reshape.102
  19.1 14.8 %all-to-all-start = ((bf16[32,16,256]{2,1,0:T(8,128)(2,1)}), bf16[32,16,256]{2,1,0:T(8,128)(2,1)S(1)}, u32[]{:S(2)}, u32[]{:S(2)}) async-start(bf16[32,16,256]{2,1,0:T(8,128)(2,1)} %bitcast.3), calls=%async_computation | async-start | bytes 524288 | tf_op jit(solution)/shard_map/all_to_all | solution.py:156
  35.7 3.3 %gather_fusion = s32[512]{0:T(512)S(1)} fusion(s32[32]{0:T(128)S(1)} %copy-done.4, s32[1024]{0:T(1024)S(1)} %pad_clamp_fusion), kind=kCustom, calls=%fused_computation | custom fusion | bytes 6144 | tf_op jit(solution)/shard_map/gather | solution.py:160
  39.3 6.3 %all-to-all-done = bf16[32,16,256]{2,1,0:T(8,128)(2,1)S(1)} async-done(((bf16[32,16,256]{2,1,0:T(8,128)(2,1)}), bf16[32,16,256]{2,1,0:T(8,128)(2,1)S(1)}, u32[]{:S(2)}, u32[]{:S(2)}) %all-to-all-start) | async-done | bytes 262176 | tf_op jit(solution)/shard_map/all_to_all | solution.py:156
  45.7 3.3 %fusion = bf16[4096,256]{1,0:T(8,128)(2,1)} fusion(bf16[512,256]{1,0:T(8,128)(2,1)S(1)} %bitcast.43, s32[4096]{0:T(1024)S(1)} %add.112), kind=kOutput, calls=%fused_computation.2 | convolution fusion | flops 1075838976 | bytes 2375680 | tf_op jit(solution)/shard_map/dot_general | solution.py:163
  49.0 2.5 %broadcast_in_dim.50 = bf16[2,4,2,8,2,16,512]{6,5,4,3,2,1,0:T(8,128)(2,1)} broadcast(bf16[]{:T(256)} %constant.28.clone.1), dimensions={} | broadcast | bytes 4194306 | tf_op jit(solution)/shard_map/broadcast_in_dim | solution.py:164
  52.3 2.2 %collective-permute-start.4 = (bf16[2,8,2,16,512]{4,3,2,1,0:T(8,128)(2,1)S(1)}, bf16[2,8,2,16,512]{4,3,2,1,0:T(8,128)(2,1)S(1)}, u32[]{:S(2)}, u32[]{:S(2)}) collective-permute-start(bf16[2,8,2,16,512]{4,3,2,1,0:T(8,128)(2,1)S(1)} %collective-permute-done.3), channel_id=1, source_target_pairs={{0,2},{1,3},{2,4},{3,5},{4,6},{5,7},{6,0},{7,1},{8,10},{9,11},{10,... | collective-permute-start | bytes 1572872 | tf_op jit(solution)/shard_map/ppermute | solution.py:106
  54.6 2.8 %collective-permute-start.5 = (bf16[2,8,2,16,512]{4,3,2,1,0:T(8,128)(2,1)S(1)}, bf16[2,8,2,16,512]{4,3,2,1,0:T(8,128)(2,1)S(1)}, u32[]{:S(2)}, u32[]{:S(2)}) collective-permute-start(bf16[2,8,2,16,512]{4,3,2,1,0:T(8,128)(2,1)S(1)} %collective-permute-done.3), channel_id=1, source_target_pairs={{0,4},{1,5},{2,6},{3,7},{4,0},{5,1},{6,2},{7,3},{8,12},{9,13},{10,... | collective-permute-start | bytes 1572872 | tf_op jit(solution)/shard_map/ppermute | solution.py:106
  57.3 3.5 %collective-permute-start.6 = (bf16[2,8,2,16,512]{4,3,2,1,0:T(8,128)(2,1)S(1)}, bf16[2,8,2,16,512]{4,3,2,1,0:T(8,128)(2,1)S(1)}, u32[]{:S(2)}, u32[]{:S(2)}) collective-permute-start(bf16[2,8,2,16,512]{4,3,2,1,0:T(8,128)(2,1)S(1)} %collective-permute-done.3), channel_id=1, source_target_pairs={{0,6},{1,7},{2,0},{3,1},{4,2},{5,3},{6,4},{7,5},{8,14},{9,15},{10,... | collective-permute-start | bytes 1572872 | tf_op jit(solution)/shard_map/ppermute | solution.py:106
  64.2 2.3 %collective-permute-done.4 = bf16[2,8,2,16,512]{4,3,2,1,0:T(8,128)(2,1)S(1)} collective-permute-done((bf16[2,8,2,16,512]{4,3,2,1,0:T(8,128)(2,1)S(1)}, bf16[2,8,2,16,512]{4,3,2,1,0:T(8,128)(2,1)S(1)}, u32[]{:S(2)}, u32[]{:S(2)}) %collective-permute-start.4) | collective-permute-done | bytes 524320 | tf_op jit(solution)/shard_map/ppermute | solution.py:106
  67.4 7.8 %collective-permute-done.5 = bf16[2,8,2,16,512]{4,3,2,1,0:T(8,128)(2,1)S(1)} collective-permute-done((bf16[2,8,2,16,512]{4,3,2,1,0:T(8,128)(2,1)S(1)}, bf16[2,8,2,16,512]{4,3,2,1,0:T(8,128)(2,1)S(1)}, u32[]{:S(2)}, u32[]{:S(2)}) %collective-permute-start.5) | collective-permute-done | bytes 524320 | tf_op jit(solution)/shard_map/ppermute | solution.py:106
  76.0 6.0 %collective-permute-done.6 = bf16[2,8,2,16,512]{4,3,2,1,0:T(8,128)(2,1)S(1)} collective-permute-done((bf16[2,8,2,16,512]{4,3,2,1,0:T(8,128)(2,1)S(1)}, bf16[2,8,2,16,512]{4,3,2,1,0:T(8,128)(2,1)S(1)}, u32[]{:S(2)}, u32[]{:S(2)}) %collective-permute-start.6) | collective-permute-done | bytes 524320 | tf_op jit(solution)/shard_map/ppermute | solution.py:106
  82.8 3.5 %collective-permute-start.7 = (bf16[2,4,2,8,2,16,512]{6,5,4,3,2,1,0:T(8,128)(2,1)}, bf16[2,4,2,8,2,16,512]{6,5,4,3,2,1,0:T(8,128)(2,1)}, u32[]{:S(2)}, u32[]{:S(2)}) collective-permute-start(bf16[2,4,2,8,2,16,512]{6,5,4,3,2,1,0:T(8,128)(2,1)} %bitcast_dynamic-update-slice_fusion), channel_id=1, source_target_pairs={{0,1},{1,0},{2,3},{3,2},{4,5},{5,4},{6,7},{7,6},{8,9},{9,8},{10,11... | collective-permute-start | bytes 12582920 | tf_op jit(solution)/shard_map/ppermute | solution.py:106
  86.3 7.1 %all-to-all-start.1 = ((bf16[32,8,16,256]{3,2,1,0:T(8,128)(2,1)}), bf16[32,8,16,256]{3,2,1,0:T(8,128)(2,1)S(1)}, u32[]{:S(2)}, u32[]{:S(2)}) async-start(bf16[32,8,16,256]{3,2,1,0:T(8,128)(2,1)} %bitcast.41), calls=%async_computation.1 | async-start | bytes 4194304 | tf_op jit(solution)/shard_map/all_to_all | solution.py:167
  93.7 62.8 %all-to-all-done.1 = bf16[32,8,16,256]{3,2,1,0:T(8,128)(2,1)S(1)} async-done(((bf16[32,8,16,256]{3,2,1,0:T(8,128)(2,1)}), bf16[32,8,16,256]{3,2,1,0:T(8,128)(2,1)S(1)}, u32[]{:S(2)}, u32[]{:S(2)}) %all-to-all-start.1) | async-done | bytes 2097184 | tf_op jit(solution)/shard_map/all_to_all | solution.py:167
  156.5 7.5 %products.1 = (bf16[8,2,16,512]{3,2,1,0:T(8,128)(2,1)}, bf16[8,2,16,512]{3,2,1,0:T(8,128)(2,1)}, bf16[16,3,2,16,512]{4,3,2,1,0:T(8,128)(2,1)S(1)}) custom-call(s32[8]{0:T(128)S(1)} %pad_add_fusion.kept, bf16[16,2,8,16,256]{4,3,2,1,0:T(8,128)(2,1)S(1)} %bitcast.36, bf16[8,2,8,2,16,512]{5,4,3,2,1,0:T(8,128)(2,1)} %bitcast.15.mine, ...), custom_call_target="tpu_custom_call" | custom-call | tf_op jit(solution)/shard_map/products/pallas_call | solution.py:175
  164.0 29.2 %all_to_all.15.arrived = bf16[16,3,2,16,512]{4,3,2,1,0:T(8,128)(2,1)} all-to-all(bf16[16,3,2,16,512]{4,3,2,1,0:T(8,128)(2,1)S(1)} %get-tuple-element.15), channel_id=1, replica_groups=mesh['group'=32,'proc'=16] {'proc'}, dimensions={0} | all-to-all | bytes 3145728 | tf_op jit(solution)/shard_map/all_to_all | solution.py:188
  193.1 2.3 %final.1 = (bf16[2,16,512]{2,1,0:T(8,128)(2,1)}, bf16[8,2,16,512]{3,2,1,0:T(8,128)(2,1)}, bf16[2,16,512]{2,1,0:T(8,128)(2,1)}) custom-call(bf16[16,3,2,16,512]{4,3,2,1,0:T(8,128)(2,1)} %all_to_all.15.arrived, bf16[2,16,512]{2,1,0:T(8,128)(2,1)} %bitcast.39, bf16[2,16,512]{2,1,0:T(8,128)(2,1)} %bitcast.46, ...), custom_call_target="tpu_custom_call", output_to_operand_aliasing={{1}: (3, {})} | custom-call | tf_op jit(solution)/shard_map/final/pallas_call | solution.py:190
  (39 shorter events, 9.9 us)
Async XLA Ops:
  0.6 92.8 %copy-start = (s32[32,7]{0,1:T(8,128)S(1)}, s32[32,7]{0,1:T(8,128)}, u32[]{:S(2)}) copy-start(s32[32,7]{0,1:T(8,128)} %param.11) | copy-start | bytes 2692
  0.6 35.0 %copy-start.4 = (s32[32]{0:T(128)S(1)}, s32[32]{0:T(128)}, u32[]{:S(2)}) copy-start(s32[32]{0:T(128)} %param.9) | copy-start | bytes 388
  2.6 54.7 %collective-permute-start = (bf16[2,8,2,16,512]{4,3,2,1,0:T(8,128)(2,1)S(1)}, bf16[2,8,2,16,512]{4,3,2,1,0:T(8,128)(2,1)S(1)}, u32[]{:S(2)}, u32[]{:S(2)}) collective-permute-start(bf16[2,8,2,16,512]{4,3,2,1,0:T(8,128)(2,1)S(1)} %constant_dynamic-update-slice_fusion), channel_id=1, source_target_pairs={{0,2},{1,3},{2,4},{3,5},{4,6},{5,7},{6,0},{7,1},{8,10},{9,11},{10,... | collective-permute-start | bytes 1572872 | tf_op jit(solution)/shard_map/ppermute | solution.py:106
  6.6 55.1 %collective-permute-start.1 = (bf16[2,8,2,16,512]{4,3,2,1,0:T(8,128)(2,1)S(1)}, bf16[2,8,2,16,512]{4,3,2,1,0:T(8,128)(2,1)S(1)}, u32[]{:S(2)}, u32[]{:S(2)}) collective-permute-start(bf16[2,8,2,16,512]{4,3,2,1,0:T(8,128)(2,1)S(1)} %constant_dynamic-update-slice_fusion), channel_id=1, source_target_pairs={{0,4},{1,5},{2,6},{3,7},{4,0},{5,1},{6,2},{7,3},{8,12},{9,13},{10,... | collective-permute-start | bytes 1572872 | tf_op jit(solution)/shard_map/ppermute | solution.py:106
  10.9 51.6 %collective-permute-start.2 = (bf16[2,8,2,16,512]{4,3,2,1,0:T(8,128)(2,1)S(1)}, bf16[2,8,2,16,512]{4,3,2,1,0:T(8,128)(2,1)S(1)}, u32[]{:S(2)}, u32[]{:S(2)}) collective-permute-start(bf16[2,8,2,16,512]{4,3,2,1,0:T(8,128)(2,1)S(1)} %constant_dynamic-update-slice_fusion), channel_id=1, source_target_pairs={{0,6},{1,7},{2,0},{3,1},{4,2},{5,3},{6,4},{7,5},{8,14},{9,15},{10,... | collective-permute-start | bytes 1572872 | tf_op jit(solution)/shard_map/ppermute | solution.py:106
  14.0 38.3 %collective-permute-start.3 = (bf16[2,8,2,16,512]{4,3,2,1,0:T(8,128)(2,1)S(1)}, bf16[2,8,2,16,512]{4,3,2,1,0:T(8,128)(2,1)S(1)}, u32[]{:S(2)}, u32[]{:S(2)}) collective-permute-start(bf16[2,8,2,16,512]{4,3,2,1,0:T(8,128)(2,1)S(1)} %constant_dynamic-update-slice_fusion), channel_id=1, source_target_pairs={{0,8},{1,9},{2,10},{3,11},{4,12},{5,13},{6,14},{7,15},{8,0},{9,1},... | collective-permute-start | bytes 1572872 | tf_op jit(solution)/shard_map/ppermute | solution.py:106
  19.1 26.6 %all-to-all-start = ((bf16[32,16,256]{2,1,0:T(8,128)(2,1)}), bf16[32,16,256]{2,1,0:T(8,128)(2,1)S(1)}, u32[]{:S(2)}, u32[]{:S(2)}) async-start(bf16[32,16,256]{2,1,0:T(8,128)(2,1)} %bitcast.3), calls=%async_computation | async-start | bytes 524288 | tf_op jit(solution)/shard_map/all_to_all | solution.py:156
  52.3 14.2 %collective-permute-start.4 = (bf16[2,8,2,16,512]{4,3,2,1,0:T(8,128)(2,1)S(1)}, bf16[2,8,2,16,512]{4,3,2,1,0:T(8,128)(2,1)S(1)}, u32[]{:S(2)}, u32[]{:S(2)}) collective-permute-start(bf16[2,8,2,16,512]{4,3,2,1,0:T(8,128)(2,1)S(1)} %collective-permute-done.3), channel_id=1, source_target_pairs={{0,2},{1,3},{2,4},{3,5},{4,6},{5,7},{6,0},{7,1},{8,10},{9,11},{10,... | collective-permute-start | bytes 1572872 | tf_op jit(solution)/shard_map/ppermute | solution.py:106
  54.6 20.6 %collective-permute-start.5 = (bf16[2,8,2,16,512]{4,3,2,1,0:T(8,128)(2,1)S(1)}, bf16[2,8,2,16,512]{4,3,2,1,0:T(8,128)(2,1)S(1)}, u32[]{:S(2)}, u32[]{:S(2)}) collective-permute-start(bf16[2,8,2,16,512]{4,3,2,1,0:T(8,128)(2,1)S(1)} %collective-permute-done.3), channel_id=1, source_target_pairs={{0,4},{1,5},{2,6},{3,7},{4,0},{5,1},{6,2},{7,3},{8,12},{9,13},{10,... | collective-permute-start | bytes 1572872 | tf_op jit(solution)/shard_map/ppermute | solution.py:106
  57.3 24.6 %collective-permute-start.6 = (bf16[2,8,2,16,512]{4,3,2,1,0:T(8,128)(2,1)S(1)}, bf16[2,8,2,16,512]{4,3,2,1,0:T(8,128)(2,1)S(1)}, u32[]{:S(2)}, u32[]{:S(2)}) collective-permute-start(bf16[2,8,2,16,512]{4,3,2,1,0:T(8,128)(2,1)S(1)} %collective-permute-done.3), channel_id=1, source_target_pairs={{0,6},{1,7},{2,0},{3,1},{4,2},{5,3},{6,4},{7,5},{8,14},{9,15},{10,... | collective-permute-start | bytes 1572872 | tf_op jit(solution)/shard_map/ppermute | solution.py:106
  63.4 93.1 %copy-start.1 = (bf16[1,8,2,16,512]{4,3,2,1,0:T(8,128)(2,1)S(1)}, bf16[1,8,2,16,512]{4,3,2,1,0:T(8,128)(2,1)}, u32[]{:S(2)}) copy-start(bf16[1,8,2,16,512]{4,3,2,1,0:T(8,128)(2,1)} %param.12) | copy-start | bytes 786436
  63.4 93.1 %copy-start.2 = (bf16[1,8,2,16,512]{4,3,2,1,0:T(8,128)(2,1)S(1)}, bf16[1,8,2,16,512]{4,3,2,1,0:T(8,128)(2,1)}, u32[]{:S(2)}) copy-start(bf16[1,8,2,16,512]{4,3,2,1,0:T(8,128)(2,1)} %param.13) | copy-start | bytes 786436
  63.4 93.1 %copy-start.3 = (bf16[1,2,16,512]{3,2,1,0:T(8,128)(2,1)S(1)}, bf16[1,2,16,512]{3,2,1,0:T(8,128)(2,1)}, u32[]{:S(2)}) copy-start(bf16[1,2,16,512]{3,2,1,0:T(8,128)(2,1)} %param.14) | copy-start | bytes 98308
  82.8 73.7 %collective-permute-start.7 = (bf16[2,4,2,8,2,16,512]{6,5,4,3,2,1,0:T(8,128)(2,1)}, bf16[2,4,2,8,2,16,512]{6,5,4,3,2,1,0:T(8,128)(2,1)}, u32[]{:S(2)}, u32[]{:S(2)}) collective-permute-start(bf16[2,4,2,8,2,16,512]{6,5,4,3,2,1,0:T(8,128)(2,1)} %bitcast_dynamic-update-slice_fusion), channel_id=1, source_target_pairs={{0,1},{1,0},{2,3},{3,2},{4,5},{5,4},{6,7},{7,6},{8,9},{9,8},{10,11... | collective-permute-start | bytes 12582920 | tf_op jit(solution)/shard_map/ppermute | solution.py:106
  86.3 70.2 %all-to-all-start.1 = ((bf16[32,8,16,256]{3,2,1,0:T(8,128)(2,1)}), bf16[32,8,16,256]{3,2,1,0:T(8,128)(2,1)S(1)}, u32[]{:S(2)}, u32[]{:S(2)}) async-start(bf16[32,8,16,256]{3,2,1,0:T(8,128)(2,1)} %bitcast.41), calls=%async_computation.1 | async-start | bytes 4194304 | tf_op jit(solution)/shard_map/all_to_all | solution.py:167

commit v3 on v2

--- a/solution.py
+++ b/solution.py
@@ -21,22 +21,37 @@
     return lax.dot_general(a, b, (((0,), (0,)), ((), ())), preferred_element_type=F32)
 
 
-def products_kernel(kept, upper, mine, theirs, own_first, own_second, pivot, column_out, child_out, sums_out):
+def products_kernel(
+    kept, upper, mine, theirs, own_first, own_second, pivot, column_out, child_out, sums_out, panels, sems
+):
     strip, pieces, blocks, slabs, half = upper.shape
-    procs, width = CORES * mine.shape[0], mine.shape[-1]
-    first_core = kept[blocks - 1] == 0
+    procs, width = PROCS, panels.shape[-1]
     rows = strip * slabs
+    core = kept[blocks - 1]
+    order = [(1, 0)] + [(0, b) for b in range(blocks)] + [(1, b) for b in range(1, blocks)]
+    copies = {}
+    for n, b in order:
+        copies[n, b] = [
+            pltpu.make_async_copy(mine.at[:, n, b], panels.at[:, core, n, b], sems.at[n, b, 0]),
+            pltpu.make_async_copy(theirs.at[:, n, b], panels.at[:, 1 - core, n, b], sems.at[n, b, 1]),
+        ]
+        for copy in copies[n, b]:
+            copy.start()
 
     def left(h, b):
         return upper[:, h, b].reshape(rows, half)
 
     def right(n, b, h):
-        a, b = mine[:, n, b, h], theirs[:, n, b, h]
-        pair = jnp.stack([jnp.where(first_core, a, b), jnp.where(first_core, b, a)], axis=1)
-        return pair.reshape(half, width)
-
+        return panels[:, :, n, b, h].reshape(half, width)
+
+    def arrive(n, b):
+        for copy in copies[n, b]:
+            copy.wait()
+
+    arrive(1, 0)
     total = jnp.zeros((rows, width), F32)
     for b in range(blocks):
+        arrive(0, b)
         for h in range(pieces):
             total += dot(left(h, b), right(0, b, h))
     column = (-total).astype(BF16)
@@ -57,6 +72,7 @@
     top = [right(1, 0, h) for h in range(pieces)]
     total = jnp.zeros((rows, width), F32)
     for b in range(1, blocks):
+        arrive(1, b)
         for h in range(pieces):
             total += dot(left(h, kept[b - 1]), right(1, b, h))
     for h in range(pieces):
@@ -156,8 +172,9 @@
     spread = lax.all_to_all(
         spread.reshape(groups, tops, half), "group", split_axis=0, concat_axis=0, tiled=True
     )
-    wanted = structure[:, :, None] * pieces + jnp.arange(pieces, dtype=jnp.int32)
-    owner = piece_owner[wanted.reshape(groups, slabs)]
+    owners = piece_owner.reshape(tops, pieces)
+    same = structure[:, :, None, None] == jnp.arange(tops, dtype=jnp.int32)[:, None]
+    owner = jnp.where(same, owners, 0).sum(axis=2).reshape(groups, slabs)
     index = owner[:, None, :] * tops + structure[:, :, None]
     choice = jax.nn.one_hot(index.reshape(-1), groups * tops, dtype=BF16)
     outgoing = jnp.dot(choice, spread.reshape(groups * tops, half), preferred_element_type=BF16)
@@ -171,7 +188,9 @@
 
     core = lax.axis_index("proc") & (CORES - 1)
     scalars = jnp.concatenate([kept_blocks[group_index], core[None].astype(jnp.int32)])
+    smem = pl.BlockSpec(memory_space=pltpu.SMEM)
     vmem = pl.BlockSpec(memory_space=pltpu.VMEM)
+    anywhere = pl.BlockSpec(memory_space=pl.ANY)
     column_parent, column_child, sums = pl.pallas_call(
         products_kernel,
         out_shape=(
@@ -179,8 +198,12 @@
             jax.ShapeDtypeStruct((blocks, pieces, strip, width), BF16),
             jax.ShapeDtypeStruct((procs, 3, pieces, strip, width), BF16),
         ),
-        in_specs=[pl.BlockSpec(memory_space=pltpu.SMEM)] + [vmem] * 6,
+        in_specs=[smem, vmem, anywhere, anywhere, vmem, vmem, vmem],
         out_specs=(vmem, vmem, vmem),
+        scratch_shapes=[
+            pltpu.VMEM(mine.shape[:1] + (CORES,) + mine.shape[1:], BF16),
+            pltpu.SemaphoreType.DMA((2, blocks, 2)),
+        ],
         compiler_params=pltpu.CompilerParams(vmem_limit_bytes=32 * 1024 * 1024),
         interpret=INTERPRET,
         name="products",

time: 198 us -> 196 us (0.990)
  waiting for transfers between devices: 85.2 us -> 89 us
  local copies, waits for them, and re-layouts: 17.9 us -> 15.2 us
  blocking collectives: 29.2 us -> 27 us
    gather x1 -> x0, local copies, waits for them, and re-layouts: 3.34 us -> none  [per_device(): owner = piece_owner[wanted.reshape(groups, slabs)]]
    all_to_all x1, waiting for transfers between devices: 6.32 us -> 9.52 us  [per_device(): lax.all_to_all(spread.reshape(groups, tops, half), 'group', split_axis=0,...]
    all_to_all x1, blocking collectives: 29.2 us -> 27 us  [per_device(): lax.all_to_all(sums, 'proc', split_axis=0, concat_axis=0, tiled=True)]
  transfers between devices with their start and end apart: 10 -> 10, of which waited for: 5 -> 5; matrix products, arithmetic and copies ran while one was open for 10% -> 8% of each run, Pallas kernels for 0% -> 0%
where the time goes in v3:
time: 196 us; the launch traced here: 193 us
  waiting for transfers between devices  89 us (45%)
  starting transfers between devices  48.4 us (25%)
  blocking collectives  27 us (14%)
  local copies, waits for them, and re-layouts  15.2 us (8%)
  Pallas kernels  9.15 us (5%)
  matrix products  3.29 us (2%)
    all_to_all x1, waiting for transfers between devices, per_device(): lax.all_to_all(outgoing.reshape(groups, blocks, slabs, half), 'group', sp...  63.4 us
    all_to_all x1, blocking collectives, per_device(): lax.all_to_all(sums, 'proc', split_axis=0, concat_axis=0, tiled=True)  27 us
    ppermute x8, starting transfers between devices, moved(): return lax.ppermute(value, 'proc', pairs)  26.4 us
    ppermute x8, waiting for transfers between devices, moved(): return lax.ppermute(value, 'proc', pairs)  16.1 us
    all_to_all x1, starting transfers between devices, per_device(): lax.all_to_all(spread.reshape(groups, tops, half), 'group', split_axis=0,...  14.8 us
    all_to_all x1, waiting for transfers between devices, per_device(): lax.all_to_all(spread.reshape(groups, tops, half), 'group', split_axis=0,...  9.52 us
    all_to_all x1, starting transfers between devices, per_device(): lax.all_to_all(outgoing.reshape(groups, blocks, slabs, half), 'group', sp...  7.14 us
    pallas_call x1, Pallas kernels, per_device(): pl.pallas_call(products_kernel, out_shape=(jax.ShapeDtypeStruct((blocks,...  6.89 us
  transfers between devices with their start and end apart: 10, of which 5 were waited for; matrix products, arithmetic and copies ran while one was open for 8% of the time, Pallas kernels for 0%

profile of v3, /device:TPU:1, one launch (start us, length us, event | category | flops | bytes accessed | tf_op | source)
XLA Modules:
  0.0 193.2 jit_solution(4061016974857938881)
XLA Ops:
  0.6 1.0 constant_dynamic-update-slice_fusion.1
  1.6 1.0 constant_dynamic-update-slice_fusion
  2.6 3.9 %collective-permute-start = (bf16[2,8,2,16,512]{4,3,2,1,0:T(8,128)(2,1)S(1)}, bf16[2,8,2,16,512]{4,3,2,1,0:T(8,128)(2,1)S(1)}, u32[]{:S(2)}, u32[]{:S(2)}) collective-permute-start(bf16[2,8,2,16,512]{4,3,2,1,0:T(8,128)(2,1)S(1)} %constant_dynamic-update-slice_fusion), channel_id=1, source_target_pairs={{0,2},{1,3},{2,4},{3,5},{4,6},{5,7},{6,0},{7,1},{8,10},{9,11},{10,... | collective-permute-start | bytes 1572872 | tf_op jit(solution)/shard_map/ppermute | solution.py:122
  6.5 4.4 %collective-permute-start.1 = (bf16[2,8,2,16,512]{4,3,2,1,0:T(8,128)(2,1)S(1)}, bf16[2,8,2,16,512]{4,3,2,1,0:T(8,128)(2,1)S(1)}, u32[]{:S(2)}, u32[]{:S(2)}) collective-permute-start(bf16[2,8,2,16,512]{4,3,2,1,0:T(8,128)(2,1)S(1)} %constant_dynamic-update-slice_fusion), channel_id=1, source_target_pairs={{0,4},{1,5},{2,6},{3,7},{4,0},{5,1},{6,2},{7,3},{8,12},{9,13},{10,... | collective-permute-start | bytes 1572872 | tf_op jit(solution)/shard_map/ppermute | solution.py:122
  10.9 3.1 %collective-permute-start.2 = (bf16[2,8,2,16,512]{4,3,2,1,0:T(8,128)(2,1)S(1)}, bf16[2,8,2,16,512]{4,3,2,1,0:T(8,128)(2,1)S(1)}, u32[]{:S(2)}, u32[]{:S(2)}) collective-permute-start(bf16[2,8,2,16,512]{4,3,2,1,0:T(8,128)(2,1)S(1)} %constant_dynamic-update-slice_fusion), channel_id=1, source_target_pairs={{0,6},{1,7},{2,0},{3,1},{4,2},{5,3},{6,4},{7,5},{8,14},{9,15},{10,... | collective-permute-start | bytes 1572872 | tf_op jit(solution)/shard_map/ppermute | solution.py:122
  14.0 3.2 %collective-permute-start.3 = (bf16[2,8,2,16,512]{4,3,2,1,0:T(8,128)(2,1)S(1)}, bf16[2,8,2,16,512]{4,3,2,1,0:T(8,128)(2,1)S(1)}, u32[]{:S(2)}, u32[]{:S(2)}) collective-permute-start(bf16[2,8,2,16,512]{4,3,2,1,0:T(8,128)(2,1)S(1)} %constant_dynamic-update-slice_fusion), channel_id=1, source_target_pairs={{0,8},{1,9},{2,10},{3,11},{4,12},{5,13},{6,14},{7,15},{8,0},{9,1},... | collective-permute-start | bytes 1572872 | tf_op jit(solution)/shard_map/ppermute | solution.py:122
  17.2 1.1 reshape.67
  19.1 14.8 %all-to-all-start = ((bf16[32,16,256]{2,1,0:T(8,128)(2,1)}), bf16[32,16,256]{2,1,0:T(8,128)(2,1)S(1)}, u32[]{:S(2)}, u32[]{:S(2)}) async-start(bf16[32,16,256]{2,1,0:T(8,128)(2,1)} %bitcast.3), calls=%async_computation | async-start | bytes 524288 | tf_op jit(solution)/shard_map/all_to_all | solution.py:172
  36.1 9.5 %all-to-all-done = bf16[32,16,256]{2,1,0:T(8,128)(2,1)S(1)} async-done(((bf16[32,16,256]{2,1,0:T(8,128)(2,1)}), bf16[32,16,256]{2,1,0:T(8,128)(2,1)S(1)}, u32[]{:S(2)}, u32[]{:S(2)}) %all-to-all-start) | async-done | bytes 262176 | tf_op jit(solution)/shard_map/all_to_all | solution.py:172
  45.7 3.3 %fusion = bf16[4096,256]{1,0:T(8,128)(2,1)} fusion(bf16[512,256]{1,0:T(8,128)(2,1)S(1)} %bitcast.41, s32[4096]{0:T(1024)S(1)} %add.61), kind=kOutput, calls=%fused_computation.1 | convolution fusion | flops 1075838976 | bytes 2375680 | tf_op jit(solution)/shard_map/dot_general | solution.py:180
  48.9 2.5 %broadcast_in_dim.66 = bf16[2,4,2,8,2,16,512]{6,5,4,3,2,1,0:T(8,128)(2,1)} broadcast(bf16[]{:T(256)} %constant.24.clone.1), dimensions={} | broadcast | bytes 4194306 | tf_op jit(solution)/shard_map/broadcast_in_dim | solution.py:181
  52.3 2.2 %collective-permute-start.4 = (bf16[2,8,2,16,512]{4,3,2,1,0:T(8,128)(2,1)S(1)}, bf16[2,8,2,16,512]{4,3,2,1,0:T(8,128)(2,1)S(1)}, u32[]{:S(2)}, u32[]{:S(2)}) collective-permute-start(bf16[2,8,2,16,512]{4,3,2,1,0:T(8,128)(2,1)S(1)} %collective-permute-done.3), channel_id=1, source_target_pairs={{0,2},{1,3},{2,4},{3,5},{4,6},{5,7},{6,0},{7,1},{8,10},{9,11},{10,... | collective-permute-start | bytes 1572872 | tf_op jit(solution)/shard_map/ppermute | solution.py:122
  54.5 2.8 %collective-permute-start.5 = (bf16[2,8,2,16,512]{4,3,2,1,0:T(8,128)(2,1)S(1)}, bf16[2,8,2,16,512]{4,3,2,1,0:T(8,128)(2,1)S(1)}, u32[]{:S(2)}, u32[]{:S(2)}) collective-permute-start(bf16[2,8,2,16,512]{4,3,2,1,0:T(8,128)(2,1)S(1)} %collective-permute-done.3), channel_id=1, source_target_pairs={{0,4},{1,5},{2,6},{3,7},{4,0},{5,1},{6,2},{7,3},{8,12},{9,13},{10,... | collective-permute-start | bytes 1572872 | tf_op jit(solution)/shard_map/ppermute | solution.py:122
  57.3 3.5 %collective-permute-start.6 = (bf16[2,8,2,16,512]{4,3,2,1,0:T(8,128)(2,1)S(1)}, bf16[2,8,2,16,512]{4,3,2,1,0:T(8,128)(2,1)S(1)}, u32[]{:S(2)}, u32[]{:S(2)}) collective-permute-start(bf16[2,8,2,16,512]{4,3,2,1,0:T(8,128)(2,1)S(1)} %collective-permute-done.3), channel_id=1, source_target_pairs={{0,6},{1,7},{2,0},{3,1},{4,2},{5,3},{6,4},{7,5},{8,14},{9,15},{10,... | collective-permute-start | bytes 1572872 | tf_op jit(solution)/shard_map/ppermute | solution.py:122
  61.6 0.9 bitcast_dynamic-update-slice_fusion.5
  64.2 2.3 %collective-permute-done.4 = bf16[2,8,2,16,512]{4,3,2,1,0:T(8,128)(2,1)S(1)} collective-permute-done((bf16[2,8,2,16,512]{4,3,2,1,0:T(8,128)(2,1)S(1)}, bf16[2,8,2,16,512]{4,3,2,1,0:T(8,128)(2,1)S(1)}, u32[]{:S(2)}, u32[]{:S(2)}) %collective-permute-start.4) | collective-permute-done | bytes 524320 | tf_op jit(solution)/shard_map/ppermute | solution.py:122
  67.4 7.7 %collective-permute-done.5 = bf16[2,8,2,16,512]{4,3,2,1,0:T(8,128)(2,1)S(1)} collective-permute-done((bf16[2,8,2,16,512]{4,3,2,1,0:T(8,128)(2,1)S(1)}, bf16[2,8,2,16,512]{4,3,2,1,0:T(8,128)(2,1)S(1)}, u32[]{:S(2)}, u32[]{:S(2)}) %collective-permute-start.5) | collective-permute-done | bytes 524320 | tf_op jit(solution)/shard_map/ppermute | solution.py:122
  75.9 6.0 %collective-permute-done.6 = bf16[2,8,2,16,512]{4,3,2,1,0:T(8,128)(2,1)S(1)} collective-permute-done((bf16[2,8,2,16,512]{4,3,2,1,0:T(8,128)(2,1)S(1)}, bf16[2,8,2,16,512]{4,3,2,1,0:T(8,128)(2,1)S(1)}, u32[]{:S(2)}, u32[]{:S(2)}) %collective-permute-start.6) | collective-permute-done | bytes 524320 | tf_op jit(solution)/shard_map/ppermute | solution.py:122
  82.7 3.5 %collective-permute-start.7 = (bf16[2,4,2,8,2,16,512]{6,5,4,3,2,1,0:T(8,128)(2,1)}, bf16[2,4,2,8,2,16,512]{6,5,4,3,2,1,0:T(8,128)(2,1)}, u32[]{:S(2)}, u32[]{:S(2)}) collective-permute-start(bf16[2,4,2,8,2,16,512]{6,5,4,3,2,1,0:T(8,128)(2,1)} %bitcast_dynamic-update-slice_fusion), channel_id=1, source_target_pairs={{0,1},{1,0},{2,3},{3,2},{4,5},{5,4},{6,7},{7,6},{8,9},{9,8},{10,11... | collective-permute-start | bytes 12582920 | tf_op jit(solution)/shard_map/ppermute | solution.py:122
  86.2 7.1 %all-to-all-start.1 = ((bf16[32,8,16,256]{3,2,1,0:T(8,128)(2,1)}), bf16[32,8,16,256]{3,2,1,0:T(8,128)(2,1)S(1)}, u32[]{:S(2)}, u32[]{:S(2)}) async-start(bf16[32,8,16,256]{3,2,1,0:T(8,128)(2,1)} %bitcast.39), calls=%async_computation.1 | async-start | bytes 4194304 | tf_op jit(solution)/shard_map/all_to_all | solution.py:184
  93.6 63.4 %all-to-all-done.1 = bf16[32,8,16,256]{3,2,1,0:T(8,128)(2,1)S(1)} async-done(((bf16[32,8,16,256]{3,2,1,0:T(8,128)(2,1)}), bf16[32,8,16,256]{3,2,1,0:T(8,128)(2,1)S(1)}, u32[]{:S(2)}, u32[]{:S(2)}) %all-to-all-start.1) | async-done | bytes 2097184 | tf_op jit(solution)/shard_map/all_to_all | solution.py:184
  157.0 6.9 %products.1 = (bf16[8,2,16,512]{3,2,1,0:T(8,128)(2,1)}, bf16[8,2,16,512]{3,2,1,0:T(8,128)(2,1)}, bf16[16,3,2,16,512]{4,3,2,1,0:T(8,128)(2,1)S(1)}) custom-call(s32[8]{0:T(128)S(1)} %pad_add_fusion.kept, bf16[16,2,8,16,256]{4,3,2,1,0:T(8,128)(2,1)S(1)} %bitcast.34, bf16[8,2,8,2,16,512]{5,4,3,2,1,0:T(8,128)(2,1)} %bitcast.15.mine, ...), custom_call_target="tpu_custom_call" | custom-call | tf_op jit(solution)/shard_map/products/pallas_call | solution.py:194
  163.9 27.0 %all_to_all.15.arrived = bf16[16,3,2,16,512]{4,3,2,1,0:T(8,128)(2,1)} all-to-all(bf16[16,3,2,16,512]{4,3,2,1,0:T(8,128)(2,1)S(1)} %get-tuple-element.15), channel_id=1, replica_groups=mesh['group'=32,'proc'=16] {'proc'}, dimensions={0} | all-to-all | bytes 3145728 | tf_op jit(solution)/shard_map/all_to_all | solution.py:211
  191.0 2.3 %final.1 = (bf16[2,16,512]{2,1,0:T(8,128)(2,1)}, bf16[8,2,16,512]{3,2,1,0:T(8,128)(2,1)}, bf16[2,16,512]{2,1,0:T(8,128)(2,1)}) custom-call(bf16[16,3,2,16,512]{4,3,2,1,0:T(8,128)(2,1)} %all_to_all.15.arrived, bf16[2,16,512]{2,1,0:T(8,128)(2,1)} %bitcast.37, bf16[2,16,512]{2,1,0:T(8,128)(2,1)} %bitcast.44, ...), custom_call_target="tpu_custom_call", output_to_operand_aliasing={{1}: (3, {})} | custom-call | tf_op jit(solution)/shard_map/final/pallas_call | solution.py:213
  (33 shorter events, 9.1 us)
Async XLA Ops:
  0.6 92.7 %copy-start = (s32[32,7]{0,1:T(8,128)S(1)}, s32[32,7]{0,1:T(8,128)}, u32[]{:S(2)}) copy-start(s32[32,7]{0,1:T(8,128)} %param.11) | copy-start | bytes 2692
  2.6 54.7 %collective-permute-start = (bf16[2,8,2,16,512]{4,3,2,1,0:T(8,128)(2,1)S(1)}, bf16[2,8,2,16,512]{4,3,2,1,0:T(8,128)(2,1)S(1)}, u32[]{:S(2)}, u32[]{:S(2)}) collective-permute-start(bf16[2,8,2,16,512]{4,3,2,1,0:T(8,128)(2,1)S(1)} %constant_dynamic-update-slice_fusion), channel_id=1, source_target_pairs={{0,2},{1,3},{2,4},{3,5},{4,6},{5,7},{6,0},{7,1},{8,10},{9,11},{10,... | collective-permute-start | bytes 1572872 | tf_op jit(solution)/shard_map/ppermute | solution.py:122
  6.5 55.0 %collective-permute-start.1 = (bf16[2,8,2,16,512]{4,3,2,1,0:T(8,128)(2,1)S(1)}, bf16[2,8,2,16,512]{4,3,2,1,0:T(8,128)(2,1)S(1)}, u32[]{:S(2)}, u32[]{:S(2)}) collective-permute-start(bf16[2,8,2,16,512]{4,3,2,1,0:T(8,128)(2,1)S(1)} %constant_dynamic-update-slice_fusion), channel_id=1, source_target_pairs={{0,4},{1,5},{2,6},{3,7},{4,0},{5,1},{6,2},{7,3},{8,12},{9,13},{10,... | collective-permute-start | bytes 1572872 | tf_op jit(solution)/shard_map/ppermute | solution.py:122
  10.9 51.6 %collective-permute-start.2 = (bf16[2,8,2,16,512]{4,3,2,1,0:T(8,128)(2,1)S(1)}, bf16[2,8,2,16,512]{4,3,2,1,0:T(8,128)(2,1)S(1)}, u32[]{:S(2)}, u32[]{:S(2)}) collective-permute-start(bf16[2,8,2,16,512]{4,3,2,1,0:T(8,128)(2,1)S(1)} %constant_dynamic-update-slice_fusion), channel_id=1, source_target_pairs={{0,6},{1,7},{2,0},{3,1},{4,2},{5,3},{6,4},{7,5},{8,14},{9,15},{10,... | collective-permute-start | bytes 1572872 | tf_op jit(solution)/shard_map/ppermute | solution.py:122
  14.0 38.3 %collective-permute-start.3 = (bf16[2,8,2,16,512]{4,3,2,1,0:T(8,128)(2,1)S(1)}, bf16[2,8,2,16,512]{4,3,2,1,0:T(8,128)(2,1)S(1)}, u32[]{:S(2)}, u32[]{:S(2)}) collective-permute-start(bf16[2,8,2,16,512]{4,3,2,1,0:T(8,128)(2,1)S(1)} %constant_dynamic-update-slice_fusion), channel_id=1, source_target_pairs={{0,8},{1,9},{2,10},{3,11},{4,12},{5,13},{6,14},{7,15},{8,0},{9,1},... | collective-permute-start | bytes 1572872 | tf_op jit(solution)/shard_map/ppermute | solution.py:122
  19.1 26.6 %all-to-all-start = ((bf16[32,16,256]{2,1,0:T(8,128)(2,1)}), bf16[32,16,256]{2,1,0:T(8,128)(2,1)S(1)}, u32[]{:S(2)}, u32[]{:S(2)}) async-start(bf16[32,16,256]{2,1,0:T(8,128)(2,1)} %bitcast.3), calls=%async_computation | async-start | bytes 524288 | tf_op jit(solution)/shard_map/all_to_all | solution.py:172
  52.3 14.2 %collective-permute-start.4 = (bf16[2,8,2,16,512]{4,3,2,1,0:T(8,128)(2,1)S(1)}, bf16[2,8,2,16,512]{4,3,2,1,0:T(8,128)(2,1)S(1)}, u32[]{:S(2)}, u32[]{:S(2)}) collective-permute-start(bf16[2,8,2,16,512]{4,3,2,1,0:T(8,128)(2,1)S(1)} %collective-permute-done.3), channel_id=1, source_target_pairs={{0,2},{1,3},{2,4},{3,5},{4,6},{5,7},{6,0},{7,1},{8,10},{9,11},{10,... | collective-permute-start | bytes 1572872 | tf_op jit(solution)/shard_map/ppermute | solution.py:122
  54.5 20.6 %collective-permute-start.5 = (bf16[2,8,2,16,512]{4,3,2,1,0:T(8,128)(2,1)S(1)}, bf16[2,8,2,16,512]{4,3,2,1,0:T(8,128)(2,1)S(1)}, u32[]{:S(2)}, u32[]{:S(2)}) collective-permute-start(bf16[2,8,2,16,512]{4,3,2,1,0:T(8,128)(2,1)S(1)} %collective-permute-done.3), channel_id=1, source_target_pairs={{0,4},{1,5},{2,6},{3,7},{4,0},{5,1},{6,2},{7,3},{8,12},{9,13},{10,... | collective-permute-start | bytes 1572872 | tf_op jit(solution)/shard_map/ppermute | solution.py:122
  57.3 24.7 %collective-permute-start.6 = (bf16[2,8,2,16,512]{4,3,2,1,0:T(8,128)(2,1)S(1)}, bf16[2,8,2,16,512]{4,3,2,1,0:T(8,128)(2,1)S(1)}, u32[]{:S(2)}, u32[]{:S(2)}) collective-permute-start(bf16[2,8,2,16,512]{4,3,2,1,0:T(8,128)(2,1)S(1)} %collective-permute-done.3), channel_id=1, source_target_pairs={{0,6},{1,7},{2,0},{3,1},{4,2},{5,3},{6,4},{7,5},{8,14},{9,15},{10,... | collective-permute-start | bytes 1572872 | tf_op jit(solution)/shard_map/ppermute | solution.py:122
  63.3 93.7 %copy-start.1 = (bf16[1,8,2,16,512]{4,3,2,1,0:T(8,128)(2,1)S(1)}, bf16[1,8,2,16,512]{4,3,2,1,0:T(8,128)(2,1)}, u32[]{:S(2)}) copy-start(bf16[1,8,2,16,512]{4,3,2,1,0:T(8,128)(2,1)} %param.12) | copy-start | bytes 786436
  63.3 93.7 %copy-start.2 = (bf16[1,8,2,16,512]{4,3,2,1,0:T(8,128)(2,1)S(1)}, bf16[1,8,2,16,512]{4,3,2,1,0:T(8,128)(2,1)}, u32[]{:S(2)}) copy-start(bf16[1,8,2,16,512]{4,3,2,1,0:T(8,128)(2,1)} %param.13) | copy-start | bytes 786436
  63.3 93.7 %copy-start.3 = (bf16[1,2,16,512]{3,2,1,0:T(8,128)(2,1)S(1)}, bf16[1,2,16,512]{3,2,1,0:T(8,128)(2,1)}, u32[]{:S(2)}) copy-start(bf16[1,2,16,512]{3,2,1,0:T(8,128)(2,1)} %param.14) | copy-start | bytes 98308
  82.7 74.3 %collective-permute-start.7 = (bf16[2,4,2,8,2,16,512]{6,5,4,3,2,1,0:T(8,128)(2,1)}, bf16[2,4,2,8,2,16,512]{6,5,4,3,2,1,0:T(8,128)(2,1)}, u32[]{:S(2)}, u32[]{:S(2)}) collective-permute-start(bf16[2,4,2,8,2,16,512]{6,5,4,3,2,1,0:T(8,128)(2,1)} %bitcast_dynamic-update-slice_fusion), channel_id=1, source_target_pairs={{0,1},{1,0},{2,3},{3,2},{4,5},{5,4},{6,7},{7,6},{8,9},{9,8},{10,11... | collective-permute-start | bytes 12582920 | tf_op jit(solution)/shard_map/ppermute | solution.py:122
  86.2 70.8 %all-to-all-start.1 = ((bf16[32,8,16,256]{3,2,1,0:T(8,128)(2,1)}), bf16[32,8,16,256]{3,2,1,0:T(8,128)(2,1)S(1)}, u32[]{:S(2)}, u32[]{:S(2)}) async-start(bf16[32,8,16,256]{3,2,1,0:T(8,128)(2,1)} %bitcast.39), calls=%async_computation.1 | async-start | bytes 4194304 | tf_op jit(solution)/shard_map/all_to_all | solution.py:184

commit v4 on v3

--- a/solution.py
+++ b/solution.py
@@ -22,7 +22,7 @@
 
 
 def products_kernel(
-    kept, upper, mine, theirs, own_first, own_second, pivot, column_out, child_out, sums_out, panels, sems
+    kept, upper, mine, theirs, own_first, own_second, pivot, column_out, child_out, keep_out, give_out, panels, sems
 ):
     strip, pieces, blocks, slabs, half = upper.shape
     procs, width = PROCS, panels.shape[-1]
@@ -97,9 +97,11 @@
         child_sum += dot_rows(top[h], head_sum[h * half : (h + 1) * half])
     for n, value in enumerate((parent_sum.astype(BF16), head_sum, child_sum.astype(BF16))):
         for h in range(pieces):
-            for p in range(procs):
-                start = h * half + p * strip
-                sums_out[p, n, h] = value[start : start + strip]
+            for place in range(procs // CORES):
+                start = h * half + place * CORES * strip
+                a, b = value[start : start + strip], value[start + strip : start + CORES * strip]
+                keep_out[place, n, h] = jnp.where(core == 0, a, b)
+                give_out[place, n, h] = jnp.where(core == 0, b, a)
 
 
 def final_kernel(arrived, pivot_first, pivot_second, child_in, block_first, child_out, block_second):
@@ -191,15 +193,16 @@
     smem = pl.BlockSpec(memory_space=pltpu.SMEM)
     vmem = pl.BlockSpec(memory_space=pltpu.VMEM)
     anywhere = pl.BlockSpec(memory_space=pl.ANY)
-    column_parent, column_child, sums = pl.pallas_call(
+    column_parent, column_child, keep, give = pl.pallas_call(
         products_kernel,
         out_shape=(
             jax.ShapeDtypeStruct((blocks, pieces, strip, width), BF16),
             jax.ShapeDtypeStruct((blocks, pieces, strip, width), BF16),
-            jax.ShapeDtypeStruct((procs, 3, pieces, strip, width), BF16),
+            jax.ShapeDtypeStruct((procs // CORES, 3, pieces, strip, width), BF16),
+            jax.ShapeDtypeStruct((procs // CORES, 3, pieces, strip, width), BF16),
         ),
         in_specs=[smem, vmem, anywhere, anywhere, vmem, vmem, vmem],
-        out_specs=(vmem, vmem, vmem),
+        out_specs=(vmem, vmem, vmem, vmem),
         scratch_shapes=[
             pltpu.VMEM(mine.shape[:1] + (CORES,) + mine.shape[1:], BF16),
             pltpu.SemaphoreType.DMA((2, blocks, 2)),
@@ -208,7 +211,11 @@
         interpret=INTERPRET,
         name="products",
     )(scalars, upper, mine, theirs, panel_parent[0], panel_child[0], pivot_parent[0])
-    arrived = lax.all_to_all(sums, "proc", split_axis=0, concat_axis=0, tiled=True)
+    sums = (keep.astype(F32) + moved(give, (0, 0, 1)).astype(F32)).astype(BF16)
+    same_core = [[place * CORES + c for place in range(procs // CORES)] for c in range(CORES)]
+    arrived = lax.all_to_all(
+        sums, "proc", split_axis=0, concat_axis=0, tiled=True, axis_index_groups=same_core
+    )
     whole = pl.BlockSpec((pieces, strip, width), lambda i: (0, 0, 0))
     block_parent, column_child, block_child = pl.pallas_call(
         final_kernel,

time: 196 us -> 192 us (0.980)
  blocking collectives: 27 us -> 15.6 us
  starting transfers between devices: 48.4 us -> 53.1 us
  waiting for transfers between devices: 89 us -> 91.4 us
    all_to_all x1, blocking collectives: 27 us -> 15.6 us  [per_device(): lax.all_to_all(sums, 'proc', split_axis=0, concat_axis=0, tiled=True, axi...]
    ppermute x8 -> x9, starting transfers between devices: 26.4 us -> 31.2 us  [moved(): return lax.ppermute(value, 'proc', pairs)]
    ppermute x8 -> x9, waiting for transfers between devices: 16.1 us -> 18 us  [moved(): return lax.ppermute(value, 'proc', pairs)]
  transfers between devices with their start and end apart: 10 -> 11, of which waited for: 5 -> 6; matrix products, arithmetic and copies ran while one was open for 8% -> 8% of each run, Pallas kernels for 0% -> 0%
where the time goes in v4:
time: 192 us; the launch traced here: 189 us
  waiting for transfers between devices  91.4 us (48%)
  starting transfers between devices  53.1 us (28%)
  blocking collectives  15.6 us (8%)
  local copies, waits for them, and re-layouts  15.2 us (8%)
  Pallas kernels  8.78 us (5%)
  matrix products  3.29 us (2%)
    all_to_all x1, waiting for transfers between devices, per_device(): lax.all_to_all(outgoing.reshape(groups, blocks, slabs, half), 'group', sp...  63.9 us
    ppermute x9, starting transfers between devices, moved(): return lax.ppermute(value, 'proc', pairs)  31.2 us
    ppermute x9, waiting for transfers between devices, moved(): return lax.ppermute(value, 'proc', pairs)  18 us
    all_to_all x1, blocking collectives, per_device(): lax.all_to_all(sums, 'proc', split_axis=0, concat_axis=0, tiled=True, axi...  15.6 us
    all_to_all x1, starting transfers between devices, per_device(): lax.all_to_all(spread.reshape(groups, tops, half), 'group', split_axis=0,...  14.8 us
    all_to_all x1, waiting for transfers between devices, per_device(): lax.all_to_all(spread.reshape(groups, tops, half), 'group', split_axis=0,...  9.52 us
    all_to_all x1, starting transfers between devices, per_device(): lax.all_to_all(outgoing.reshape(groups, blocks, slabs, half), 'group', sp...  7.14 us
    pallas_call x1, Pallas kernels, per_device(): pl.pallas_call(products_kernel, out_shape=(jax.ShapeDtypeStruct((blocks,...  6.9 us
  transfers between devices with their start and end apart: 11, of which 6 were waited for; matrix products, arithmetic and copies ran while one was open for 8% of the time, Pallas kernels for 0%

profile of v4, /device:TPU:1, one launch (start us, length us, event | category | flops | bytes accessed | tf_op | source)
XLA Modules:
  0.0 189.0 jit_solution(17497925510790266127)
XLA Ops:
  0.6 1.0 constant_dynamic-update-slice_fusion.1
  2.6 3.9 %collective-permute-start = (bf16[2,8,2,16,512]{4,3,2,1,0:T(8,128)(2,1)S(1)}, bf16[2,8,2,16,512]{4,3,2,1,0:T(8,128)(2,1)S(1)}, u32[]{:S(2)}, u32[]{:S(2)}) collective-permute-start(bf16[2,8,2,16,512]{4,3,2,1,0:T(8,128)(2,1)S(1)} %constant_dynamic-update-slice_fusion), channel_id=1, source_target_pairs={{0,2},{1,3},{2,4},{3,5},{4,6},{5,7},{6,0},{7,1},{8,10},{9,11},{10,... | collective-permute-start | bytes 1572872 | tf_op jit(solution)/shard_map/ppermute | solution.py:124
  6.5 4.4 %collective-permute-start.1 = (bf16[2,8,2,16,512]{4,3,2,1,0:T(8,128)(2,1)S(1)}, bf16[2,8,2,16,512]{4,3,2,1,0:T(8,128)(2,1)S(1)}, u32[]{:S(2)}, u32[]{:S(2)}) collective-permute-start(bf16[2,8,2,16,512]{4,3,2,1,0:T(8,128)(2,1)S(1)} %constant_dynamic-update-slice_fusion), channel_id=1, source_target_pairs={{0,4},{1,5},{2,6},{3,7},{4,0},{5,1},{6,2},{7,3},{8,12},{9,13},{10,... | collective-permute-start | bytes 1572872 | tf_op jit(solution)/shard_map/ppermute | solution.py:124
  10.9 3.1 %collective-permute-start.2 = (bf16[2,8,2,16,512]{4,3,2,1,0:T(8,128)(2,1)S(1)}, bf16[2,8,2,16,512]{4,3,2,1,0:T(8,128)(2,1)S(1)}, u32[]{:S(2)}, u32[]{:S(2)}) collective-permute-start(bf16[2,8,2,16,512]{4,3,2,1,0:T(8,128)(2,1)S(1)} %constant_dynamic-update-slice_fusion), channel_id=1, source_target_pairs={{0,6},{1,7},{2,0},{3,1},{4,2},{5,3},{6,4},{7,5},{8,14},{9,15},{10,... | collective-permute-start | bytes 1572872 | tf_op jit(solution)/shard_map/ppermute | solution.py:124
  14.0 3.2 %collective-permute-start.3 = (bf16[2,8,2,16,512]{4,3,2,1,0:T(8,128)(2,1)S(1)}, bf16[2,8,2,16,512]{4,3,2,1,0:T(8,128)(2,1)S(1)}, u32[]{:S(2)}, u32[]{:S(2)}) collective-permute-start(bf16[2,8,2,16,512]{4,3,2,1,0:T(8,128)(2,1)S(1)} %constant_dynamic-update-slice_fusion), channel_id=1, source_target_pairs={{0,8},{1,9},{2,10},{3,11},{4,12},{5,13},{6,14},{7,15},{8,0},{9,1},... | collective-permute-start | bytes 1572872 | tf_op jit(solution)/shard_map/ppermute | solution.py:124
  17.2 1.1 reshape.67
  19.1 14.8 %all-to-all-start = ((bf16[32,16,256]{2,1,0:T(8,128)(2,1)}), bf16[32,16,256]{2,1,0:T(8,128)(2,1)S(1)}, u32[]{:S(2)}, u32[]{:S(2)}) async-start(bf16[32,16,256]{2,1,0:T(8,128)(2,1)} %bitcast.3), calls=%async_computation | async-start | bytes 524288 | tf_op jit(solution)/shard_map/all_to_all | solution.py:174
  36.1 9.5 %all-to-all-done = bf16[32,16,256]{2,1,0:T(8,128)(2,1)S(1)} async-done(((bf16[32,16,256]{2,1,0:T(8,128)(2,1)}), bf16[32,16,256]{2,1,0:T(8,128)(2,1)S(1)}, u32[]{:S(2)}, u32[]{:S(2)}) %all-to-all-start) | async-done | bytes 262176 | tf_op jit(solution)/shard_map/all_to_all | solution.py:174
  45.7 3.3 %fusion = bf16[4096,256]{1,0:T(8,128)(2,1)} fusion(bf16[512,256]{1,0:T(8,128)(2,1)S(1)} %bitcast.42, s32[4096]{0:T(1024)S(1)} %add.64), kind=kOutput, calls=%fused_computation.1 | convolution fusion | flops 1075838976 | bytes 2375680 | tf_op jit(solution)/shard_map/dot_general | solution.py:182
  48.9 2.5 %broadcast_in_dim.66 = bf16[2,4,2,8,2,16,512]{6,5,4,3,2,1,0:T(8,128)(2,1)} broadcast(bf16[]{:T(256)} %constant.24.clone.1), dimensions={} | broadcast | bytes 4194306 | tf_op jit(solution)/shard_map/broadcast_in_dim | solution.py:183
  52.3 2.2 %collective-permute-start.4 = (bf16[2,8,2,16,512]{4,3,2,1,0:T(8,128)(2,1)S(1)}, bf16[2,8,2,16,512]{4,3,2,1,0:T(8,128)(2,1)S(1)}, u32[]{:S(2)}, u32[]{:S(2)}) collective-permute-start(bf16[2,8,2,16,512]{4,3,2,1,0:T(8,128)(2,1)S(1)} %collective-permute-done.3), channel_id=1, source_target_pairs={{0,2},{1,3},{2,4},{3,5},{4,6},{5,7},{6,0},{7,1},{8,10},{9,11},{10,... | collective-permute-start | bytes 1572872 | tf_op jit(solution)/shard_map/ppermute | solution.py:124
  54.5 2.8 %collective-permute-start.5 = (bf16[2,8,2,16,512]{4,3,2,1,0:T(8,128)(2,1)S(1)}, bf16[2,8,2,16,512]{4,3,2,1,0:T(8,128)(2,1)S(1)}, u32[]{:S(2)}, u32[]{:S(2)}) collective-permute-start(bf16[2,8,2,16,512]{4,3,2,1,0:T(8,128)(2,1)S(1)} %collective-permute-done.3), channel_id=1, source_target_pairs={{0,4},{1,5},{2,6},{3,7},{4,0},{5,1},{6,2},{7,3},{8,12},{9,13},{10,... | collective-permute-start | bytes 1572872 | tf_op jit(solution)/shard_map/ppermute | solution.py:124
  57.3 3.5 %collective-permute-start.6 = (bf16[2,8,2,16,512]{4,3,2,1,0:T(8,128)(2,1)S(1)}, bf16[2,8,2,16,512]{4,3,2,1,0:T(8,128)(2,1)S(1)}, u32[]{:S(2)}, u32[]{:S(2)}) collective-permute-start(bf16[2,8,2,16,512]{4,3,2,1,0:T(8,128)(2,1)S(1)} %collective-permute-done.3), channel_id=1, source_target_pairs={{0,6},{1,7},{2,0},{3,1},{4,2},{5,3},{6,4},{7,5},{8,14},{9,15},{10,... | collective-permute-start | bytes 1572872 | tf_op jit(solution)/shard_map/ppermute | solution.py:124
  64.2 2.3 %collective-permute-done.4 = bf16[2,8,2,16,512]{4,3,2,1,0:T(8,128)(2,1)S(1)} collective-permute-done((bf16[2,8,2,16,512]{4,3,2,1,0:T(8,128)(2,1)S(1)}, bf16[2,8,2,16,512]{4,3,2,1,0:T(8,128)(2,1)S(1)}, u32[]{:S(2)}, u32[]{:S(2)}) %collective-permute-start.4) | collective-permute-done | bytes 524320 | tf_op jit(solution)/shard_map/ppermute | solution.py:124
  67.4 7.8 %collective-permute-done.5 = bf16[2,8,2,16,512]{4,3,2,1,0:T(8,128)(2,1)S(1)} collective-permute-done((bf16[2,8,2,16,512]{4,3,2,1,0:T(8,128)(2,1)S(1)}, bf16[2,8,2,16,512]{4,3,2,1,0:T(8,128)(2,1)S(1)}, u32[]{:S(2)}, u32[]{:S(2)}) %collective-permute-start.5) | collective-permute-done | bytes 524320 | tf_op jit(solution)/shard_map/ppermute | solution.py:124
  75.9 6.0 %collective-permute-done.6 = bf16[2,8,2,16,512]{4,3,2,1,0:T(8,128)(2,1)S(1)} collective-permute-done((bf16[2,8,2,16,512]{4,3,2,1,0:T(8,128)(2,1)S(1)}, bf16[2,8,2,16,512]{4,3,2,1,0:T(8,128)(2,1)S(1)}, u32[]{:S(2)}, u32[]{:S(2)}) %collective-permute-start.6) | collective-permute-done | bytes 524320 | tf_op jit(solution)/shard_map/ppermute | solution.py:124
  82.8 3.5 %collective-permute-start.7 = (bf16[2,4,2,8,2,16,512]{6,5,4,3,2,1,0:T(8,128)(2,1)}, bf16[2,4,2,8,2,16,512]{6,5,4,3,2,1,0:T(8,128)(2,1)}, u32[]{:S(2)}, u32[]{:S(2)}) collective-permute-start(bf16[2,4,2,8,2,16,512]{6,5,4,3,2,1,0:T(8,128)(2,1)} %bitcast_dynamic-update-slice_fusion), channel_id=1, source_target_pairs={{0,1},{1,0},{2,3},{3,2},{4,5},{5,4},{6,7},{7,6},{8,9},{9,8},{10,11... | collective-permute-start | bytes 12582920 | tf_op jit(solution)/shard_map/ppermute | solution.py:124
  86.2 7.1 %all-to-all-start.1 = ((bf16[32,8,16,256]{3,2,1,0:T(8,128)(2,1)}), bf16[32,8,16,256]{3,2,1,0:T(8,128)(2,1)S(1)}, u32[]{:S(2)}, u32[]{:S(2)}) async-start(bf16[32,8,16,256]{3,2,1,0:T(8,128)(2,1)} %bitcast.39), calls=%async_computation.1 | async-start | bytes 4194304 | tf_op jit(solution)/shard_map/all_to_all | solution.py:186
  93.6 63.9 %all-to-all-done.1 = bf16[32,8,16,256]{3,2,1,0:T(8,128)(2,1)S(1)} async-done(((bf16[32,8,16,256]{3,2,1,0:T(8,128)(2,1)}), bf16[32,8,16,256]{3,2,1,0:T(8,128)(2,1)S(1)}, u32[]{:S(2)}, u32[]{:S(2)}) %all-to-all-start.1) | async-done | bytes 2097184 | tf_op jit(solution)/shard_map/all_to_all | solution.py:186
  157.6 6.9 %products.1 = (bf16[8,2,16,512]{3,2,1,0:T(8,128)(2,1)}, bf16[8,2,16,512]{3,2,1,0:T(8,128)(2,1)}, bf16[8,3,2,16,512]{4,3,2,1,0:T(8,128)(2,1)S(1)}, bf16[8,3,2,16,512]{4,3,2,1,0:T(8,128)(2,1)S(1)}) custom-call(s32[8]{0:T(128)S(1)} %pad_add_fusion.kept, bf16[16,2,8,16,256]{4,3,2,1,0:T(8,128)(2,1)S(1)} %bitcast.34, ...), custom_call_target="tpu_custom_call" | custom-call | tf_op jit(solution)/shard_map/products/pallas_call | solution.py:196
  164.5 4.8 %collective-permute-start.8 = (bf16[8,3,2,16,512]{4,3,2,1,0:T(8,128)(2,1)S(1)}, bf16[8,3,2,16,512]{4,3,2,1,0:T(8,128)(2,1)S(1)}, u32[]{:S(2)}, u32[]{:S(2)}) collective-permute-start(bf16[8,3,2,16,512]{4,3,2,1,0:T(8,128)(2,1)S(1)} %get-tuple-element.17), channel_id=1, source_target_pairs={{0,1},{1,0},{2,3},{3,2},{4,5},{5,4},{6,7},{7,6},{8,9},{9,8},{10,11... | collective-permute-start | bytes 2359304 | tf_op jit(solution)/shard_map/ppermute | solution.py:124
  169.3 1.9 %collective-permute-done.8 = bf16[8,3,2,16,512]{4,3,2,1,0:T(8,128)(2,1)S(1)} collective-permute-done((bf16[8,3,2,16,512]{4,3,2,1,0:T(8,128)(2,1)S(1)}, bf16[8,3,2,16,512]{4,3,2,1,0:T(8,128)(2,1)S(1)}, u32[]{:S(2)}, u32[]{:S(2)}) %collective-permute-start.8) | collective-permute-done | bytes 786464 | tf_op jit(solution)/shard_map/ppermute | solution.py:124
  171.5 15.6 %all_to_all.15.arrived = bf16[8,3,2,16,512]{4,3,2,1,0:T(8,128)(2,1)} all-to-all(bf16[8,3,2,16,512]{4,3,2,1,0:T(8,128)(2,1)S(1)} %add_convert_fusion), channel_id=1, replica_groups={{0,2,4,6,8,10,12,14},{1,3,5,7,9,11,13,15},{16,18,20,22,24,26,28,30},{17..., dimensions={0} | all-to-all | bytes 1572864 | tf_op jit(solution)/shard_map/all_to_all | solution.py:216
  187.1 1.9 final.1
  (36 shorter events, 11.3 us)
Async XLA Ops:
  0.6 92.7 %copy-start = (s32[32,7]{0,1:T(8,128)S(1)}, s32[32,7]{0,1:T(8,128)}, u32[]{:S(2)}) copy-start(s32[32,7]{0,1:T(8,128)} %param.11) | copy-start | bytes 2692
  2.6 54.7 %collective-permute-start = (bf16[2,8,2,16,512]{4,3,2,1,0:T(8,128)(2,1)S(1)}, bf16[2,8,2,16,512]{4,3,2,1,0:T(8,128)(2,1)S(1)}, u32[]{:S(2)}, u32[]{:S(2)}) collective-permute-start(bf16[2,8,2,16,512]{4,3,2,1,0:T(8,128)(2,1)S(1)} %constant_dynamic-update-slice_fusion), channel_id=1, source_target_pairs={{0,2},{1,3},{2,4},{3,5},{4,6},{5,7},{6,0},{7,1},{8,10},{9,11},{10,... | collective-permute-start | bytes 1572872 | tf_op jit(solution)/shard_map/ppermute | solution.py:124
  6.5 55.1 %collective-permute-start.1 = (bf16[2,8,2,16,512]{4,3,2,1,0:T(8,128)(2,1)S(1)}, bf16[2,8,2,16,512]{4,3,2,1,0:T(8,128)(2,1)S(1)}, u32[]{:S(2)}, u32[]{:S(2)}) collective-permute-start(bf16[2,8,2,16,512]{4,3,2,1,0:T(8,128)(2,1)S(1)} %constant_dynamic-update-slice_fusion), channel_id=1, source_target_pairs={{0,4},{1,5},{2,6},{3,7},{4,0},{5,1},{6,2},{7,3},{8,12},{9,13},{10,... | collective-permute-start | bytes 1572872 | tf_op jit(solution)/shard_map/ppermute | solution.py:124
  10.9 51.6 %collective-permute-start.2 = (bf16[2,8,2,16,512]{4,3,2,1,0:T(8,128)(2,1)S(1)}, bf16[2,8,2,16,512]{4,3,2,1,0:T(8,128)(2,1)S(1)}, u32[]{:S(2)}, u32[]{:S(2)}) collective-permute-start(bf16[2,8,2,16,512]{4,3,2,1,0:T(8,128)(2,1)S(1)} %constant_dynamic-update-slice_fusion), channel_id=1, source_target_pairs={{0,6},{1,7},{2,0},{3,1},{4,2},{5,3},{6,4},{7,5},{8,14},{9,15},{10,... | collective-permute-start | bytes 1572872 | tf_op jit(solution)/shard_map/ppermute | solution.py:124
  14.0 38.3 %collective-permute-start.3 = (bf16[2,8,2,16,512]{4,3,2,1,0:T(8,128)(2,1)S(1)}, bf16[2,8,2,16,512]{4,3,2,1,0:T(8,128)(2,1)S(1)}, u32[]{:S(2)}, u32[]{:S(2)}) collective-permute-start(bf16[2,8,2,16,512]{4,3,2,1,0:T(8,128)(2,1)S(1)} %constant_dynamic-update-slice_fusion), channel_id=1, source_target_pairs={{0,8},{1,9},{2,10},{3,11},{4,12},{5,13},{6,14},{7,15},{8,0},{9,1},... | collective-permute-start | bytes 1572872 | tf_op jit(solution)/shard_map/ppermute | solution.py:124
  19.1 26.6 %all-to-all-start = ((bf16[32,16,256]{2,1,0:T(8,128)(2,1)}), bf16[32,16,256]{2,1,0:T(8,128)(2,1)S(1)}, u32[]{:S(2)}, u32[]{:S(2)}) async-start(bf16[32,16,256]{2,1,0:T(8,128)(2,1)} %bitcast.3), calls=%async_computation | async-start | bytes 524288 | tf_op jit(solution)/shard_map/all_to_all | solution.py:174
  52.3 14.2 %collective-permute-start.4 = (bf16[2,8,2,16,512]{4,3,2,1,0:T(8,128)(2,1)S(1)}, bf16[2,8,2,16,512]{4,3,2,1,0:T(8,128)(2,1)S(1)}, u32[]{:S(2)}, u32[]{:S(2)}) collective-permute-start(bf16[2,8,2,16,512]{4,3,2,1,0:T(8,128)(2,1)S(1)} %collective-permute-done.3), channel_id=1, source_target_pairs={{0,2},{1,3},{2,4},{3,5},{4,6},{5,7},{6,0},{7,1},{8,10},{9,11},{10,... | collective-permute-start | bytes 1572872 | tf_op jit(solution)/shard_map/ppermute | solution.py:124
  54.5 20.6 %collective-permute-start.5 = (bf16[2,8,2,16,512]{4,3,2,1,0:T(8,128)(2,1)S(1)}, bf16[2,8,2,16,512]{4,3,2,1,0:T(8,128)(2,1)S(1)}, u32[]{:S(2)}, u32[]{:S(2)}) collective-permute-start(bf16[2,8,2,16,512]{4,3,2,1,0:T(8,128)(2,1)S(1)} %collective-permute-done.3), channel_id=1, source_target_pairs={{0,4},{1,5},{2,6},{3,7},{4,0},{5,1},{6,2},{7,3},{8,12},{9,13},{10,... | collective-permute-start | bytes 1572872 | tf_op jit(solution)/shard_map/ppermute | solution.py:124
  57.3 24.7 %collective-permute-start.6 = (bf16[2,8,2,16,512]{4,3,2,1,0:T(8,128)(2,1)S(1)}, bf16[2,8,2,16,512]{4,3,2,1,0:T(8,128)(2,1)S(1)}, u32[]{:S(2)}, u32[]{:S(2)}) collective-permute-start(bf16[2,8,2,16,512]{4,3,2,1,0:T(8,128)(2,1)S(1)} %collective-permute-done.3), channel_id=1, source_target_pairs={{0,6},{1,7},{2,0},{3,1},{4,2},{5,3},{6,4},{7,5},{8,14},{9,15},{10,... | collective-permute-start | bytes 1572872 | tf_op jit(solution)/shard_map/ppermute | solution.py:124
  63.3 94.2 %copy-start.1 = (bf16[1,8,2,16,512]{4,3,2,1,0:T(8,128)(2,1)S(1)}, bf16[1,8,2,16,512]{4,3,2,1,0:T(8,128)(2,1)}, u32[]{:S(2)}) copy-start(bf16[1,8,2,16,512]{4,3,2,1,0:T(8,128)(2,1)} %param.12) | copy-start | bytes 786436
  63.3 94.2 %copy-start.2 = (bf16[1,8,2,16,512]{4,3,2,1,0:T(8,128)(2,1)S(1)}, bf16[1,8,2,16,512]{4,3,2,1,0:T(8,128)(2,1)}, u32[]{:S(2)}) copy-start(bf16[1,8,2,16,512]{4,3,2,1,0:T(8,128)(2,1)} %param.13) | copy-start | bytes 786436
  63.3 94.2 %copy-start.3 = (bf16[1,2,16,512]{3,2,1,0:T(8,128)(2,1)S(1)}, bf16[1,2,16,512]{3,2,1,0:T(8,128)(2,1)}, u32[]{:S(2)}) copy-start(bf16[1,2,16,512]{3,2,1,0:T(8,128)(2,1)} %param.14) | copy-start | bytes 98308
  82.8 74.8 %collective-permute-start.7 = (bf16[2,4,2,8,2,16,512]{6,5,4,3,2,1,0:T(8,128)(2,1)}, bf16[2,4,2,8,2,16,512]{6,5,4,3,2,1,0:T(8,128)(2,1)}, u32[]{:S(2)}, u32[]{:S(2)}) collective-permute-start(bf16[2,4,2,8,2,16,512]{6,5,4,3,2,1,0:T(8,128)(2,1)} %bitcast_dynamic-update-slice_fusion), channel_id=1, source_target_pairs={{0,1},{1,0},{2,3},{3,2},{4,5},{5,4},{6,7},{7,6},{8,9},{9,8},{10,11... | collective-permute-start | bytes 12582920 | tf_op jit(solution)/shard_map/ppermute | solution.py:124
  86.2 71.3 %all-to-all-start.1 = ((bf16[32,8,16,256]{3,2,1,0:T(8,128)(2,1)}), bf16[32,8,16,256]{3,2,1,0:T(8,128)(2,1)S(1)}, u32[]{:S(2)}, u32[]{:S(2)}) async-start(bf16[32,8,16,256]{3,2,1,0:T(8,128)(2,1)} %bitcast.39), calls=%async_computation.1 | async-start | bytes 4194304 | tf_op jit(solution)/shard_map/all_to_all | solution.py:186
  164.5 6.7 %collective-permute-start.8 = (bf16[8,3,2,16,512]{4,3,2,1,0:T(8,128)(2,1)S(1)}, bf16[8,3,2,16,512]{4,3,2,1,0:T(8,128)(2,1)S(1)}, u32[]{:S(2)}, u32[]{:S(2)}) collective-permute-start(bf16[8,3,2,16,512]{4,3,2,1,0:T(8,128)(2,1)S(1)} %get-tuple-element.17), channel_id=1, source_target_pairs={{0,1},{1,0},{2,3},{3,2},{4,5},{5,4},{6,7},{7,6},{8,9},{9,8},{10,11... | collective-permute-start | bytes 2359304 | tf_op jit(solution)/shard_map/ppermute | solution.py:124

commit v5 on v4

--- a/solution.py
+++ b/solution.py
@@ -22,19 +22,22 @@
 
 
 def products_kernel(
-    kept, upper, mine, theirs, own_first, own_second, pivot, column_out, child_out, keep_out, give_out, panels, sems
+    kept, received, near, near_other, far, far_other, own_first, own_second, pivot, column_out, child_out, keep_out, give_out, upper, panels, sems, upper_sems
 ):
     strip, pieces, blocks, slabs, half = upper.shape
     procs, width = PROCS, panels.shape[-1]
     rows = strip * slabs
-    core = kept[blocks - 1]
+    core, y = kept[blocks - 1], kept[blocks]
+    sources = ((near, y, core), (near_other, y, 1 - core), (far, 1 - y, core), (far_other, 1 - y, 1 - core))
     order = [(1, 0)] + [(0, b) for b in range(blocks)] + [(1, b) for b in range(1, blocks)]
     copies = {}
     for n, b in order:
         copies[n, b] = [
-            pltpu.make_async_copy(mine.at[:, n, b], panels.at[:, core, n, b], sems.at[n, b, 0]),
-            pltpu.make_async_copy(theirs.at[:, n, b], panels.at[:, 1 - core, n, b], sems.at[n, b, 1]),
+            pltpu.make_async_copy(source.at[:, n, b], panels.at[at_y, :, at_core, n, b], sems.at[n, b, k])
+            for k, (source, at_y, at_core) in enumerate(sources)
         ]
+        if n == 0:
+            copies[n, b].append(pltpu.make_async_copy(received.at[:, :, b], upper.at[:, :, b], upper_sems.at[b]))
         for copy in copies[n, b]:
             copy.start()
 
@@ -42,7 +45,7 @@
         return upper[:, h, b].reshape(rows, half)
 
     def right(n, b, h):
-        return panels[:, :, n, b, h].reshape(half, width)
+        return panels[:, :, :, n, b, h].reshape(half, width)
 
     def arrive(n, b):
         for copy in copies[n, b]:
@@ -70,16 +73,6 @@
     column_out[...] = column_natural.reshape(column_out.shape)
 
     top = [right(1, 0, h) for h in range(pieces)]
-    total = jnp.zeros((rows, width), F32)
-    for b in range(1, blocks):
-        arrive(1, b)
-        for h in range(pieces):
-            total += dot(left(h, kept[b - 1]), right(1, b, h))
-    for h in range(pieces):
-        total += dot(column[:, h * half : (h + 1) * half], top[h])
-    child = dot(in_child, (-total).astype(BF16)).astype(BF16)
-    child_out[...] = child.reshape(child_out.shape)
-
     first = own_first[...].reshape(rows, width)
     second = own_second[...].reshape(rows, width)
     diagonal = pivot[...].reshape(strip * pieces, width)
@@ -92,9 +85,20 @@
         - dot_rows(column_natural, cross.astype(BF16))
         + dot_rows(diagonal, second[: strip * pieces])
     ).astype(BF16)
-    child_sum = -dot_rows(second, child)
+    child_sum = jnp.zeros((width, width), F32)
     for h in range(pieces):
         child_sum += dot_rows(top[h], head_sum[h * half : (h + 1) * half])
+
+    total = jnp.zeros((rows, width), F32)
+    for b in range(1, blocks):
+        arrive(1, b)
+        for h in range(pieces):
+            total += dot(left(h, kept[b - 1]), right(1, b, h))
+    for h in range(pieces):
+        total += dot(column[:, h * half : (h + 1) * half], top[h])
+    child = dot(in_child, (-total).astype(BF16)).astype(BF16)
+    child_out[...] = child.reshape(child_out.shape)
+    child_sum -= dot_rows(second, child)
     for n, value in enumerate((parent_sum.astype(BF16), head_sum, child_sum.astype(BF16))):
         for h in range(pieces):
             for place in range(procs // CORES):
@@ -129,23 +133,24 @@
 
 
 def shifted(shard):
-    here = lax.axis_index("proc")
-    y, x = here >> 3, (here >> 1) & (XS - 1)
+    x = (lax.axis_index("proc") >> 1) & (XS - 1)
     other = moved(shard, (1, 0, 0))
-    parts = []
-    for dy, part in ((0, shard), (1, other)):
-        for dx in range(XS):
-            arrived = moved(part, (0, dx, 0)) if dx else part
-            parts.append((arrived, ((y + dy) & (YS - 1), (x - dx) & (XS - 1))))
-    return parts
-
-
-def gathered(parts, start):
-    for part, where in parts:
-        start = placed(start, part[None, None], where)
-    other_core = moved(start, (0, 0, 1))
-    shape = (YS * XS,) + start.shape[2:]
-    return start.reshape(shape), other_core.reshape(shape)
+    rows = []
+    for part in (shard, other):
+        row = [(part, x)]
+        for dx in range(1, XS):
+            row.append((moved(part, (0, dx, 0)), (x - dx) & (XS - 1)))
+        rows.append(row)
+    return rows
+
+
+def gathered(rows, starts):
+    both = []
+    for row, start in zip(rows, starts):
+        for part, x in row:
+            start = placed(start, part[None], (x,))
+        both += [start, moved(start, (0, 0, 1))]
+    return both
 
 
 def per_device(
@@ -168,7 +173,7 @@
     tops = ancestor_rows.shape[2] // width
     slabs = blocks * pieces
 
-    parts = shifted(jnp.stack([panel_parent[0], panel_child[0]]))
+    rows = shifted(jnp.stack([panel_parent[0], panel_child[0]]))
 
     spread = ancestor_rows.reshape(strip, tops, pieces, half).transpose(0, 2, 1, 3)
     spread = lax.all_to_all(
@@ -180,16 +185,18 @@
     index = owner[:, None, :] * tops + structure[:, :, None]
     choice = jax.nn.one_hot(index.reshape(-1), groups * tops, dtype=BF16)
     outgoing = jnp.dot(choice, spread.reshape(groups * tops, half), preferred_element_type=BF16)
-    start = jnp.zeros((YS, XS) + parts[0][0].shape, BF16)
-    outgoing, start = lax.optimization_barrier((outgoing, start))
-    mine, theirs = gathered(parts, start)
+    panels_shape = (XS, 2) + panel_parent.shape[1:]
+    starts = [jnp.zeros(panels_shape, BF16) for _ in range(YS)]
+    outgoing, starts = lax.optimization_barrier((outgoing, starts))
+    gathered_panels = gathered(rows, starts)
     upper = lax.all_to_all(
         outgoing.reshape(groups, blocks, slabs, half), "group", split_axis=0, concat_axis=0, tiled=True
     )
     upper = upper.reshape(strip, pieces, blocks, slabs, half)
 
-    core = lax.axis_index("proc") & (CORES - 1)
-    scalars = jnp.concatenate([kept_blocks[group_index], core[None].astype(jnp.int32)])
+    here = lax.axis_index("proc")
+    place = jnp.stack([here & (CORES - 1), here >> 3]).astype(jnp.int32)
+    scalars = jnp.concatenate([kept_blocks[group_index], place])
     smem = pl.BlockSpec(memory_space=pltpu.SMEM)
     vmem = pl.BlockSpec(memory_space=pltpu.VMEM)
     anywhere = pl.BlockSpec(memory_space=pl.ANY)
@@ -201,16 +208,18 @@
             jax.ShapeDtypeStruct((procs // CORES, 3, pieces, strip, width), BF16),
             jax.ShapeDtypeStruct((procs // CORES, 3, pieces, strip, width), BF16),
         ),
-        in_specs=[smem, vmem, anywhere, anywhere, vmem, vmem, vmem],
+        in_specs=[smem] + [anywhere] * 5 + [vmem] * 3,
         out_specs=(vmem, vmem, vmem, vmem),
         scratch_shapes=[
-            pltpu.VMEM(mine.shape[:1] + (CORES,) + mine.shape[1:], BF16),
-            pltpu.SemaphoreType.DMA((2, blocks, 2)),
+            pltpu.VMEM(upper.shape, BF16),
+            pltpu.VMEM((YS, XS, CORES) + panels_shape[1:], BF16),
+            pltpu.SemaphoreType.DMA((2, blocks, 4)),
+            pltpu.SemaphoreType.DMA((blocks,)),
         ],
         compiler_params=pltpu.CompilerParams(vmem_limit_bytes=32 * 1024 * 1024),
         interpret=INTERPRET,
         name="products",
-    )(scalars, upper, mine, theirs, panel_parent[0], panel_child[0], pivot_parent[0])
+    )(scalars, upper, *gathered_panels, panel_parent[0], panel_child[0], pivot_parent[0])
     sums = (keep.astype(F32) + moved(give, (0, 0, 1)).astype(F32)).astype(BF16)
     same_core = [[place * CORES + c for place in range(procs // CORES)] for c in range(CORES)]
     arrived = lax.all_to_all(

time: 192 us -> 156 us (0.81)
  the two profiles are of different devices: /device:TPU:1 before, /device:TPU:120 now
where the time goes in v5:
time: 156 us; the launch traced here: 155 us
  starting transfers between devices  51.5 us (33%)
  waiting for transfers between devices  39.1 us (25%)
  blocking collectives  36.4 us (23%)
  local copies, waits for them, and re-layouts  12.9 us (8%)
  Pallas kernels  10.2 us (7%)
  matrix products  3.24 us (2%)
    all_to_all x1, blocking collectives, per_device(): lax.all_to_all(sums, 'proc', split_axis=0, concat_axis=0, tiled=True, axi...  36.4 us
    ppermute x10, starting transfers between devices, moved(): return lax.ppermute(value, 'proc', pairs)  29.5 us
    ppermute x10, waiting for transfers between devices, moved(): return lax.ppermute(value, 'proc', pairs)  18.9 us
    all_to_all x1, starting transfers between devices, per_device(): lax.all_to_all(spread.reshape(groups, tops, half), 'group', split_axis=0,...  14.7 us
    all_to_all x1, waiting for transfers between devices, per_device(): lax.all_to_all(outgoing.reshape(groups, blocks, slabs, half), 'group', sp...  10.6 us
    all_to_all x1, waiting for transfers between devices, per_device(): lax.all_to_all(spread.reshape(groups, tops, half), 'group', split_axis=0,...  9.62 us
    pallas_call x1, Pallas kernels, per_device(): pl.pallas_call(products_kernel, out_shape=(jax.ShapeDtypeStruct((blocks,...  8.34 us
    all_to_all x1, starting transfers between devices, per_device(): lax.all_to_all(outgoing.reshape(groups, blocks, slabs, half), 'group', sp...  7.26 us
  transfers between devices with their start and end apart: 12, of which 6 were waited for; matrix products, arithmetic and copies ran while one was open for 9% of the time, Pallas kernels for 0%

profile of v5, /device:TPU:120, one launch (start us, length us, event | category | flops | bytes accessed | tf_op | source)
XLA Modules:
  0.0 155.1 jit_solution(6733927856793346376)
XLA Ops:
  2.6 3.4 %collective-permute-start = (bf16[2,8,2,16,512]{4,3,2,1,0:T(8,128)(2,1)S(1)}, bf16[2,8,2,16,512]{4,3,2,1,0:T(8,128)(2,1)}, u32[]{:S(2)}, u32[]{:S(2)}) collective-permute-start(bf16[2,8,2,16,512]{4,3,2,1,0:T(8,128)(2,1)S(1)} %constant_dynamic-update-slice_fusion), channel_id=1, source_target_pairs={{0,2},{1,3},{2,4},{3,5},{4,6},{5,7},{6,0},{7,1},{8,10},{9,11},{10,... | collective-permute-start | bytes 1572872 | tf_op jit(solution)/shard_map/ppermute | solution.py:128
  6.0 4.6 %collective-permute-start.1 = (bf16[2,8,2,16,512]{4,3,2,1,0:T(8,128)(2,1)S(1)}, bf16[2,8,2,16,512]{4,3,2,1,0:T(8,128)(2,1)}, u32[]{:S(2)}, u32[]{:S(2)}) collective-permute-start(bf16[2,8,2,16,512]{4,3,2,1,0:T(8,128)(2,1)S(1)} %constant_dynamic-update-slice_fusion), channel_id=1, source_target_pairs={{0,4},{1,5},{2,6},{3,7},{4,0},{5,1},{6,2},{7,3},{8,12},{9,13},{10,... | collective-permute-start | bytes 1572872 | tf_op jit(solution)/shard_map/ppermute | solution.py:128
  10.7 3.3 %collective-permute-start.2 = (bf16[2,8,2,16,512]{4,3,2,1,0:T(8,128)(2,1)S(1)}, bf16[2,8,2,16,512]{4,3,2,1,0:T(8,128)(2,1)}, u32[]{:S(2)}, u32[]{:S(2)}) collective-permute-start(bf16[2,8,2,16,512]{4,3,2,1,0:T(8,128)(2,1)S(1)} %constant_dynamic-update-slice_fusion), channel_id=1, source_target_pairs={{0,6},{1,7},{2,0},{3,1},{4,2},{5,3},{6,4},{7,5},{8,14},{9,15},{10,... | collective-permute-start | bytes 1572872 | tf_op jit(solution)/shard_map/ppermute | solution.py:128
  14.0 3.3 %collective-permute-start.4 = (bf16[2,8,2,16,512]{4,3,2,1,0:T(8,128)(2,1)S(1)}, bf16[2,8,2,16,512]{4,3,2,1,0:T(8,128)(2,1)S(1)}, u32[]{:S(2)}, u32[]{:S(2)}) collective-permute-start(bf16[2,8,2,16,512]{4,3,2,1,0:T(8,128)(2,1)S(1)} %constant_dynamic-update-slice_fusion), channel_id=1, source_target_pairs={{0,8},{1,9},{2,10},{3,11},{4,12},{5,13},{6,14},{7,15},{8,0},{9,1},... | collective-permute-start | bytes 1572872 | tf_op jit(solution)/shard_map/ppermute | solution.py:128
  17.3 1.1 reshape.61
  19.2 14.7 %all-to-all-start = ((bf16[32,16,256]{2,1,0:T(8,128)(2,1)}), bf16[32,16,256]{2,1,0:T(8,128)(2,1)S(1)}, u32[]{:S(2)}, u32[]{:S(2)}) async-start(bf16[32,16,256]{2,1,0:T(8,128)(2,1)} %bitcast.4), calls=%async_computation | async-start | bytes 524288 | tf_op jit(solution)/shard_map/all_to_all | solution.py:179
  34.8 9.6 %all-to-all-done = bf16[32,16,256]{2,1,0:T(8,128)(2,1)S(1)} async-done(((bf16[32,16,256]{2,1,0:T(8,128)(2,1)}), bf16[32,16,256]{2,1,0:T(8,128)(2,1)S(1)}, u32[]{:S(2)}, u32[]{:S(2)}) %all-to-all-start) | async-done | bytes 262176 | tf_op jit(solution)/shard_map/all_to_all | solution.py:179
  44.4 3.2 %fusion = bf16[4096,256]{1,0:T(8,128)(2,1)} fusion(bf16[512,256]{1,0:T(8,128)(2,1)S(1)} %bitcast.39, s32[4096]{0:T(1024)S(1)} %add.46), kind=kOutput, calls=%fused_computation.1 | convolution fusion | flops 1075838976 | bytes 2375680 | tf_op jit(solution)/shard_map/dot_general | solution.py:187
  47.7 7.3 %all-to-all-start.1 = ((bf16[32,8,16,256]{3,2,1,0:T(8,128)(2,1)}), bf16[32,8,16,256]{3,2,1,0:T(8,128)(2,1)}, u32[]{:S(2)}, u32[]{:S(2)}) async-start(bf16[32,8,16,256]{3,2,1,0:T(8,128)(2,1)} %bitcast.6), calls=%async_computation.1 | async-start | bytes 4194304 | tf_op jit(solution)/shard_map/all_to_all | solution.py:192
  55.2 1.4 copy.29
  56.6 2.5 %collective-permute-start.5 = (bf16[2,8,2,16,512]{4,3,2,1,0:T(8,128)(2,1)S(1)}, bf16[2,8,2,16,512]{4,3,2,1,0:T(8,128)(2,1)S(1)}, u32[]{:S(2)}, u32[]{:S(2)}) collective-permute-start(bf16[2,8,2,16,512]{4,3,2,1,0:T(8,128)(2,1)S(1)} %collective-permute-done.4), channel_id=1, source_target_pairs={{0,2},{1,3},{2,4},{3,5},{4,6},{5,7},{6,0},{7,1},{8,10},{9,11},{10,... | collective-permute-start | bytes 1572872 | tf_op jit(solution)/shard_map/ppermute | solution.py:128
  59.1 3.1 %collective-permute-start.6 = (bf16[2,8,2,16,512]{4,3,2,1,0:T(8,128)(2,1)S(1)}, bf16[2,8,2,16,512]{4,3,2,1,0:T(8,128)(2,1)S(1)}, u32[]{:S(2)}, u32[]{:S(2)}) collective-permute-start(bf16[2,8,2,16,512]{4,3,2,1,0:T(8,128)(2,1)S(1)} %collective-permute-done.4), channel_id=1, source_target_pairs={{0,4},{1,5},{2,6},{3,7},{4,0},{5,1},{6,2},{7,3},{8,12},{9,13},{10,... | collective-permute-start | bytes 1572872 | tf_op jit(solution)/shard_map/ppermute | solution.py:128
  64.4 1.1 bitcast_dynamic-update-slice_fusion.4.near
  65.5 2.1 %collective-permute-start.3 = (bf16[4,2,8,2,16,512]{5,4,3,2,1,0:T(8,128)(2,1)S(1)}, bf16[4,2,8,2,16,512]{5,4,3,2,1,0:T(8,128)(2,1)}, u32[]{:S(2)}, u32[]{:S(2)}) collective-permute-start(bf16[4,2,8,2,16,512]{5,4,3,2,1,0:T(8,128)(2,1)S(1)} %bitcast_dynamic-update-slice_fusion.4.near), channel_id=1, source_target_pairs={{0,1},{1,0},{2,3},{3,2},{4,5},{5,4},{6,7},{7,6},{8,9},{9,8},{10,11... | collective-permute-start | bytes 6291464 | tf_op jit(solution)/shard_map/ppermute | solution.py:128
  67.6 3.4 %collective-permute-start.7 = (bf16[2,8,2,16,512]{4,3,2,1,0:T(8,128)(2,1)S(1)}, bf16[2,8,2,16,512]{4,3,2,1,0:T(8,128)(2,1)S(1)}, u32[]{:S(2)}, u32[]{:S(2)}) collective-permute-start(bf16[2,8,2,16,512]{4,3,2,1,0:T(8,128)(2,1)S(1)} %collective-permute-done.4), channel_id=1, source_target_pairs={{0,6},{1,7},{2,0},{3,1},{4,2},{5,3},{6,4},{7,5},{8,14},{9,15},{10,... | collective-permute-start | bytes 1572872 | tf_op jit(solution)/shard_map/ppermute | solution.py:128
  71.9 11.7 %collective-permute-done.5 = bf16[2,8,2,16,512]{4,3,2,1,0:T(8,128)(2,1)S(1)} collective-permute-done((bf16[2,8,2,16,512]{4,3,2,1,0:T(8,128)(2,1)S(1)}, bf16[2,8,2,16,512]{4,3,2,1,0:T(8,128)(2,1)S(1)}, u32[]{:S(2)}, u32[]{:S(2)}) %collective-permute-start.5) | collective-permute-done | bytes 524320 | tf_op jit(solution)/shard_map/ppermute | solution.py:128
  86.9 1.9 %collective-permute-start.8 = (bf16[4,2,8,2,16,512]{5,4,3,2,1,0:T(8,128)(2,1)}, bf16[4,2,8,2,16,512]{5,4,3,2,1,0:T(8,128)(2,1)}, u32[]{:S(2)}, u32[]{:S(2)}) collective-permute-start(bf16[4,2,8,2,16,512]{5,4,3,2,1,0:T(8,128)(2,1)} %bitcast_dynamic-update-slice_fusion.far), channel_id=1, source_target_pairs={{0,1},{1,0},{2,3},{3,2},{4,5},{5,4},{6,7},{7,6},{8,9},{9,8},{10,11... | collective-permute-start | bytes 6291464 | tf_op jit(solution)/shard_map/ppermute | solution.py:128
  89.1 4.2 %collective-permute-done.8.far_other = bf16[4,2,8,2,16,512]{5,4,3,2,1,0:T(8,128)(2,1)} collective-permute-done((bf16[4,2,8,2,16,512]{5,4,3,2,1,0:T(8,128)(2,1)}, bf16[4,2,8,2,16,512]{5,4,3,2,1,0:T(8,128)(2,1)}, u32[]{:S(2)}, u32[]{:S(2)}) %collective-permute-start.8) | collective-permute-done | bytes 2097184 | tf_op jit(solution)/shard_map/ppermute | solution.py:128
  93.3 10.6 %all-to-all-done.1 = bf16[32,8,16,256]{3,2,1,0:T(8,128)(2,1)} async-done(((bf16[32,8,16,256]{3,2,1,0:T(8,128)(2,1)}), bf16[32,8,16,256]{3,2,1,0:T(8,128)(2,1)}, u32[]{:S(2)}, u32[]{:S(2)}) %all-to-all-start.1) | async-done | bytes 2097184 | tf_op jit(solution)/shard_map/all_to_all | solution.py:192
  103.9 8.3 %products.1 = (bf16[8,2,16,512]{3,2,1,0:T(8,128)(2,1)}, bf16[8,2,16,512]{3,2,1,0:T(8,128)(2,1)}, bf16[8,3,2,16,512]{4,3,2,1,0:T(8,128)(2,1)S(1)}, bf16[8,3,2,16,512]{4,3,2,1,0:T(8,128)(2,1)S(1)}) custom-call(s32[9]{0:T(128)S(1)} %pad_add_fusion.kept, bf16[16,2,8,16,256]{4,3,2,1,0:T(8,128)(2,1)} %bitcast.7.received, ...), custom_call_target="tpu_custom_call" | custom-call | tf_op jit(solution)/shard_map/products/pallas_call | solution.py:203
  112.3 1.9 %collective-permute-start.9 = (bf16[8,3,2,16,512]{4,3,2,1,0:T(8,128)(2,1)S(1)}, bf16[8,3,2,16,512]{4,3,2,1,0:T(8,128)(2,1)S(1)}, u32[]{:S(2)}, u32[]{:S(2)}) collective-permute-start(bf16[8,3,2,16,512]{4,3,2,1,0:T(8,128)(2,1)S(1)} %get-tuple-element.19), channel_id=1, source_target_pairs={{0,1},{1,0},{2,3},{3,2},{4,5},{5,4},{6,7},{7,6},{8,9},{9,8},{10,11... | collective-permute-start | bytes 2359304 | tf_op jit(solution)/shard_map/ppermute | solution.py:128
  114.2 2.3 %collective-permute-done.9 = bf16[8,3,2,16,512]{4,3,2,1,0:T(8,128)(2,1)S(1)} collective-permute-done((bf16[8,3,2,16,512]{4,3,2,1,0:T(8,128)(2,1)S(1)}, bf16[8,3,2,16,512]{4,3,2,1,0:T(8,128)(2,1)S(1)}, u32[]{:S(2)}, u32[]{:S(2)}) %collective-permute-start.9) | collective-permute-done | bytes 786464 | tf_op jit(solution)/shard_map/ppermute | solution.py:128
  116.8 36.4 %all_to_all.15.arrived = bf16[8,3,2,16,512]{4,3,2,1,0:T(8,128)(2,1)} all-to-all(bf16[8,3,2,16,512]{4,3,2,1,0:T(8,128)(2,1)S(1)} %add_convert_fusion), channel_id=1, replica_groups={{0,2,4,6,8,10,12,14},{1,3,5,7,9,11,13,15},{16,18,20,22,24,26,28,30},{17..., dimensions={0} | all-to-all | bytes 1572864 | tf_op jit(solution)/shard_map/all_to_all | solution.py:225
  153.2 1.9 %final.1 = (bf16[2,16,512]{2,1,0:T(8,128)(2,1)}, bf16[8,2,16,512]{3,2,1,0:T(8,128)(2,1)}, bf16[2,16,512]{2,1,0:T(8,128)(2,1)}) custom-call(bf16[8,3,2,16,512]{4,3,2,1,0:T(8,128)(2,1)} %all_to_all.15.arrived, bf16[2,16,512]{2,1,0:T(8,128)(2,1)} %bitcast.35, bf16[2,16,512]{2,1,0:T(8,128)(2,1)} %bitcast.40, ...), custom_call_target="tpu_custom_call", output_to_operand_aliasing={{1}: (3, {})} | custom-call | tf_op jit(solution)/shard_map/final/pallas_call | solution.py:229
  (43 shorter events, 10.8 us)
Async XLA Ops:
  0.6 88.2 %copy-start = (s32[32,7]{0,1:T(8,128)S(1)}, s32[32,7]{0,1:T(8,128)}, u32[]{:S(2)}) copy-start(s32[32,7]{0,1:T(8,128)} %param.11) | copy-start | bytes 2692
  0.6 33.3 %copy-start.5 = (s32[32]{0:T(128)S(1)}, s32[32]{0:T(128)}, u32[]{:S(2)}) copy-start(s32[32]{0:T(128)} %param.9) | copy-start | bytes 388
  0.7 33.4 %copy-start.4 = (s32[32,8]{0,1:T(8,128)S(1)}, s32[32,8]{0,1:T(8,128)}, u32[]{:S(2)}) copy-start(s32[32,8]{0,1:T(8,128)} %param.10) | copy-start | bytes 3076
  2.6 59.6 %collective-permute-start = (bf16[2,8,2,16,512]{4,3,2,1,0:T(8,128)(2,1)S(1)}, bf16[2,8,2,16,512]{4,3,2,1,0:T(8,128)(2,1)}, u32[]{:S(2)}, u32[]{:S(2)}) collective-permute-start(bf16[2,8,2,16,512]{4,3,2,1,0:T(8,128)(2,1)S(1)} %constant_dynamic-update-slice_fusion), channel_id=1, source_target_pairs={{0,2},{1,3},{2,4},{3,5},{4,6},{5,7},{6,0},{7,1},{8,10},{9,11},{10,... | collective-permute-start | bytes 1572872 | tf_op jit(solution)/shard_map/ppermute | solution.py:128
  6.0 57.3 %collective-permute-start.1 = (bf16[2,8,2,16,512]{4,3,2,1,0:T(8,128)(2,1)S(1)}, bf16[2,8,2,16,512]{4,3,2,1,0:T(8,128)(2,1)}, u32[]{:S(2)}, u32[]{:S(2)}) collective-permute-start(bf16[2,8,2,16,512]{4,3,2,1,0:T(8,128)(2,1)S(1)} %constant_dynamic-update-slice_fusion), channel_id=1, source_target_pairs={{0,4},{1,5},{2,6},{3,7},{4,0},{5,1},{6,2},{7,3},{8,12},{9,13},{10,... | collective-permute-start | bytes 1572872 | tf_op jit(solution)/shard_map/ppermute | solution.py:128
  10.7 53.7 %collective-permute-start.2 = (bf16[2,8,2,16,512]{4,3,2,1,0:T(8,128)(2,1)S(1)}, bf16[2,8,2,16,512]{4,3,2,1,0:T(8,128)(2,1)}, u32[]{:S(2)}, u32[]{:S(2)}) collective-permute-start(bf16[2,8,2,16,512]{4,3,2,1,0:T(8,128)(2,1)S(1)} %constant_dynamic-update-slice_fusion), channel_id=1, source_target_pairs={{0,6},{1,7},{2,0},{3,1},{4,2},{5,3},{6,4},{7,5},{8,14},{9,15},{10,... | collective-permute-start | bytes 1572872 | tf_op jit(solution)/shard_map/ppermute | solution.py:128
  14.0 42.6 %collective-permute-start.4 = (bf16[2,8,2,16,512]{4,3,2,1,0:T(8,128)(2,1)S(1)}, bf16[2,8,2,16,512]{4,3,2,1,0:T(8,128)(2,1)S(1)}, u32[]{:S(2)}, u32[]{:S(2)}) collective-permute-start(bf16[2,8,2,16,512]{4,3,2,1,0:T(8,128)(2,1)S(1)} %constant_dynamic-update-slice_fusion), channel_id=1, source_target_pairs={{0,8},{1,9},{2,10},{3,11},{4,12},{5,13},{6,14},{7,15},{8,0},{9,1},... | collective-permute-start | bytes 1572872 | tf_op jit(solution)/shard_map/ppermute | solution.py:128
  19.2 25.2 %all-to-all-start = ((bf16[32,16,256]{2,1,0:T(8,128)(2,1)}), bf16[32,16,256]{2,1,0:T(8,128)(2,1)S(1)}, u32[]{:S(2)}, u32[]{:S(2)}) async-start(bf16[32,16,256]{2,1,0:T(8,128)(2,1)} %bitcast.4), calls=%async_computation | async-start | bytes 524288 | tf_op jit(solution)/shard_map/all_to_all | solution.py:179
  47.7 56.2 %all-to-all-start.1 = ((bf16[32,8,16,256]{3,2,1,0:T(8,128)(2,1)}), bf16[32,8,16,256]{3,2,1,0:T(8,128)(2,1)}, u32[]{:S(2)}, u32[]{:S(2)}) async-start(bf16[32,8,16,256]{3,2,1,0:T(8,128)(2,1)} %bitcast.6), calls=%async_computation.1 | async-start | bytes 4194304 | tf_op jit(solution)/shard_map/all_to_all | solution.py:192
  56.6 27.0 %collective-permute-start.5 = (bf16[2,8,2,16,512]{4,3,2,1,0:T(8,128)(2,1)S(1)}, bf16[2,8,2,16,512]{4,3,2,1,0:T(8,128)(2,1)S(1)}, u32[]{:S(2)}, u32[]{:S(2)}) collective-permute-start(bf16[2,8,2,16,512]{4,3,2,1,0:T(8,128)(2,1)S(1)} %collective-permute-done.4), channel_id=1, source_target_pairs={{0,2},{1,3},{2,4},{3,5},{4,6},{5,7},{6,0},{7,1},{8,10},{9,11},{10,... | collective-permute-start | bytes 1572872 | tf_op jit(solution)/shard_map/ppermute | solution.py:128
  59.1 25.4 %collective-permute-start.6 = (bf16[2,8,2,16,512]{4,3,2,1,0:T(8,128)(2,1)S(1)}, bf16[2,8,2,16,512]{4,3,2,1,0:T(8,128)(2,1)S(1)}, u32[]{:S(2)}, u32[]{:S(2)}) collective-permute-start(bf16[2,8,2,16,512]{4,3,2,1,0:T(8,128)(2,1)S(1)} %collective-permute-done.4), channel_id=1, source_target_pairs={{0,4},{1,5},{2,6},{3,7},{4,0},{5,1},{6,2},{7,3},{8,12},{9,13},{10,... | collective-permute-start | bytes 1572872 | tf_op jit(solution)/shard_map/ppermute | solution.py:128
  65.5 38.4 %copy-start.1 = (bf16[1,8,2,16,512]{4,3,2,1,0:T(8,128)(2,1)S(1)}, bf16[1,8,2,16,512]{4,3,2,1,0:T(8,128)(2,1)}, u32[]{:S(2)}) copy-start(bf16[1,8,2,16,512]{4,3,2,1,0:T(8,128)(2,1)} %param.12) | copy-start | bytes 786436
  65.5 38.4 %copy-start.2 = (bf16[1,8,2,16,512]{4,3,2,1,0:T(8,128)(2,1)S(1)}, bf16[1,8,2,16,512]{4,3,2,1,0:T(8,128)(2,1)}, u32[]{:S(2)}) copy-start(bf16[1,8,2,16,512]{4,3,2,1,0:T(8,128)(2,1)} %param.13) | copy-start | bytes 786436
  65.5 38.4 %copy-start.3 = (bf16[1,2,16,512]{3,2,1,0:T(8,128)(2,1)S(1)}, bf16[1,2,16,512]{3,2,1,0:T(8,128)(2,1)}, u32[]{:S(2)}) copy-start(bf16[1,2,16,512]{3,2,1,0:T(8,128)(2,1)} %param.14) | copy-start | bytes 98308
  65.5 23.6 %collective-permute-start.3 = (bf16[4,2,8,2,16,512]{5,4,3,2,1,0:T(8,128)(2,1)S(1)}, bf16[4,2,8,2,16,512]{5,4,3,2,1,0:T(8,128)(2,1)}, u32[]{:S(2)}, u32[]{:S(2)}) collective-permute-start(bf16[4,2,8,2,16,512]{5,4,3,2,1,0:T(8,128)(2,1)S(1)} %bitcast_dynamic-update-slice_fusion.4.near), channel_id=1, source_target_pairs={{0,1},{1,0},{2,3},{3,2},{4,5},{5,4},{6,7},{7,6},{8,9},{9,8},{10,11... | collective-permute-start | bytes 6291464 | tf_op jit(solution)/shard_map/ppermute | solution.py:128
  67.6 18.5 %collective-permute-start.7 = (bf16[2,8,2,16,512]{4,3,2,1,0:T(8,128)(2,1)S(1)}, bf16[2,8,2,16,512]{4,3,2,1,0:T(8,128)(2,1)S(1)}, u32[]{:S(2)}, u32[]{:S(2)}) collective-permute-start(bf16[2,8,2,16,512]{4,3,2,1,0:T(8,128)(2,1)S(1)} %collective-permute-done.4), channel_id=1, source_target_pairs={{0,6},{1,7},{2,0},{3,1},{4,2},{5,3},{6,4},{7,5},{8,14},{9,15},{10,... | collective-permute-start | bytes 1572872 | tf_op jit(solution)/shard_map/ppermute | solution.py:128
  86.9 6.4 %collective-permute-start.8 = (bf16[4,2,8,2,16,512]{5,4,3,2,1,0:T(8,128)(2,1)}, bf16[4,2,8,2,16,512]{5,4,3,2,1,0:T(8,128)(2,1)}, u32[]{:S(2)}, u32[]{:S(2)}) collective-permute-start(bf16[4,2,8,2,16,512]{5,4,3,2,1,0:T(8,128)(2,1)} %bitcast_dynamic-update-slice_fusion.far), channel_id=1, source_target_pairs={{0,1},{1,0},{2,3},{3,2},{4,5},{5,4},{6,7},{7,6},{8,9},{9,8},{10,11... | collective-permute-start | bytes 6291464 | tf_op jit(solution)/shard_map/ppermute | solution.py:128
  112.3 4.2 %collective-permute-start.9 = (bf16[8,3,2,16,512]{4,3,2,1,0:T(8,128)(2,1)S(1)}, bf16[8,3,2,16,512]{4,3,2,1,0:T(8,128)(2,1)S(1)}, u32[]{:S(2)}, u32[]{:S(2)}) collective-permute-start(bf16[8,3,2,16,512]{4,3,2,1,0:T(8,128)(2,1)S(1)} %get-tuple-element.19), channel_id=1, source_target_pairs={{0,1},{1,0},{2,3},{3,2},{4,5},{5,4},{6,7},{7,6},{8,9},{9,8},{10,11... | collective-permute-start | bytes 2359304 | tf_op jit(solution)/shard_map/ppermute | solution.py:128

commit v6 on v5

--- a/solution.py
+++ b/solution.py
@@ -22,7 +22,7 @@
 
 
 def products_kernel(
-    kept, received, near, near_other, far, far_other, own_first, own_second, pivot, column_out, child_out, keep_out, give_out, upper, panels, sems, upper_sems
+    kept, upper, near, near_other, far, far_other, own_first, own_second, pivot, column_out, child_out, keep_out, give_out, panels, sems
 ):
     strip, pieces, blocks, slabs, half = upper.shape
     procs, width = PROCS, panels.shape[-1]
@@ -36,8 +36,6 @@
             pltpu.make_async_copy(source.at[:, n, b], panels.at[at_y, :, at_core, n, b], sems.at[n, b, k])
             for k, (source, at_y, at_core) in enumerate(sources)
         ]
-        if n == 0:
-            copies[n, b].append(pltpu.make_async_copy(received.at[:, :, b], upper.at[:, :, b], upper_sems.at[b]))
         for copy in copies[n, b]:
             copy.start()
 
@@ -128,28 +126,45 @@
     return lax.ppermute(value, "proc", pairs)
 
 
-def placed(buffer, value, where):
-    return lax.dynamic_update_slice(buffer, value, tuple(where) + (0,) * (buffer.ndim - len(where)))
+def assemble_kernel(place, *refs):
+    parts, out, sems = refs[:XS], refs[XS], refs[XS + 1]
+    copies = [
+        pltpu.make_async_copy(part, out.at[(place[0] - dx) & (XS - 1)], sems.at[dx])
+        for dx, part in enumerate(parts)
+    ]
+    for copy in copies:
+        copy.start()
+    for copy in copies:
+        copy.wait()
 
 
 def shifted(shard):
-    x = (lax.axis_index("proc") >> 1) & (XS - 1)
     other = moved(shard, (1, 0, 0))
     rows = []
     for part in (shard, other):
-        row = [(part, x)]
+        row = [part]
         for dx in range(1, XS):
-            row.append((moved(part, (0, dx, 0)), (x - dx) & (XS - 1)))
+            row.append(moved(part, (0, dx, 0)))
         rows.append(row)
     return rows
 
 
-def gathered(rows, starts):
+def gathered(rows):
+    place = ((lax.axis_index("proc") >> 1) & (XS - 1))[None].astype(jnp.int32)
+    anywhere = pl.BlockSpec(memory_space=pl.ANY)
     both = []
-    for row, start in zip(rows, starts):
-        for part, x in row:
-            start = placed(start, part[None], (x,))
-        both += [start, moved(start, (0, 0, 1))]
+    for row in rows:
+        together = pl.pallas_call(
+            assemble_kernel,
+            out_shape=pltpu.HBM((XS,) + row[0].shape, BF16),
+            in_specs=[pl.BlockSpec(memory_space=pltpu.SMEM)] + [anywhere] * XS,
+            out_specs=pl.BlockSpec(memory_space=pltpu.HBM),
+            scratch_shapes=[pltpu.SemaphoreType.DMA((XS,))],
+            interpret=INTERPRET,
+            name="assemble",
+        )(place, *row)
+        pair = [together, moved(together, (0, 0, 1))]
+        both += [pltpu.with_memory_space_constraint(half, pltpu.HBM) for half in pair]
     return both
 
 
@@ -186,9 +201,7 @@
     choice = jax.nn.one_hot(index.reshape(-1), groups * tops, dtype=BF16)
     outgoing = jnp.dot(choice, spread.reshape(groups * tops, half), preferred_element_type=BF16)
     panels_shape = (XS, 2) + panel_parent.shape[1:]
-    starts = [jnp.zeros(panels_shape, BF16) for _ in range(YS)]
-    outgoing, starts = lax.optimization_barrier((outgoing, starts))
-    gathered_panels = gathered(rows, starts)
+    gathered_panels = gathered(rows)
     upper = lax.all_to_all(
         outgoing.reshape(groups, blocks, slabs, half), "group", split_axis=0, concat_axis=0, tiled=True
     )
@@ -208,13 +221,11 @@
             jax.ShapeDtypeStruct((procs // CORES, 3, pieces, strip, width), BF16),
             jax.ShapeDtypeStruct((procs // CORES, 3, pieces, strip, width), BF16),
         ),
-        in_specs=[smem] + [anywhere] * 5 + [vmem] * 3,
+        in_specs=[smem, vmem] + [anywhere] * 4 + [vmem] * 3,
         out_specs=(vmem, vmem, vmem, vmem),
         scratch_shapes=[
-            pltpu.VMEM(upper.shape, BF16),
             pltpu.VMEM((YS, XS, CORES) + panels_shape[1:], BF16),
             pltpu.SemaphoreType.DMA((2, blocks, 4)),
-            pltpu.SemaphoreType.DMA((blocks,)),
         ],
         compiler_params=pltpu.CompilerParams(vmem_limit_bytes=32 * 1024 * 1024),
         interpret=INTERPRET,

time: 156 us -> 286 us (1.83)
  the two profiles are of different devices: /device:TPU:120 before, /device:TPU:256 now
where the time goes in v6:
time: 286 us
  Pallas kernels  139 us (49%)
  waiting for transfers between devices  67.7 us (24%)
  starting transfers between devices  50.9 us (18%)
  blocking collectives  18.3 us (6%)
  local copies, waits for them, and re-layouts  3.88 us (1%)
    pallas_call x2, Pallas kernels, gathered(): pl.pallas_call(assemble_kernel, out_shape=pltpu.HBM((XS,) + row[0].shape,...  129 us
    ppermute x10, waiting for transfers between devices, moved(): return lax.ppermute(value, 'proc', pairs)  59.8 us
    ppermute x10, starting transfers between devices, moved(): return lax.ppermute(value, 'proc', pairs)  29.6 us
    all_to_all x1, blocking collectives, per_device(): lax.all_to_all(sums, 'proc', split_axis=0, concat_axis=0, tiled=True, axi...  18.3 us
    all_to_all x1, starting transfers between devices, per_device(): lax.all_to_all(spread.reshape(groups, tops, half), 'group', split_axis=0,...  12.7 us
    all_to_all x1, starting transfers between devices, per_device(): lax.all_to_all(outgoing.reshape(groups, blocks, slabs, half), 'group', sp...  8.59 us
    pallas_call x1, Pallas kernels, per_device(): pl.pallas_call(products_kernel, out_shape=(jax.ShapeDtypeStruct((blocks,...  8.05 us
    all_to_all x1, waiting for transfers between devices, per_device(): lax.all_to_all(spread.reshape(groups, tops, half), 'group', split_axis=0,...  7.97 us
  transfers between devices with their start and end apart: 12, of which 4 were waited for; matrix products, arithmetic and copies ran while one was open for 1% of the time, Pallas kernels for 45%

profile of v6, /device:TPU:256, one launch (start us, length us, event | category | flops | bytes accessed | tf_op | source)
XLA Modules:
  0.0 285.6 jit_solution(12289077104854991215)
XLA Ops:
  0.6 1.1 reshape.79
  2.5 12.7 %all-to-all-start = ((bf16[32,16,256]{2,1,0:T(8,128)(2,1)}), bf16[32,16,256]{2,1,0:T(8,128)(2,1)S(1)}, u32[]{:S(2)}, u32[]{:S(2)}) async-start(bf16[32,16,256]{2,1,0:T(8,128)(2,1)} %bitcast.5), calls=%async_computation | async-start | bytes 524288 | tf_op jit(solution)/shard_map/all_to_all | solution.py:194
  17.7 8.0 %all-to-all-done = bf16[32,16,256]{2,1,0:T(8,128)(2,1)S(1)} async-done(((bf16[32,16,256]{2,1,0:T(8,128)(2,1)}), bf16[32,16,256]{2,1,0:T(8,128)(2,1)S(1)}, u32[]{:S(2)}, u32[]{:S(2)}) %all-to-all-start) | async-done | bytes 262176 | tf_op jit(solution)/shard_map/all_to_all | solution.py:194
  25.6 2.7 fusion.1
  28.4 8.6 %all-to-all-start.1 = ((bf16[32,8,16,256]{3,2,1,0:T(8,128)(2,1)}), bf16[32,8,16,256]{3,2,1,0:T(8,128)(2,1)S(1)}, u32[]{:S(2)}, u32[]{:S(2)}) async-start(bf16[32,8,16,256]{3,2,1,0:T(8,128)(2,1)} %fusion.1), calls=%async_computation.1 | async-start | bytes 4194304 | tf_op jit(solution)/shard_map/all_to_all | solution.py:205
  37.0 2.3 collective-permute-start.4
  39.3 4.7 %collective-permute-start.2 = (bf16[2,8,2,16,512]{4,3,2,1,0:T(8,128)(2,1)S(1)}, bf16[2,8,2,16,512]{4,3,2,1,0:T(8,128)(2,1)S(1)}, u32[]{:S(2)}, u32[]{:S(2)}) collective-permute-start(bf16[2,8,2,16,512]{4,3,2,1,0:T(8,128)(2,1)S(1)} %constant_dynamic-update-slice_fusion.refs_0_), channel_id=1, source_target_pairs={{0,6},{1,7},{2,0},{3,1},{4,2},{5,3},{6,4},{7,5},{8,14},{9,15},{10,... | collective-permute-start | bytes 1572872 | tf_op jit(solution)/shard_map/ppermute | solution.py:126
  44.0 2.7 collective-permute-start.1
  46.7 2.8 collective-permute-start
  49.5 54.0 %collective-permute-done.4.refs_0_ = bf16[2,8,2,16,512]{4,3,2,1,0:T(8,128)(2,1)} collective-permute-done((bf16[2,8,2,16,512]{4,3,2,1,0:T(8,128)(2,1)S(1)}, bf16[2,8,2,16,512]{4,3,2,1,0:T(8,128)(2,1)}, u32[]{:S(2)}, u32[]{:S(2)}) %collective-permute-start.4) | collective-permute-done | bytes 524320 | tf_op jit(solution)/shard_map/ppermute | solution.py:126
  103.6 4.3 %collective-permute-start.7 = (bf16[2,8,2,16,512]{4,3,2,1,0:T(8,128)(2,1)}, bf16[2,8,2,16,512]{4,3,2,1,0:T(8,128)(2,1)}, u32[]{:S(2)}, u32[]{:S(2)}) collective-permute-start(bf16[2,8,2,16,512]{4,3,2,1,0:T(8,128)(2,1)} %collective-permute-done.4.refs_0_), channel_id=1, source_target_pairs={{0,6},{1,7},{2,0},{3,1},{4,2},{5,3},{6,4},{7,5},{8,14},{9,15},{10,... | collective-permute-start | bytes 1572872 | tf_op jit(solution)/shard_map/ppermute | solution.py:126
  107.9 2.9 %collective-permute-start.6 = (bf16[2,8,2,16,512]{4,3,2,1,0:T(8,128)(2,1)}, bf16[2,8,2,16,512]{4,3,2,1,0:T(8,128)(2,1)}, u32[]{:S(2)}, u32[]{:S(2)}) collective-permute-start(bf16[2,8,2,16,512]{4,3,2,1,0:T(8,128)(2,1)} %collective-permute-done.4.refs_0_), channel_id=1, source_target_pairs={{0,4},{1,5},{2,6},{3,7},{4,0},{5,1},{6,2},{7,3},{8,12},{9,13},{10,... | collective-permute-start | bytes 1572872 | tf_op jit(solution)/shard_map/ppermute | solution.py:126
  110.8 0.8 copy-done.5
  111.6 3.3 %collective-permute-start.5 = (bf16[2,8,2,16,512]{4,3,2,1,0:T(8,128)(2,1)}, bf16[2,8,2,16,512]{4,3,2,1,0:T(8,128)(2,1)}, u32[]{:S(2)}, u32[]{:S(2)}) collective-permute-start(bf16[2,8,2,16,512]{4,3,2,1,0:T(8,128)(2,1)} %collective-permute-done.4.refs_0_), channel_id=1, source_target_pairs={{0,2},{1,3},{2,4},{3,5},{4,6},{5,7},{6,0},{7,1},{8,10},{9,11},{10,... | collective-permute-start | bytes 1572872 | tf_op jit(solution)/shard_map/ppermute | solution.py:126
  115.0 64.7 %assemble.2.near = bf16[4,2,8,2,16,512]{5,4,3,2,1,0:T(8,128)(2,1)} custom-call(s32[1]{0:T(128)} %bitcast.10.place, bf16[2,8,2,16,512]{4,3,2,1,0:T(8,128)(2,1)} %copy-done.4, bf16[2,8,2,16,512]{4,3,2,1,0:T(8,128)(2,1)} %collective-permute-done.refs_1_, bf16[2,8,2,16,512]{4,3,2,1,0:T(8,128)(2,1)} %collective-permute-done.1.refs_2_, ...), custom_call_target="tpu_custom_call" | custom-call | tf_op jit(solution)/shard_map/assemble/pallas_call | solution.py:157
  179.7 1.9 collective-permute-start.3
  181.6 64.7 %assemble.3.far = bf16[4,2,8,2,16,512]{5,4,3,2,1,0:T(8,128)(2,1)} custom-call(s32[1]{0:T(128)} %bitcast.10.place, bf16[2,8,2,16,512]{4,3,2,1,0:T(8,128)(2,1)} %collective-permute-done.4.refs_0_, bf16[2,8,2,16,512]{4,3,2,1,0:T(8,128)(2,1)} %collective-permute-done.5.refs_1_, bf16[2,8,2,16,512]{4,3,2,1,0:T(8,128)(2,1)} %collective-permute-done.6.refs_2_, ...), custom_call_target="tpu_custom_call" | custom-call | tf_op jit(solution)/shard_map/assemble/pallas_call | solution.py:157
  246.3 2.4 collective-permute-start.8
  249.0 3.8 %collective-permute-done.8.far_other = bf16[4,2,8,2,16,512]{5,4,3,2,1,0:T(8,128)(2,1)} collective-permute-done((bf16[4,2,8,2,16,512]{5,4,3,2,1,0:T(8,128)(2,1)}, bf16[4,2,8,2,16,512]{5,4,3,2,1,0:T(8,128)(2,1)}, u32[]{:S(2)}, u32[]{:S(2)}) %collective-permute-start.8) | collective-permute-done | bytes 2097184 | tf_op jit(solution)/shard_map/ppermute | solution.py:126
  252.8 8.1 %products.1 = (bf16[8,2,16,512]{3,2,1,0:T(8,128)(2,1)}, bf16[8,2,16,512]{3,2,1,0:T(8,128)(2,1)}, bf16[8,3,2,16,512]{4,3,2,1,0:T(8,128)(2,1)S(1)}, bf16[8,3,2,16,512]{4,3,2,1,0:T(8,128)(2,1)S(1)}) custom-call(s32[9]{0:T(128)S(1)} %pad_add_fusion.kept, bf16[16,2,8,16,256]{4,3,2,1,0:T(8,128)(2,1)S(1)} %bitcast.24, ...), custom_call_target="tpu_custom_call" | custom-call | tf_op jit(solution)/shard_map/products/pallas_call | solution.py:216
  260.9 2.3 collective-permute-start.9
  263.2 1.9 collective-permute-done.9
  265.4 18.3 %all_to_all.15.arrived = bf16[8,3,2,16,512]{4,3,2,1,0:T(8,128)(2,1)} all-to-all(bf16[8,3,2,16,512]{4,3,2,1,0:T(8,128)(2,1)S(1)} %add_convert_fusion), channel_id=1, replica_groups={{0,2,4,6,8,10,12,14},{1,3,5,7,9,11,13,15},{16,18,20,22,24,26,28,30},{17..., dimensions={0} | all-to-all | bytes 1572864 | tf_op jit(solution)/shard_map/all_to_all | solution.py:236
  283.8 1.9 final.1
  (32 shorter events, 3.9 us)
Async XLA Ops:
  0.6 248.1 %copy-start = (s32[32,7]{0,1:T(8,128)S(1)}, s32[32,7]{0,1:T(8,128)}, u32[]{:S(2)}) copy-start(s32[32,7]{0,1:T(8,128)} %param.11) | copy-start | bytes 2692
  2.5 23.1 %all-to-all-start = ((bf16[32,16,256]{2,1,0:T(8,128)(2,1)}), bf16[32,16,256]{2,1,0:T(8,128)(2,1)S(1)}, u32[]{:S(2)}, u32[]{:S(2)}) async-start(bf16[32,16,256]{2,1,0:T(8,128)(2,1)} %bitcast.5), calls=%async_computation | async-start | bytes 524288 | tf_op jit(solution)/shard_map/all_to_all | solution.py:194
  28.4 8.6 %copy-start.1 = (bf16[1,8,2,16,512]{4,3,2,1,0:T(8,128)(2,1)S(1)}, bf16[1,8,2,16,512]{4,3,2,1,0:T(8,128)(2,1)}, u32[]{:S(2)}) copy-start(bf16[1,8,2,16,512]{4,3,2,1,0:T(8,128)(2,1)} %param.12) | copy-start | bytes 786436
  28.4 8.6 %copy-start.2 = (bf16[1,8,2,16,512]{4,3,2,1,0:T(8,128)(2,1)S(1)}, bf16[1,8,2,16,512]{4,3,2,1,0:T(8,128)(2,1)}, u32[]{:S(2)}) copy-start(bf16[1,8,2,16,512]{4,3,2,1,0:T(8,128)(2,1)} %param.13) | copy-start | bytes 786436
  28.4 224.5 %all-to-all-start.1 = ((bf16[32,8,16,256]{3,2,1,0:T(8,128)(2,1)}), bf16[32,8,16,256]{3,2,1,0:T(8,128)(2,1)S(1)}, u32[]{:S(2)}, u32[]{:S(2)}) async-start(bf16[32,8,16,256]{3,2,1,0:T(8,128)(2,1)} %fusion.1), calls=%async_computation.1 | async-start | bytes 4194304 | tf_op jit(solution)/shard_map/all_to_all | solution.py:205
  37.0 77.9 %copy-start.4 = (bf16[2,8,2,16,512]{4,3,2,1,0:T(8,128)(2,1)}, bf16[2,8,2,16,512]{4,3,2,1,0:T(8,128)(2,1)S(1)}, u32[]{:S(2)}) copy-start(bf16[2,8,2,16,512]{4,3,2,1,0:T(8,128)(2,1)S(1)} %constant_dynamic-update-slice_fusion.refs_0_) | copy-start | bytes 1572868
  37.0 66.5 %collective-permute-start.4 = (bf16[2,8,2,16,512]{4,3,2,1,0:T(8,128)(2,1)S(1)}, bf16[2,8,2,16,512]{4,3,2,1,0:T(8,128)(2,1)}, u32[]{:S(2)}, u32[]{:S(2)}) collective-permute-start(bf16[2,8,2,16,512]{4,3,2,1,0:T(8,128)(2,1)S(1)} %constant_dynamic-update-slice_fusion.refs_0_), channel_id=1, source_target_pairs={{0,8},{1,9},{2,10},{3,11},{4,12},{5,13},{6,14},{7,15},{8,0},{9,1},... | collective-permute-start | bytes 1572872 | tf_op jit(solution)/shard_map/ppermute | solution.py:126
  39.3 71.5 %collective-permute-start.2 = (bf16[2,8,2,16,512]{4,3,2,1,0:T(8,128)(2,1)S(1)}, bf16[2,8,2,16,512]{4,3,2,1,0:T(8,128)(2,1)S(1)}, u32[]{:S(2)}, u32[]{:S(2)}) collective-permute-start(bf16[2,8,2,16,512]{4,3,2,1,0:T(8,128)(2,1)S(1)} %constant_dynamic-update-slice_fusion.refs_0_), channel_id=1, source_target_pairs={{0,6},{1,7},{2,0},{3,1},{4,2},{5,3},{6,4},{7,5},{8,14},{9,15},{10,... | collective-permute-start | bytes 1572872 | tf_op jit(solution)/shard_map/ppermute | solution.py:126
  44.0 70.9 %collective-permute-start.1 = (bf16[2,8,2,16,512]{4,3,2,1,0:T(8,128)(2,1)S(1)}, bf16[2,8,2,16,512]{4,3,2,1,0:T(8,128)(2,1)}, u32[]{:S(2)}, u32[]{:S(2)}) collective-permute-start(bf16[2,8,2,16,512]{4,3,2,1,0:T(8,128)(2,1)S(1)} %constant_dynamic-update-slice_fusion.refs_0_), channel_id=1, source_target_pairs={{0,4},{1,5},{2,6},{3,7},{4,0},{5,1},{6,2},{7,3},{8,12},{9,13},{10,... | collective-permute-start | bytes 1572872 | tf_op jit(solution)/shard_map/ppermute | solution.py:126
  46.7 68.2 %collective-permute-start = (bf16[2,8,2,16,512]{4,3,2,1,0:T(8,128)(2,1)S(1)}, bf16[2,8,2,16,512]{4,3,2,1,0:T(8,128)(2,1)}, u32[]{:S(2)}, u32[]{:S(2)}) collective-permute-start(bf16[2,8,2,16,512]{4,3,2,1,0:T(8,128)(2,1)S(1)} %constant_dynamic-update-slice_fusion.refs_0_), channel_id=1, source_target_pairs={{0,2},{1,3},{2,4},{3,5},{4,6},{5,7},{6,0},{7,1},{8,10},{9,11},{10,... | collective-permute-start | bytes 1572872 | tf_op jit(solution)/shard_map/ppermute | solution.py:126
  103.6 78.1 %collective-permute-start.7 = (bf16[2,8,2,16,512]{4,3,2,1,0:T(8,128)(2,1)}, bf16[2,8,2,16,512]{4,3,2,1,0:T(8,128)(2,1)}, u32[]{:S(2)}, u32[]{:S(2)}) collective-permute-start(bf16[2,8,2,16,512]{4,3,2,1,0:T(8,128)(2,1)} %collective-permute-done.4.refs_0_), channel_id=1, source_target_pairs={{0,6},{1,7},{2,0},{3,1},{4,2},{5,3},{6,4},{7,5},{8,14},{9,15},{10,... | collective-permute-start | bytes 1572872 | tf_op jit(solution)/shard_map/ppermute | solution.py:126
  107.9 73.7 %collective-permute-start.6 = (bf16[2,8,2,16,512]{4,3,2,1,0:T(8,128)(2,1)}, bf16[2,8,2,16,512]{4,3,2,1,0:T(8,128)(2,1)}, u32[]{:S(2)}, u32[]{:S(2)}) collective-permute-start(bf16[2,8,2,16,512]{4,3,2,1,0:T(8,128)(2,1)} %collective-permute-done.4.refs_0_), channel_id=1, source_target_pairs={{0,4},{1,5},{2,6},{3,7},{4,0},{5,1},{6,2},{7,3},{8,12},{9,13},{10,... | collective-permute-start | bytes 1572872 | tf_op jit(solution)/shard_map/ppermute | solution.py:126
  110.8 0.8 copy-start.5
  111.6 70.0 %collective-permute-start.5 = (bf16[2,8,2,16,512]{4,3,2,1,0:T(8,128)(2,1)}, bf16[2,8,2,16,512]{4,3,2,1,0:T(8,128)(2,1)}, u32[]{:S(2)}, u32[]{:S(2)}) collective-permute-start(bf16[2,8,2,16,512]{4,3,2,1,0:T(8,128)(2,1)} %collective-permute-done.4.refs_0_), channel_id=1, source_target_pairs={{0,2},{1,3},{2,4},{3,5},{4,6},{5,7},{6,0},{7,1},{8,10},{9,11},{10,... | collective-permute-start | bytes 1572872 | tf_op jit(solution)/shard_map/ppermute | solution.py:126
  179.7 73.2 %copy-start.3 = (bf16[1,2,16,512]{3,2,1,0:T(8,128)(2,1)S(1)}, bf16[1,2,16,512]{3,2,1,0:T(8,128)(2,1)}, u32[]{:S(2)}) copy-start(bf16[1,2,16,512]{3,2,1,0:T(8,128)(2,1)} %param.14) | copy-start | bytes 98308
  179.7 69.3 %collective-permute-start.3 = (bf16[4,2,8,2,16,512]{5,4,3,2,1,0:T(8,128)(2,1)}, bf16[4,2,8,2,16,512]{5,4,3,2,1,0:T(8,128)(2,1)}, u32[]{:S(2)}, u32[]{:S(2)}) collective-permute-start(bf16[4,2,8,2,16,512]{5,4,3,2,1,0:T(8,128)(2,1)} %assemble.2.near), channel_id=1, source_target_pairs={{0,1},{1,0},{2,3},{3,2},{4,5},{5,4},{6,7},{7,6},{8,9},{9,8},{10,11... | collective-permute-start | bytes 6291464 | tf_op jit(solution)/shard_map/ppermute | solution.py:126
  246.3 6.5 %collective-permute-start.8 = (bf16[4,2,8,2,16,512]{5,4,3,2,1,0:T(8,128)(2,1)}, bf16[4,2,8,2,16,512]{5,4,3,2,1,0:T(8,128)(2,1)}, u32[]{:S(2)}, u32[]{:S(2)}) collective-permute-start(bf16[4,2,8,2,16,512]{5,4,3,2,1,0:T(8,128)(2,1)} %assemble.3.far), channel_id=1, source_target_pairs={{0,1},{1,0},{2,3},{3,2},{4,5},{5,4},{6,7},{7,6},{8,9},{9,8},{10,11... | collective-permute-start | bytes 6291464 | tf_op jit(solution)/shard_map/ppermute | solution.py:126
  260.9 4.2 %collective-permute-start.9 = (bf16[8,3,2,16,512]{4,3,2,1,0:T(8,128)(2,1)S(1)}, bf16[8,3,2,16,512]{4,3,2,1,0:T(8,128)(2,1)S(1)}, u32[]{:S(2)}, u32[]{:S(2)}) collective-permute-start(bf16[8,3,2,16,512]{4,3,2,1,0:T(8,128)(2,1)S(1)} %get-tuple-element.13), channel_id=1, source_target_pairs={{0,1},{1,0},{2,3},{3,2},{4,5},{5,4},{6,7},{7,6},{8,9},{9,8},{10,11... | collective-permute-start | bytes 2359304 | tf_op jit(solution)/shard_map/ppermute | solution.py:126

commit v7 on v6

--- a/solution.py
+++ b/solution.py
@@ -29,15 +29,17 @@
     rows = strip * slabs
     core, y = kept[blocks - 1], kept[blocks]
     sources = ((near, y, core), (near_other, y, 1 - core), (far, 1 - y, core), (far_other, 1 - y, 1 - core))
-    order = [(1, 0)] + [(0, b) for b in range(blocks)] + [(1, b) for b in range(1, blocks)]
+    many = blocks // 2
     copies = {}
-    for n, b in order:
-        copies[n, b] = [
-            pltpu.make_async_copy(source.at[:, n, b], panels.at[at_y, :, at_core, n, b], sems.at[n, b, k])
-            for k, (source, at_y, at_core) in enumerate(sources)
-        ]
-        for copy in copies[n, b]:
-            copy.start()
+    for n in range(2):
+        for part in range(2):
+            span = pl.ds(part * many, many)
+            copies[n, part] = [
+                pltpu.make_async_copy(source.at[:, n, span], panels.at[at_y, :, at_core, n, span], sems.at[n, part, k])
+                for k, (source, at_y, at_core) in enumerate(sources)
+            ]
+            for copy in copies[n, part]:
+                copy.start()
 
     def left(h, b):
         return upper[:, h, b].reshape(rows, half)
@@ -46,10 +48,10 @@
         return panels[:, :, :, n, b, h].reshape(half, width)
 
     def arrive(n, b):
-        for copy in copies[n, b]:
-            copy.wait()
-
-    arrive(1, 0)
+        if b % many == 0:
+            for copy in copies[n, b // many]:
+                copy.wait()
+
     total = jnp.zeros((rows, width), F32)
     for b in range(blocks):
         arrive(0, b)
@@ -70,6 +72,7 @@
     column_kept = dot(in_child, column).astype(BF16)
     column_out[...] = column_natural.reshape(column_out.shape)
 
+    arrive(1, 0)
     top = [right(1, 0, h) for h in range(pieces)]
     first = own_first[...].reshape(rows, width)
     second = own_second[...].reshape(rows, width)
@@ -127,15 +130,9 @@
 
 
 def assemble_kernel(place, *refs):
-    parts, out, sems = refs[:XS], refs[XS], refs[XS + 1]
-    copies = [
-        pltpu.make_async_copy(part, out.at[(place[0] - dx) & (XS - 1)], sems.at[dx])
-        for dx, part in enumerate(parts)
-    ]
-    for copy in copies:
-        copy.start()
-    for copy in copies:
-        copy.wait()
+    out = refs[XS]
+    for dx in range(XS):
+        out[(place[0] - dx) & (XS - 1)] = refs[dx][...]
 
 
 def shifted(shard):
@@ -151,15 +148,15 @@
 
 def gathered(rows):
     place = ((lax.axis_index("proc") >> 1) & (XS - 1))[None].astype(jnp.int32)
-    anywhere = pl.BlockSpec(memory_space=pl.ANY)
+    vmem = pl.BlockSpec(memory_space=pltpu.VMEM)
     both = []
     for row in rows:
         together = pl.pallas_call(
             assemble_kernel,
-            out_shape=pltpu.HBM((XS,) + row[0].shape, BF16),
-            in_specs=[pl.BlockSpec(memory_space=pltpu.SMEM)] + [anywhere] * XS,
-            out_specs=pl.BlockSpec(memory_space=pltpu.HBM),
-            scratch_shapes=[pltpu.SemaphoreType.DMA((XS,))],
+            out_shape=jax.ShapeDtypeStruct((XS,) + row[0].shape, BF16),
+            in_specs=[pl.BlockSpec(memory_space=pltpu.SMEM)] + [vmem] * XS,
+            out_specs=vmem,
+            compiler_params=pltpu.CompilerParams(vmem_limit_bytes=16 * 1024 * 1024),
             interpret=INTERPRET,
             name="assemble",
         )(place, *row)
@@ -225,7 +222,7 @@
         out_specs=(vmem, vmem, vmem, vmem),
         scratch_shapes=[
             pltpu.VMEM((YS, XS, CORES) + panels_shape[1:], BF16),
-            pltpu.SemaphoreType.DMA((2, blocks, 4)),
+            pltpu.SemaphoreType.DMA((2, 2, 4)),
         ],
         compiler_params=pltpu.CompilerParams(vmem_limit_bytes=32 * 1024 * 1024),
         interpret=INTERPRET,

time: 286 us -> 177 us (0.62)
  the two profiles are of different devices: /device:TPU:256 before, /device:TPU:248 now
where the time goes in v7:
time: 177 us; the launch traced here: 176 us
  waiting for transfers between devices  80.9 us (46%)
  starting transfers between devices  52.1 us (29%)
  blocking collectives  17.7 us (10%)
  Pallas kernels  14.8 us (8%)
  local copies, waits for them, and re-layouts  4.9 us (3%)
  matrix products  2.71 us (2%)
  other arithmetic  1.93 us (1%)
    ppermute x10, waiting for transfers between devices, moved(): return lax.ppermute(value, 'proc', pairs)  74.6 us
    ppermute x10, starting transfers between devices, moved(): return lax.ppermute(value, 'proc', pairs)  29.2 us
    all_to_all x1, blocking collectives, per_device(): lax.all_to_all(sums, 'proc', split_axis=0, concat_axis=0, tiled=True, axi...  17.7 us
    all_to_all x1, starting transfers between devices, per_device(): lax.all_to_all(spread.reshape(groups, tops, half), 'group', split_axis=0,...  12.9 us
    all_to_all x1, starting transfers between devices, per_device(): lax.all_to_all(outgoing.reshape(groups, blocks, slabs, half), 'group', sp...  10 us
    pallas_call x1, Pallas kernels, per_device(): pl.pallas_call(products_kernel, out_shape=(jax.ShapeDtypeStruct((blocks,...  7.26 us
    all_to_all x1, waiting for transfers between devices, per_device(): lax.all_to_all(spread.reshape(groups, tops, half), 'group', split_axis=0,...  6.23 us
    pallas_call x2, Pallas kernels, gathered(): pl.pallas_call(assemble_kernel, out_shape=jax.ShapeDtypeStruct((XS,) + ro...  5.67 us
  transfers between devices with their start and end apart: 12, of which 6 were waited for; matrix products, arithmetic and copies ran while one was open for 2% of the time, Pallas kernels for 3%

profile of v7, /device:TPU:248, one launch (start us, length us, event | category | flops | bytes accessed | tf_op | source)
XLA Modules:
  0.0 176.0 jit_solution(3294729148514902410)
XLA Ops:
  2.5 12.9 %all-to-all-start = ((bf16[32,16,256]{2,1,0:T(8,128)(2,1)}), bf16[32,16,256]{2,1,0:T(8,128)(2,1)S(1)}, u32[]{:S(2)}, u32[]{:S(2)}) async-start(bf16[32,16,256]{2,1,0:T(8,128)(2,1)} %bitcast.5), calls=%async_computation | async-start | bytes 524288 | tf_op jit(solution)/shard_map/all_to_all | solution.py:191
  17.9 6.2 %all-to-all-done = bf16[32,16,256]{2,1,0:T(8,128)(2,1)S(1)} async-done(((bf16[32,16,256]{2,1,0:T(8,128)(2,1)}), bf16[32,16,256]{2,1,0:T(8,128)(2,1)S(1)}, u32[]{:S(2)}, u32[]{:S(2)}) %all-to-all-start) | async-done | bytes 262176 | tf_op jit(solution)/shard_map/all_to_all | solution.py:191
  24.1 2.7 %fusion.1 = bf16[32,8,16,256]{3,2,1,0:T(8,128)(2,1)} fusion(bf16[512,256,1,1]{1,0,3,2:T(8,128)(2,1)S(1)} %bitcast.31, s32[32,8,16]{2,1,0:T(8,128)S(1)} %copy.19), kind=kOutput, calls=%fused_computation.2 | convolution fusion | flops 1075838976 | bytes 2375680 | tf_op jit(solution)/shard_map/dot_general | solution.py:199
  26.8 10.0 %all-to-all-start.1 = ((bf16[32,8,16,256]{3,2,1,0:T(8,128)(2,1)}), bf16[32,8,16,256]{3,2,1,0:T(8,128)(2,1)S(1)}, u32[]{:S(2)}, u32[]{:S(2)}) async-start(bf16[32,8,16,256]{3,2,1,0:T(8,128)(2,1)} %fusion.1), calls=%async_computation.1 | async-start | bytes 4194304 | tf_op jit(solution)/shard_map/all_to_all | solution.py:202
  37.0 3.6 %collective-permute-start.4 = (bf16[2,8,2,16,512]{4,3,2,1,0:T(8,128)(2,1)S(1)}, bf16[2,8,2,16,512]{4,3,2,1,0:T(8,128)(2,1)}, u32[]{:S(2)}, u32[]{:S(2)}) collective-permute-start(bf16[2,8,2,16,512]{4,3,2,1,0:T(8,128)(2,1)S(1)} %constant_dynamic-update-slice_fusion.refs_0_), channel_id=1, source_target_pairs={{0,8},{1,9},{2,10},{3,11},{4,12},{5,13},{6,14},{7,15},{8,0},{9,1},... | collective-permute-start | bytes 1572872 | tf_op jit(solution)/shard_map/ppermute | solution.py:129
  40.5 4.7 %collective-permute-start.2 = (bf16[2,8,2,16,512]{4,3,2,1,0:T(8,128)(2,1)S(1)}, bf16[2,8,2,16,512]{4,3,2,1,0:T(8,128)(2,1)S(1)}, u32[]{:S(2)}, u32[]{:S(2)}) collective-permute-start(bf16[2,8,2,16,512]{4,3,2,1,0:T(8,128)(2,1)S(1)} %constant_dynamic-update-slice_fusion.refs_0_), channel_id=1, source_target_pairs={{0,6},{1,7},{2,0},{3,1},{4,2},{5,3},{6,4},{7,5},{8,14},{9,15},{10,... | collective-permute-start | bytes 1572872 | tf_op jit(solution)/shard_map/ppermute | solution.py:129
  45.2 2.7 %collective-permute-start.1 = (bf16[2,8,2,16,512]{4,3,2,1,0:T(8,128)(2,1)S(1)}, bf16[2,8,2,16,512]{4,3,2,1,0:T(8,128)(2,1)}, u32[]{:S(2)}, u32[]{:S(2)}) collective-permute-start(bf16[2,8,2,16,512]{4,3,2,1,0:T(8,128)(2,1)S(1)} %constant_dynamic-update-slice_fusion.refs_0_), channel_id=1, source_target_pairs={{0,4},{1,5},{2,6},{3,7},{4,0},{5,1},{6,2},{7,3},{8,12},{9,13},{10,... | collective-permute-start | bytes 1572872 | tf_op jit(solution)/shard_map/ppermute | solution.py:129
  47.9 2.8 %collective-permute-start = (bf16[2,8,2,16,512]{4,3,2,1,0:T(8,128)(2,1)S(1)}, bf16[2,8,2,16,512]{4,3,2,1,0:T(8,128)(2,1)}, u32[]{:S(2)}, u32[]{:S(2)}) collective-permute-start(bf16[2,8,2,16,512]{4,3,2,1,0:T(8,128)(2,1)S(1)} %constant_dynamic-update-slice_fusion.refs_0_), channel_id=1, source_target_pairs={{0,2},{1,3},{2,4},{3,5},{4,6},{5,7},{6,0},{7,1},{8,10},{9,11},{10,... | collective-permute-start | bytes 1572872 | tf_op jit(solution)/shard_map/ppermute | solution.py:129
  50.7 51.8 %collective-permute-done.4.refs_0_ = bf16[2,8,2,16,512]{4,3,2,1,0:T(8,128)(2,1)} collective-permute-done((bf16[2,8,2,16,512]{4,3,2,1,0:T(8,128)(2,1)S(1)}, bf16[2,8,2,16,512]{4,3,2,1,0:T(8,128)(2,1)}, u32[]{:S(2)}, u32[]{:S(2)}) %collective-permute-start.4) | collective-permute-done | bytes 524320 | tf_op jit(solution)/shard_map/ppermute | solution.py:129
  102.5 4.8 %collective-permute-start.7 = (bf16[2,8,2,16,512]{4,3,2,1,0:T(8,128)(2,1)}, bf16[2,8,2,16,512]{4,3,2,1,0:T(8,128)(2,1)}, u32[]{:S(2)}, u32[]{:S(2)}) collective-permute-start(bf16[2,8,2,16,512]{4,3,2,1,0:T(8,128)(2,1)} %collective-permute-done.4.refs_0_), channel_id=1, source_target_pairs={{0,6},{1,7},{2,0},{3,1},{4,2},{5,3},{6,4},{7,5},{8,14},{9,15},{10,... | collective-permute-start | bytes 1572872 | tf_op jit(solution)/shard_map/ppermute | solution.py:129
  107.4 2.0 %collective-permute-start.6 = (bf16[2,8,2,16,512]{4,3,2,1,0:T(8,128)(2,1)}, bf16[2,8,2,16,512]{4,3,2,1,0:T(8,128)(2,1)}, u32[]{:S(2)}, u32[]{:S(2)}) collective-permute-start(bf16[2,8,2,16,512]{4,3,2,1,0:T(8,128)(2,1)} %collective-permute-done.4.refs_0_), channel_id=1, source_target_pairs={{0,4},{1,5},{2,6},{3,7},{4,0},{5,1},{6,2},{7,3},{8,12},{9,13},{10,... | collective-permute-start | bytes 1572872 | tf_op jit(solution)/shard_map/ppermute | solution.py:129
  110.2 2.7 %collective-permute-start.5 = (bf16[2,8,2,16,512]{4,3,2,1,0:T(8,128)(2,1)}, bf16[2,8,2,16,512]{4,3,2,1,0:T(8,128)(2,1)}, u32[]{:S(2)}, u32[]{:S(2)}) collective-permute-start(bf16[2,8,2,16,512]{4,3,2,1,0:T(8,128)(2,1)} %collective-permute-done.4.refs_0_), channel_id=1, source_target_pairs={{0,2},{1,3},{2,4},{3,5},{4,6},{5,7},{6,0},{7,1},{8,10},{9,11},{10,... | collective-permute-start | bytes 1572872 | tf_op jit(solution)/shard_map/ppermute | solution.py:129
  114.0 2.7 %assemble.2.near = bf16[4,2,8,2,16,512]{5,4,3,2,1,0:T(8,128)(2,1)} custom-call(s32[1]{0:T(128)} %bitcast.10.place, bf16[2,8,2,16,512]{4,3,2,1,0:T(8,128)(2,1)S(1)} %constant_dynamic-update-slice_fusion.refs_0_, bf16[2,8,2,16,512]{4,3,2,1,0:T(8,128)(2,1)} %collective-permute-done.refs_1_, bf16[2,8,2,16,512]{4,3,2,1,0:T(8,128)(2,1)} %collective-permute-done.1.refs_2_, ...), custom_call_target="tpu_custom_call" | custom-call | tf_op jit(solution)/shard_map/assemble/pallas_call | solution.py:154
  116.6 2.0 %collective-permute-start.3 = (bf16[4,2,8,2,16,512]{5,4,3,2,1,0:T(8,128)(2,1)}, bf16[4,2,8,2,16,512]{5,4,3,2,1,0:T(8,128)(2,1)}, u32[]{:S(2)}, u32[]{:S(2)}) collective-permute-start(bf16[4,2,8,2,16,512]{5,4,3,2,1,0:T(8,128)(2,1)} %assemble.2.near), channel_id=1, source_target_pairs={{0,1},{1,0},{2,3},{3,2},{4,5},{5,4},{6,7},{7,6},{8,9},{9,8},{10,11... | collective-permute-start | bytes 6291464 | tf_op jit(solution)/shard_map/ppermute | solution.py:129
  118.7 10.9 %collective-permute-done.7.refs_3_ = bf16[2,8,2,16,512]{4,3,2,1,0:T(8,128)(2,1)} collective-permute-done((bf16[2,8,2,16,512]{4,3,2,1,0:T(8,128)(2,1)}, bf16[2,8,2,16,512]{4,3,2,1,0:T(8,128)(2,1)}, u32[]{:S(2)}, u32[]{:S(2)}) %collective-permute-start.7) | collective-permute-done | bytes 524320 | tf_op jit(solution)/shard_map/ppermute | solution.py:129
  129.6 5.6 %collective-permute-done.5.refs_1_ = bf16[2,8,2,16,512]{4,3,2,1,0:T(8,128)(2,1)} collective-permute-done((bf16[2,8,2,16,512]{4,3,2,1,0:T(8,128)(2,1)}, bf16[2,8,2,16,512]{4,3,2,1,0:T(8,128)(2,1)}, u32[]{:S(2)}, u32[]{:S(2)}) %collective-permute-start.5) | collective-permute-done | bytes 524320 | tf_op jit(solution)/shard_map/ppermute | solution.py:129
  135.2 3.0 %assemble.3.far = bf16[4,2,8,2,16,512]{5,4,3,2,1,0:T(8,128)(2,1)} custom-call(s32[1]{0:T(128)} %bitcast.10.place, bf16[2,8,2,16,512]{4,3,2,1,0:T(8,128)(2,1)} %collective-permute-done.4.refs_0_, bf16[2,8,2,16,512]{4,3,2,1,0:T(8,128)(2,1)} %collective-permute-done.5.refs_1_, bf16[2,8,2,16,512]{4,3,2,1,0:T(8,128)(2,1)} %collective-permute-done.6.refs_2_, ...), custom_call_target="tpu_custom_call" | custom-call | tf_op jit(solution)/shard_map/assemble/pallas_call | solution.py:154
  138.2 1.9 %collective-permute-start.8 = (bf16[4,2,8,2,16,512]{5,4,3,2,1,0:T(8,128)(2,1)}, bf16[4,2,8,2,16,512]{5,4,3,2,1,0:T(8,128)(2,1)}, u32[]{:S(2)}, u32[]{:S(2)}) collective-permute-start(bf16[4,2,8,2,16,512]{5,4,3,2,1,0:T(8,128)(2,1)} %assemble.3.far), channel_id=1, source_target_pairs={{0,1},{1,0},{2,3},{3,2},{4,5},{5,4},{6,7},{7,6},{8,9},{9,8},{10,11... | collective-permute-start | bytes 6291464 | tf_op jit(solution)/shard_map/ppermute | solution.py:129
  140.4 4.2 %collective-permute-done.8.far_other = bf16[4,2,8,2,16,512]{5,4,3,2,1,0:T(8,128)(2,1)} collective-permute-done((bf16[4,2,8,2,16,512]{5,4,3,2,1,0:T(8,128)(2,1)}, bf16[4,2,8,2,16,512]{5,4,3,2,1,0:T(8,128)(2,1)}, u32[]{:S(2)}, u32[]{:S(2)}) %collective-permute-start.8) | collective-permute-done | bytes 2097184 | tf_op jit(solution)/shard_map/ppermute | solution.py:129
  144.6 7.3 %products.1 = (bf16[8,2,16,512]{3,2,1,0:T(8,128)(2,1)}, bf16[8,2,16,512]{3,2,1,0:T(8,128)(2,1)}, bf16[8,3,2,16,512]{4,3,2,1,0:T(8,128)(2,1)S(1)}, bf16[8,3,2,16,512]{4,3,2,1,0:T(8,128)(2,1)S(1)}) custom-call(s32[9]{0:T(128)S(1)} %pad_add_fusion.kept, bf16[16,2,8,16,256]{4,3,2,1,0:T(8,128)(2,1)S(1)} %bitcast.24, ...), custom_call_target="tpu_custom_call" | custom-call | tf_op jit(solution)/shard_map/products/pallas_call | solution.py:213
  151.8 2.0 %collective-permute-start.9 = (bf16[8,3,2,16,512]{4,3,2,1,0:T(8,128)(2,1)S(1)}, bf16[8,3,2,16,512]{4,3,2,1,0:T(8,128)(2,1)S(1)}, u32[]{:S(2)}, u32[]{:S(2)}) collective-permute-start(bf16[8,3,2,16,512]{4,3,2,1,0:T(8,128)(2,1)S(1)} %get-tuple-element.13), channel_id=1, source_target_pairs={{0,1},{1,0},{2,3},{3,2},{4,5},{5,4},{6,7},{7,6},{8,9},{9,8},{10,11... | collective-permute-start | bytes 2359304 | tf_op jit(solution)/shard_map/ppermute | solution.py:129
  153.9 2.1 %collective-permute-done.9 = bf16[8,3,2,16,512]{4,3,2,1,0:T(8,128)(2,1)S(1)} collective-permute-done((bf16[8,3,2,16,512]{4,3,2,1,0:T(8,128)(2,1)S(1)}, bf16[8,3,2,16,512]{4,3,2,1,0:T(8,128)(2,1)S(1)}, u32[]{:S(2)}, u32[]{:S(2)}) %collective-permute-start.9) | collective-permute-done | bytes 786464 | tf_op jit(solution)/shard_map/ppermute | solution.py:129
  156.4 17.7 %all_to_all.15.arrived = bf16[8,3,2,16,512]{4,3,2,1,0:T(8,128)(2,1)} all-to-all(bf16[8,3,2,16,512]{4,3,2,1,0:T(8,128)(2,1)S(1)} %add_convert_fusion), channel_id=1, replica_groups={{0,2,4,6,8,10,12,14},{1,3,5,7,9,11,13,15},{16,18,20,22,24,26,28,30},{17..., dimensions={0} | all-to-all | bytes 1572864 | tf_op jit(solution)/shard_map/all_to_all | solution.py:233
  174.1 1.9 %final.1 = (bf16[2,16,512]{2,1,0:T(8,128)(2,1)}, bf16[8,2,16,512]{3,2,1,0:T(8,128)(2,1)}, bf16[2,16,512]{2,1,0:T(8,128)(2,1)}) custom-call(bf16[8,3,2,16,512]{4,3,2,1,0:T(8,128)(2,1)} %all_to_all.15.arrived, bf16[2,16,512]{2,1,0:T(8,128)(2,1)} %bitcast.27, bf16[2,16,512]{2,1,0:T(8,128)(2,1)} %bitcast.32, ...), custom_call_target="tpu_custom_call", output_to_operand_aliasing={{1}: (3, {})} | custom-call | tf_op jit(solution)/shard_map/final/pallas_call | solution.py:237
  (32 shorter events, 6.8 us)
Async XLA Ops:
  0.6 139.5 %copy-start = (s32[32,7]{0,1:T(8,128)S(1)}, s32[32,7]{0,1:T(8,128)}, u32[]{:S(2)}) copy-start(s32[32,7]{0,1:T(8,128)} %param.11) | copy-start | bytes 2692
  2.5 21.6 %all-to-all-start = ((bf16[32,16,256]{2,1,0:T(8,128)(2,1)}), bf16[32,16,256]{2,1,0:T(8,128)(2,1)S(1)}, u32[]{:S(2)}, u32[]{:S(2)}) async-start(bf16[32,16,256]{2,1,0:T(8,128)(2,1)} %bitcast.5), calls=%async_computation | async-start | bytes 524288 | tf_op jit(solution)/shard_map/all_to_all | solution.py:191
  26.8 10.0 %copy-start.1 = (bf16[1,8,2,16,512]{4,3,2,1,0:T(8,128)(2,1)S(1)}, bf16[1,8,2,16,512]{4,3,2,1,0:T(8,128)(2,1)}, u32[]{:S(2)}) copy-start(bf16[1,8,2,16,512]{4,3,2,1,0:T(8,128)(2,1)} %param.12) | copy-start | bytes 786436
  26.8 10.1 %copy-start.2 = (bf16[1,8,2,16,512]{4,3,2,1,0:T(8,128)(2,1)S(1)}, bf16[1,8,2,16,512]{4,3,2,1,0:T(8,128)(2,1)}, u32[]{:S(2)}) copy-start(bf16[1,8,2,16,512]{4,3,2,1,0:T(8,128)(2,1)} %param.13) | copy-start | bytes 786436
  26.8 117.7 %all-to-all-start.1 = ((bf16[32,8,16,256]{3,2,1,0:T(8,128)(2,1)}), bf16[32,8,16,256]{3,2,1,0:T(8,128)(2,1)S(1)}, u32[]{:S(2)}, u32[]{:S(2)}) async-start(bf16[32,8,16,256]{3,2,1,0:T(8,128)(2,1)} %fusion.1), calls=%async_computation.1 | async-start | bytes 4194304 | tf_op jit(solution)/shard_map/all_to_all | solution.py:202
  37.0 65.6 %collective-permute-start.4 = (bf16[2,8,2,16,512]{4,3,2,1,0:T(8,128)(2,1)S(1)}, bf16[2,8,2,16,512]{4,3,2,1,0:T(8,128)(2,1)}, u32[]{:S(2)}, u32[]{:S(2)}) collective-permute-start(bf16[2,8,2,16,512]{4,3,2,1,0:T(8,128)(2,1)S(1)} %constant_dynamic-update-slice_fusion.refs_0_), channel_id=1, source_target_pairs={{0,8},{1,9},{2,10},{3,11},{4,12},{5,13},{6,14},{7,15},{8,0},{9,1},... | collective-permute-start | bytes 1572872 | tf_op jit(solution)/shard_map/ppermute | solution.py:129
  40.5 68.8 %collective-permute-start.2 = (bf16[2,8,2,16,512]{4,3,2,1,0:T(8,128)(2,1)S(1)}, bf16[2,8,2,16,512]{4,3,2,1,0:T(8,128)(2,1)S(1)}, u32[]{:S(2)}, u32[]{:S(2)}) collective-permute-start(bf16[2,8,2,16,512]{4,3,2,1,0:T(8,128)(2,1)S(1)} %constant_dynamic-update-slice_fusion.refs_0_), channel_id=1, source_target_pairs={{0,6},{1,7},{2,0},{3,1},{4,2},{5,3},{6,4},{7,5},{8,14},{9,15},{10,... | collective-permute-start | bytes 1572872 | tf_op jit(solution)/shard_map/ppermute | solution.py:129
  45.2 67.7 %collective-permute-start.1 = (bf16[2,8,2,16,512]{4,3,2,1,0:T(8,128)(2,1)S(1)}, bf16[2,8,2,16,512]{4,3,2,1,0:T(8,128)(2,1)}, u32[]{:S(2)}, u32[]{:S(2)}) collective-permute-start(bf16[2,8,2,16,512]{4,3,2,1,0:T(8,128)(2,1)S(1)} %constant_dynamic-update-slice_fusion.refs_0_), channel_id=1, source_target_pairs={{0,4},{1,5},{2,6},{3,7},{4,0},{5,1},{6,2},{7,3},{8,12},{9,13},{10,... | collective-permute-start | bytes 1572872 | tf_op jit(solution)/shard_map/ppermute | solution.py:129
  47.9 65.0 %collective-permute-start = (bf16[2,8,2,16,512]{4,3,2,1,0:T(8,128)(2,1)S(1)}, bf16[2,8,2,16,512]{4,3,2,1,0:T(8,128)(2,1)}, u32[]{:S(2)}, u32[]{:S(2)}) collective-permute-start(bf16[2,8,2,16,512]{4,3,2,1,0:T(8,128)(2,1)S(1)} %constant_dynamic-update-slice_fusion.refs_0_), channel_id=1, source_target_pairs={{0,2},{1,3},{2,4},{3,5},{4,6},{5,7},{6,0},{7,1},{8,10},{9,11},{10,... | collective-permute-start | bytes 1572872 | tf_op jit(solution)/shard_map/ppermute | solution.py:129
  102.5 27.0 %collective-permute-start.7 = (bf16[2,8,2,16,512]{4,3,2,1,0:T(8,128)(2,1)}, bf16[2,8,2,16,512]{4,3,2,1,0:T(8,128)(2,1)}, u32[]{:S(2)}, u32[]{:S(2)}) collective-permute-start(bf16[2,8,2,16,512]{4,3,2,1,0:T(8,128)(2,1)} %collective-permute-done.4.refs_0_), channel_id=1, source_target_pairs={{0,6},{1,7},{2,0},{3,1},{4,2},{5,3},{6,4},{7,5},{8,14},{9,15},{10,... | collective-permute-start | bytes 1572872 | tf_op jit(solution)/shard_map/ppermute | solution.py:129
  107.4 22.2 %collective-permute-start.6 = (bf16[2,8,2,16,512]{4,3,2,1,0:T(8,128)(2,1)}, bf16[2,8,2,16,512]{4,3,2,1,0:T(8,128)(2,1)}, u32[]{:S(2)}, u32[]{:S(2)}) collective-permute-start(bf16[2,8,2,16,512]{4,3,2,1,0:T(8,128)(2,1)} %collective-permute-done.4.refs_0_), channel_id=1, source_target_pairs={{0,4},{1,5},{2,6},{3,7},{4,0},{5,1},{6,2},{7,3},{8,12},{9,13},{10,... | collective-permute-start | bytes 1572872 | tf_op jit(solution)/shard_map/ppermute | solution.py:129
  109.4 0.8 copy-start.3
  110.2 25.0 %collective-permute-start.5 = (bf16[2,8,2,16,512]{4,3,2,1,0:T(8,128)(2,1)}, bf16[2,8,2,16,512]{4,3,2,1,0:T(8,128)(2,1)}, u32[]{:S(2)}, u32[]{:S(2)}) collective-permute-start(bf16[2,8,2,16,512]{4,3,2,1,0:T(8,128)(2,1)} %collective-permute-done.4.refs_0_), channel_id=1, source_target_pairs={{0,2},{1,3},{2,4},{3,5},{4,6},{5,7},{6,0},{7,1},{8,10},{9,11},{10,... | collective-permute-start | bytes 1572872 | tf_op jit(solution)/shard_map/ppermute | solution.py:129
  112.9 1.0 copy-start.4
  116.6 28.0 %copy-start.5 = (bf16[1,2,16,512]{3,2,1,0:T(8,128)(2,1)S(1)}, bf16[1,2,16,512]{3,2,1,0:T(8,128)(2,1)}, u32[]{:S(2)}) copy-start(bf16[1,2,16,512]{3,2,1,0:T(8,128)(2,1)} %param.14) | copy-start | bytes 98308
  116.6 23.8 %collective-permute-start.3 = (bf16[4,2,8,2,16,512]{5,4,3,2,1,0:T(8,128)(2,1)}, bf16[4,2,8,2,16,512]{5,4,3,2,1,0:T(8,128)(2,1)}, u32[]{:S(2)}, u32[]{:S(2)}) collective-permute-start(bf16[4,2,8,2,16,512]{5,4,3,2,1,0:T(8,128)(2,1)} %assemble.2.near), channel_id=1, source_target_pairs={{0,1},{1,0},{2,3},{3,2},{4,5},{5,4},{6,7},{7,6},{8,9},{9,8},{10,11... | collective-permute-start | bytes 6291464 | tf_op jit(solution)/shard_map/ppermute | solution.py:129
  138.2 6.4 %collective-permute-start.8 = (bf16[4,2,8,2,16,512]{5,4,3,2,1,0:T(8,128)(2,1)}, bf16[4,2,8,2,16,512]{5,4,3,2,1,0:T(8,128)(2,1)}, u32[]{:S(2)}, u32[]{:S(2)}) collective-permute-start(bf16[4,2,8,2,16,512]{5,4,3,2,1,0:T(8,128)(2,1)} %assemble.3.far), channel_id=1, source_target_pairs={{0,1},{1,0},{2,3},{3,2},{4,5},{5,4},{6,7},{7,6},{8,9},{9,8},{10,11... | collective-permute-start | bytes 6291464 | tf_op jit(solution)/shard_map/ppermute | solution.py:129
  151.8 4.2 %collective-permute-start.9 = (bf16[8,3,2,16,512]{4,3,2,1,0:T(8,128)(2,1)S(1)}, bf16[8,3,2,16,512]{4,3,2,1,0:T(8,128)(2,1)S(1)}, u32[]{:S(2)}, u32[]{:S(2)}) collective-permute-start(bf16[8,3,2,16,512]{4,3,2,1,0:T(8,128)(2,1)S(1)} %get-tuple-element.13), channel_id=1, source_target_pairs={{0,1},{1,0},{2,3},{3,2},{4,5},{5,4},{6,7},{7,6},{8,9},{9,8},{10,11... | collective-permute-start | bytes 2359304 | tf_op jit(solution)/shard_map/ppermute | solution.py:129

commit v8 on v7

--- a/solution.py
+++ b/solution.py
@@ -137,13 +137,13 @@
 
 def shifted(shard):
     other = moved(shard, (1, 0, 0))
-    rows = []
-    for part in (shard, other):
-        row = [part]
-        for dx in range(1, XS):
-            row.append(moved(part, (0, dx, 0)))
-        rows.append(row)
-    return rows
+    back = moved(shard, (0, XS - 1, 0))
+    other_on = moved(other, (0, 1, 0))
+    back_twice = moved(back, (0, XS - 1, 0))
+    on = moved(shard, (0, 1, 0))
+    other_back = moved(other, (0, XS - 1, 0))
+    other_on_twice = moved(other_on, (0, 1, 0))
+    return (shard, on, back_twice, back), (other, other_on, other_on_twice, other_back)
 
 
 def gathered(rows):

time: 177 us -> 184 us (1.040)
  the two profiles are of different devices: /device:TPU:248 before, /device:TPU:256 now
where the time goes in v8:
time: 184 us; the launch traced here: 183 us
  waiting for transfers between devices  92.2 us (50%)
  starting transfers between devices  49 us (27%)
  blocking collectives  18.5 us (10%)
  Pallas kernels  14.9 us (8%)
  local copies, waits for them, and re-layouts  3.06 us (2%)
  matrix products  2.69 us (1%)
  other arithmetic  1.93 us (1%)
    ppermute x10, waiting for transfers between devices, moved(): return lax.ppermute(value, 'proc', pairs)  84.2 us
    ppermute x10, starting transfers between devices, moved(): return lax.ppermute(value, 'proc', pairs)  27.7 us
    all_to_all x1, blocking collectives, per_device(): lax.all_to_all(sums, 'proc', split_axis=0, concat_axis=0, tiled=True, axi...  18.5 us
    all_to_all x1, starting transfers between devices, per_device(): lax.all_to_all(spread.reshape(groups, tops, half), 'group', split_axis=0,...  12.7 us
    all_to_all x1, starting transfers between devices, per_device(): lax.all_to_all(outgoing.reshape(groups, blocks, slabs, half), 'group', sp...  8.59 us
    all_to_all x1, waiting for transfers between devices, per_device(): lax.all_to_all(spread.reshape(groups, tops, half), 'group', split_axis=0,...  7.97 us
    pallas_call x1, Pallas kernels, per_device(): pl.pallas_call(products_kernel, out_shape=(jax.ShapeDtypeStruct((blocks,...  7.26 us
    pallas_call x2, Pallas kernels, gathered(): pl.pallas_call(assemble_kernel, out_shape=jax.ShapeDtypeStruct((XS,) + ro...  5.81 us
  transfers between devices with their start and end apart: 12, of which 7 were waited for; matrix products, arithmetic and copies ran while one was open for 1% of the time, Pallas kernels for 3%

profile of v8, /device:TPU:256, one launch (start us, length us, event | category | flops | bytes accessed | tf_op | source)
XLA Modules:
  0.0 183.2 jit_solution(782262354090775023)
XLA Ops:
  2.5 12.7 %all-to-all-start = ((bf16[32,16,256]{2,1,0:T(8,128)(2,1)}), bf16[32,16,256]{2,1,0:T(8,128)(2,1)S(1)}, u32[]{:S(2)}, u32[]{:S(2)}) async-start(bf16[32,16,256]{2,1,0:T(8,128)(2,1)} %bitcast.5), calls=%async_computation | async-start | bytes 524288 | tf_op jit(solution)/shard_map/all_to_all | solution.py:191
  17.7 8.0 %all-to-all-done = bf16[32,16,256]{2,1,0:T(8,128)(2,1)S(1)} async-done(((bf16[32,16,256]{2,1,0:T(8,128)(2,1)}), bf16[32,16,256]{2,1,0:T(8,128)(2,1)S(1)}, u32[]{:S(2)}, u32[]{:S(2)}) %all-to-all-start) | async-done | bytes 262176 | tf_op jit(solution)/shard_map/all_to_all | solution.py:191
  25.6 2.7 %fusion.1 = bf16[32,8,16,256]{3,2,1,0:T(8,128)(2,1)} fusion(bf16[512,256,1,1]{1,0,3,2:T(8,128)(2,1)S(1)} %bitcast.31, s32[32,8,16]{2,1,0:T(8,128)S(1)} %copy.19), kind=kOutput, calls=%fused_computation.2 | convolution fusion | flops 1075838976 | bytes 2375680 | tf_op jit(solution)/shard_map/dot_general | solution.py:199
  28.3 8.6 %all-to-all-start.1 = ((bf16[32,8,16,256]{3,2,1,0:T(8,128)(2,1)}), bf16[32,8,16,256]{3,2,1,0:T(8,128)(2,1)S(1)}, u32[]{:S(2)}, u32[]{:S(2)}) async-start(bf16[32,8,16,256]{3,2,1,0:T(8,128)(2,1)} %fusion.1), calls=%async_computation.1 | async-start | bytes 4194304 | tf_op jit(solution)/shard_map/all_to_all | solution.py:202
  37.0 2.3 %collective-permute-start.4 = (bf16[2,8,2,16,512]{4,3,2,1,0:T(8,128)(2,1)S(1)}, bf16[2,8,2,16,512]{4,3,2,1,0:T(8,128)(2,1)}, u32[]{:S(2)}, u32[]{:S(2)}) collective-permute-start(bf16[2,8,2,16,512]{4,3,2,1,0:T(8,128)(2,1)S(1)} %constant_dynamic-update-slice_fusion.refs_0_), channel_id=1, source_target_pairs={{0,8},{1,9},{2,10},{3,11},{4,12},{5,13},{6,14},{7,15},{8,0},{9,1},... | collective-permute-start | bytes 1572872 | tf_op jit(solution)/shard_map/ppermute | solution.py:129
  39.3 4.7 %collective-permute-start.1 = (bf16[2,8,2,16,512]{4,3,2,1,0:T(8,128)(2,1)S(1)}, bf16[2,8,2,16,512]{4,3,2,1,0:T(8,128)(2,1)}, u32[]{:S(2)}, u32[]{:S(2)}) collective-permute-start(bf16[2,8,2,16,512]{4,3,2,1,0:T(8,128)(2,1)S(1)} %constant_dynamic-update-slice_fusion.refs_0_), channel_id=1, source_target_pairs={{0,6},{1,7},{2,0},{3,1},{4,2},{5,3},{6,4},{7,5},{8,14},{9,15},{10,... | collective-permute-start | bytes 1572872 | tf_op jit(solution)/shard_map/ppermute | solution.py:129
  44.0 59.6 %collective-permute-done.4.refs_0_ = bf16[2,8,2,16,512]{4,3,2,1,0:T(8,128)(2,1)} collective-permute-done((bf16[2,8,2,16,512]{4,3,2,1,0:T(8,128)(2,1)S(1)}, bf16[2,8,2,16,512]{4,3,2,1,0:T(8,128)(2,1)}, u32[]{:S(2)}, u32[]{:S(2)}) %collective-permute-start.4) | collective-permute-done | bytes 524320 | tf_op jit(solution)/shard_map/ppermute | solution.py:129
  103.5 1.9 %collective-permute-start.5 = (bf16[2,8,2,16,512]{4,3,2,1,0:T(8,128)(2,1)}, bf16[2,8,2,16,512]{4,3,2,1,0:T(8,128)(2,1)}, u32[]{:S(2)}, u32[]{:S(2)}) collective-permute-start(bf16[2,8,2,16,512]{4,3,2,1,0:T(8,128)(2,1)} %collective-permute-done.4.refs_0_), channel_id=1, source_target_pairs={{0,2},{1,3},{2,4},{3,5},{4,6},{5,7},{6,0},{7,1},{8,10},{9,11},{10,... | collective-permute-start | bytes 1572872 | tf_op jit(solution)/shard_map/ppermute | solution.py:129
  105.5 5.3 %collective-permute-start = (bf16[2,8,2,16,512]{4,3,2,1,0:T(8,128)(2,1)S(1)}, bf16[2,8,2,16,512]{4,3,2,1,0:T(8,128)(2,1)}, u32[]{:S(2)}, u32[]{:S(2)}) collective-permute-start(bf16[2,8,2,16,512]{4,3,2,1,0:T(8,128)(2,1)S(1)} %constant_dynamic-update-slice_fusion.refs_0_), channel_id=1, source_target_pairs={{0,2},{1,3},{2,4},{3,5},{4,6},{5,7},{6,0},{7,1},{8,10},{9,11},{10,... | collective-permute-start | bytes 1572872 | tf_op jit(solution)/shard_map/ppermute | solution.py:129
  110.7 1.9 %collective-permute-start.2 = (bf16[2,8,2,16,512]{4,3,2,1,0:T(8,128)(2,1)}, bf16[2,8,2,16,512]{4,3,2,1,0:T(8,128)(2,1)}, u32[]{:S(2)}, u32[]{:S(2)}) collective-permute-start(bf16[2,8,2,16,512]{4,3,2,1,0:T(8,128)(2,1)} %collective-permute-done.1.refs_3_), channel_id=1, source_target_pairs={{0,6},{1,7},{2,0},{3,1},{4,2},{5,3},{6,4},{7,5},{8,14},{9,15},{10,... | collective-permute-start | bytes 1572872 | tf_op jit(solution)/shard_map/ppermute | solution.py:129
  112.7 3.8 %collective-permute-start.7 = (bf16[2,8,2,16,512]{4,3,2,1,0:T(8,128)(2,1)}, bf16[2,8,2,16,512]{4,3,2,1,0:T(8,128)(2,1)}, u32[]{:S(2)}, u32[]{:S(2)}) collective-permute-start(bf16[2,8,2,16,512]{4,3,2,1,0:T(8,128)(2,1)} %collective-permute-done.4.refs_0_), channel_id=1, source_target_pairs={{0,6},{1,7},{2,0},{3,1},{4,2},{5,3},{6,4},{7,5},{8,14},{9,15},{10,... | collective-permute-start | bytes 1572872 | tf_op jit(solution)/shard_map/ppermute | solution.py:129
  116.5 5.3 %collective-permute-done.5.refs_1_ = bf16[2,8,2,16,512]{4,3,2,1,0:T(8,128)(2,1)} collective-permute-done((bf16[2,8,2,16,512]{4,3,2,1,0:T(8,128)(2,1)}, bf16[2,8,2,16,512]{4,3,2,1,0:T(8,128)(2,1)}, u32[]{:S(2)}, u32[]{:S(2)}) %collective-permute-start.5) | collective-permute-done | bytes 524320 | tf_op jit(solution)/shard_map/ppermute | solution.py:129
  121.7 1.9 %collective-permute-start.6 = (bf16[2,8,2,16,512]{4,3,2,1,0:T(8,128)(2,1)}, bf16[2,8,2,16,512]{4,3,2,1,0:T(8,128)(2,1)}, u32[]{:S(2)}, u32[]{:S(2)}) collective-permute-start(bf16[2,8,2,16,512]{4,3,2,1,0:T(8,128)(2,1)} %collective-permute-done.5.refs_1_), channel_id=1, source_target_pairs={{0,2},{1,3},{2,4},{3,5},{4,6},{5,7},{6,0},{7,1},{8,10},{9,11},{10,... | collective-permute-start | bytes 1572872 | tf_op jit(solution)/shard_map/ppermute | solution.py:129
  123.7 9.3 %collective-permute-done.refs_1_ = bf16[2,8,2,16,512]{4,3,2,1,0:T(8,128)(2,1)} collective-permute-done((bf16[2,8,2,16,512]{4,3,2,1,0:T(8,128)(2,1)S(1)}, bf16[2,8,2,16,512]{4,3,2,1,0:T(8,128)(2,1)}, u32[]{:S(2)}, u32[]{:S(2)}) %collective-permute-start) | collective-permute-done | bytes 524320 | tf_op jit(solution)/shard_map/ppermute | solution.py:129
  133.0 2.8 %assemble.2.near = bf16[4,2,8,2,16,512]{5,4,3,2,1,0:T(8,128)(2,1)} custom-call(s32[1]{0:T(128)} %bitcast.10.place, bf16[2,8,2,16,512]{4,3,2,1,0:T(8,128)(2,1)S(1)} %constant_dynamic-update-slice_fusion.refs_0_, bf16[2,8,2,16,512]{4,3,2,1,0:T(8,128)(2,1)} %collective-permute-done.refs_1_, bf16[2,8,2,16,512]{4,3,2,1,0:T(8,128)(2,1)} %collective-permute-done.2.refs_2_, ...), custom_call_target="tpu_custom_call" | custom-call | tf_op jit(solution)/shard_map/assemble/pallas_call | solution.py:154
  135.8 2.0 %collective-permute-start.3 = (bf16[4,2,8,2,16,512]{5,4,3,2,1,0:T(8,128)(2,1)}, bf16[4,2,8,2,16,512]{5,4,3,2,1,0:T(8,128)(2,1)}, u32[]{:S(2)}, u32[]{:S(2)}) collective-permute-start(bf16[4,2,8,2,16,512]{5,4,3,2,1,0:T(8,128)(2,1)} %assemble.2.near), channel_id=1, source_target_pairs={{0,1},{1,0},{2,3},{3,2},{4,5},{5,4},{6,7},{7,6},{8,9},{9,8},{10,11... | collective-permute-start | bytes 6291464 | tf_op jit(solution)/shard_map/ppermute | solution.py:129
  137.9 3.8 %collective-permute-done.6.refs_2_ = bf16[2,8,2,16,512]{4,3,2,1,0:T(8,128)(2,1)} collective-permute-done((bf16[2,8,2,16,512]{4,3,2,1,0:T(8,128)(2,1)}, bf16[2,8,2,16,512]{4,3,2,1,0:T(8,128)(2,1)}, u32[]{:S(2)}, u32[]{:S(2)}) %collective-permute-start.6) | collective-permute-done | bytes 524320 | tf_op jit(solution)/shard_map/ppermute | solution.py:129
  141.6 3.0 %assemble.3.far = bf16[4,2,8,2,16,512]{5,4,3,2,1,0:T(8,128)(2,1)} custom-call(s32[1]{0:T(128)} %bitcast.10.place, bf16[2,8,2,16,512]{4,3,2,1,0:T(8,128)(2,1)} %collective-permute-done.4.refs_0_, bf16[2,8,2,16,512]{4,3,2,1,0:T(8,128)(2,1)} %collective-permute-done.5.refs_1_, bf16[2,8,2,16,512]{4,3,2,1,0:T(8,128)(2,1)} %collective-permute-done.6.refs_2_, ...), custom_call_target="tpu_custom_call" | custom-call | tf_op jit(solution)/shard_map/assemble/pallas_call | solution.py:154
  144.6 1.9 %collective-permute-start.8 = (bf16[4,2,8,2,16,512]{5,4,3,2,1,0:T(8,128)(2,1)}, bf16[4,2,8,2,16,512]{5,4,3,2,1,0:T(8,128)(2,1)}, u32[]{:S(2)}, u32[]{:S(2)}) collective-permute-start(bf16[4,2,8,2,16,512]{5,4,3,2,1,0:T(8,128)(2,1)} %assemble.3.far), channel_id=1, source_target_pairs={{0,1},{1,0},{2,3},{3,2},{4,5},{5,4},{6,7},{7,6},{8,9},{9,8},{10,11... | collective-permute-start | bytes 6291464 | tf_op jit(solution)/shard_map/ppermute | solution.py:129
  146.8 4.2 %collective-permute-done.8.far_other = bf16[4,2,8,2,16,512]{5,4,3,2,1,0:T(8,128)(2,1)} collective-permute-done((bf16[4,2,8,2,16,512]{5,4,3,2,1,0:T(8,128)(2,1)}, bf16[4,2,8,2,16,512]{5,4,3,2,1,0:T(8,128)(2,1)}, u32[]{:S(2)}, u32[]{:S(2)}) %collective-permute-start.8) | collective-permute-done | bytes 2097184 | tf_op jit(solution)/shard_map/ppermute | solution.py:129
  151.0 7.3 %products.1 = (bf16[8,2,16,512]{3,2,1,0:T(8,128)(2,1)}, bf16[8,2,16,512]{3,2,1,0:T(8,128)(2,1)}, bf16[8,3,2,16,512]{4,3,2,1,0:T(8,128)(2,1)S(1)}, bf16[8,3,2,16,512]{4,3,2,1,0:T(8,128)(2,1)S(1)}) custom-call(s32[9]{0:T(128)S(1)} %pad_add_fusion.kept, bf16[16,2,8,16,256]{4,3,2,1,0:T(8,128)(2,1)S(1)} %bitcast.24, ...), custom_call_target="tpu_custom_call" | custom-call | tf_op jit(solution)/shard_map/products/pallas_call | solution.py:213
  158.3 2.0 %collective-permute-start.9 = (bf16[8,3,2,16,512]{4,3,2,1,0:T(8,128)(2,1)S(1)}, bf16[8,3,2,16,512]{4,3,2,1,0:T(8,128)(2,1)S(1)}, u32[]{:S(2)}, u32[]{:S(2)}) collective-permute-start(bf16[8,3,2,16,512]{4,3,2,1,0:T(8,128)(2,1)S(1)} %get-tuple-element.13), channel_id=1, source_target_pairs={{0,1},{1,0},{2,3},{3,2},{4,5},{5,4},{6,7},{7,6},{8,9},{9,8},{10,11... | collective-permute-start | bytes 2359304 | tf_op jit(solution)/shard_map/ppermute | solution.py:129
  160.3 2.1 %collective-permute-done.9 = bf16[8,3,2,16,512]{4,3,2,1,0:T(8,128)(2,1)S(1)} collective-permute-done((bf16[8,3,2,16,512]{4,3,2,1,0:T(8,128)(2,1)S(1)}, bf16[8,3,2,16,512]{4,3,2,1,0:T(8,128)(2,1)S(1)}, u32[]{:S(2)}, u32[]{:S(2)}) %collective-permute-start.9) | collective-permute-done | bytes 786464 | tf_op jit(solution)/shard_map/ppermute | solution.py:129
  162.8 18.5 %all_to_all.15.arrived = bf16[8,3,2,16,512]{4,3,2,1,0:T(8,128)(2,1)} all-to-all(bf16[8,3,2,16,512]{4,3,2,1,0:T(8,128)(2,1)S(1)} %add_convert_fusion), channel_id=1, replica_groups={{0,2,4,6,8,10,12,14},{1,3,5,7,9,11,13,15},{16,18,20,22,24,26,28,30},{17..., dimensions={0} | all-to-all | bytes 1572864 | tf_op jit(solution)/shard_map/all_to_all | solution.py:233
  (28 shorter events, 6.9 us)
Async XLA Ops:
  0.6 145.9 %copy-start = (s32[32,7]{0,1:T(8,128)S(1)}, s32[32,7]{0,1:T(8,128)}, u32[]{:S(2)}) copy-start(s32[32,7]{0,1:T(8,128)} %param.11) | copy-start | bytes 2692
  2.5 23.1 %all-to-all-start = ((bf16[32,16,256]{2,1,0:T(8,128)(2,1)}), bf16[32,16,256]{2,1,0:T(8,128)(2,1)S(1)}, u32[]{:S(2)}, u32[]{:S(2)}) async-start(bf16[32,16,256]{2,1,0:T(8,128)(2,1)} %bitcast.5), calls=%async_computation | async-start | bytes 524288 | tf_op jit(solution)/shard_map/all_to_all | solution.py:191
  28.3 8.6 %copy-start.1 = (bf16[1,8,2,16,512]{4,3,2,1,0:T(8,128)(2,1)S(1)}, bf16[1,8,2,16,512]{4,3,2,1,0:T(8,128)(2,1)}, u32[]{:S(2)}) copy-start(bf16[1,8,2,16,512]{4,3,2,1,0:T(8,128)(2,1)} %param.12) | copy-start | bytes 786436
  28.3 8.6 %copy-start.2 = (bf16[1,8,2,16,512]{4,3,2,1,0:T(8,128)(2,1)S(1)}, bf16[1,8,2,16,512]{4,3,2,1,0:T(8,128)(2,1)}, u32[]{:S(2)}) copy-start(bf16[1,8,2,16,512]{4,3,2,1,0:T(8,128)(2,1)} %param.13) | copy-start | bytes 786436
  28.3 122.7 %all-to-all-start.1 = ((bf16[32,8,16,256]{3,2,1,0:T(8,128)(2,1)}), bf16[32,8,16,256]{3,2,1,0:T(8,128)(2,1)S(1)}, u32[]{:S(2)}, u32[]{:S(2)}) async-start(bf16[32,8,16,256]{3,2,1,0:T(8,128)(2,1)} %fusion.1), calls=%async_computation.1 | async-start | bytes 4194304 | tf_op jit(solution)/shard_map/all_to_all | solution.py:202
  37.0 66.5 %collective-permute-start.4 = (bf16[2,8,2,16,512]{4,3,2,1,0:T(8,128)(2,1)S(1)}, bf16[2,8,2,16,512]{4,3,2,1,0:T(8,128)(2,1)}, u32[]{:S(2)}, u32[]{:S(2)}) collective-permute-start(bf16[2,8,2,16,512]{4,3,2,1,0:T(8,128)(2,1)S(1)} %constant_dynamic-update-slice_fusion.refs_0_), channel_id=1, source_target_pairs={{0,8},{1,9},{2,10},{3,11},{4,12},{5,13},{6,14},{7,15},{8,0},{9,1},... | collective-permute-start | bytes 1572872 | tf_op jit(solution)/shard_map/ppermute | solution.py:129
  39.3 71.4 %collective-permute-start.1 = (bf16[2,8,2,16,512]{4,3,2,1,0:T(8,128)(2,1)S(1)}, bf16[2,8,2,16,512]{4,3,2,1,0:T(8,128)(2,1)}, u32[]{:S(2)}, u32[]{:S(2)}) collective-permute-start(bf16[2,8,2,16,512]{4,3,2,1,0:T(8,128)(2,1)S(1)} %constant_dynamic-update-slice_fusion.refs_0_), channel_id=1, source_target_pairs={{0,6},{1,7},{2,0},{3,1},{4,2},{5,3},{6,4},{7,5},{8,14},{9,15},{10,... | collective-permute-start | bytes 1572872 | tf_op jit(solution)/shard_map/ppermute | solution.py:129
  103.5 18.2 %collective-permute-start.5 = (bf16[2,8,2,16,512]{4,3,2,1,0:T(8,128)(2,1)}, bf16[2,8,2,16,512]{4,3,2,1,0:T(8,128)(2,1)}, u32[]{:S(2)}, u32[]{:S(2)}) collective-permute-start(bf16[2,8,2,16,512]{4,3,2,1,0:T(8,128)(2,1)} %collective-permute-done.4.refs_0_), channel_id=1, source_target_pairs={{0,2},{1,3},{2,4},{3,5},{4,6},{5,7},{6,0},{7,1},{8,10},{9,11},{10,... | collective-permute-start | bytes 1572872 | tf_op jit(solution)/shard_map/ppermute | solution.py:129
  105.5 27.5 %collective-permute-start = (bf16[2,8,2,16,512]{4,3,2,1,0:T(8,128)(2,1)S(1)}, bf16[2,8,2,16,512]{4,3,2,1,0:T(8,128)(2,1)}, u32[]{:S(2)}, u32[]{:S(2)}) collective-permute-start(bf16[2,8,2,16,512]{4,3,2,1,0:T(8,128)(2,1)S(1)} %constant_dynamic-update-slice_fusion.refs_0_), channel_id=1, source_target_pairs={{0,2},{1,3},{2,4},{3,5},{4,6},{5,7},{6,0},{7,1},{8,10},{9,11},{10,... | collective-permute-start | bytes 1572872 | tf_op jit(solution)/shard_map/ppermute | solution.py:129
  110.7 22.2 %collective-permute-start.2 = (bf16[2,8,2,16,512]{4,3,2,1,0:T(8,128)(2,1)}, bf16[2,8,2,16,512]{4,3,2,1,0:T(8,128)(2,1)}, u32[]{:S(2)}, u32[]{:S(2)}) collective-permute-start(bf16[2,8,2,16,512]{4,3,2,1,0:T(8,128)(2,1)} %collective-permute-done.1.refs_3_), channel_id=1, source_target_pairs={{0,6},{1,7},{2,0},{3,1},{4,2},{5,3},{6,4},{7,5},{8,14},{9,15},{10,... | collective-permute-start | bytes 1572872 | tf_op jit(solution)/shard_map/ppermute | solution.py:129
  112.7 25.2 %collective-permute-start.7 = (bf16[2,8,2,16,512]{4,3,2,1,0:T(8,128)(2,1)}, bf16[2,8,2,16,512]{4,3,2,1,0:T(8,128)(2,1)}, u32[]{:S(2)}, u32[]{:S(2)}) collective-permute-start(bf16[2,8,2,16,512]{4,3,2,1,0:T(8,128)(2,1)} %collective-permute-done.4.refs_0_), channel_id=1, source_target_pairs={{0,6},{1,7},{2,0},{3,1},{4,2},{5,3},{6,4},{7,5},{8,14},{9,15},{10,... | collective-permute-start | bytes 1572872 | tf_op jit(solution)/shard_map/ppermute | solution.py:129
  121.7 19.9 %collective-permute-start.6 = (bf16[2,8,2,16,512]{4,3,2,1,0:T(8,128)(2,1)}, bf16[2,8,2,16,512]{4,3,2,1,0:T(8,128)(2,1)}, u32[]{:S(2)}, u32[]{:S(2)}) collective-permute-start(bf16[2,8,2,16,512]{4,3,2,1,0:T(8,128)(2,1)} %collective-permute-done.5.refs_1_), channel_id=1, source_target_pairs={{0,2},{1,3},{2,4},{3,5},{4,6},{5,7},{6,0},{7,1},{8,10},{9,11},{10,... | collective-permute-start | bytes 1572872 | tf_op jit(solution)/shard_map/ppermute | solution.py:129
  135.8 15.2 %copy-start.3 = (bf16[1,2,16,512]{3,2,1,0:T(8,128)(2,1)S(1)}, bf16[1,2,16,512]{3,2,1,0:T(8,128)(2,1)}, u32[]{:S(2)}) copy-start(bf16[1,2,16,512]{3,2,1,0:T(8,128)(2,1)} %param.14) | copy-start | bytes 98308
  135.8 11.0 %collective-permute-start.3 = (bf16[4,2,8,2,16,512]{5,4,3,2,1,0:T(8,128)(2,1)}, bf16[4,2,8,2,16,512]{5,4,3,2,1,0:T(8,128)(2,1)}, u32[]{:S(2)}, u32[]{:S(2)}) collective-permute-start(bf16[4,2,8,2,16,512]{5,4,3,2,1,0:T(8,128)(2,1)} %assemble.2.near), channel_id=1, source_target_pairs={{0,1},{1,0},{2,3},{3,2},{4,5},{5,4},{6,7},{7,6},{8,9},{9,8},{10,11... | collective-permute-start | bytes 6291464 | tf_op jit(solution)/shard_map/ppermute | solution.py:129
  144.6 6.4 %collective-permute-start.8 = (bf16[4,2,8,2,16,512]{5,4,3,2,1,0:T(8,128)(2,1)}, bf16[4,2,8,2,16,512]{5,4,3,2,1,0:T(8,128)(2,1)}, u32[]{:S(2)}, u32[]{:S(2)}) collective-permute-start(bf16[4,2,8,2,16,512]{5,4,3,2,1,0:T(8,128)(2,1)} %assemble.3.far), channel_id=1, source_target_pairs={{0,1},{1,0},{2,3},{3,2},{4,5},{5,4},{6,7},{7,6},{8,9},{9,8},{10,11... | collective-permute-start | bytes 6291464 | tf_op jit(solution)/shard_map/ppermute | solution.py:129
  158.3 4.2 %collective-permute-start.9 = (bf16[8,3,2,16,512]{4,3,2,1,0:T(8,128)(2,1)S(1)}, bf16[8,3,2,16,512]{4,3,2,1,0:T(8,128)(2,1)S(1)}, u32[]{:S(2)}, u32[]{:S(2)}) collective-permute-start(bf16[8,3,2,16,512]{4,3,2,1,0:T(8,128)(2,1)S(1)} %get-tuple-element.13), channel_id=1, source_target_pairs={{0,1},{1,0},{2,3},{3,2},{4,5},{5,4},{6,7},{7,6},{8,9},{9,8},{10,11... | collective-permute-start | bytes 2359304 | tf_op jit(solution)/shard_map/ppermute | solution.py:129

commit v9 on v8

--- a/solution.py
+++ b/solution.py
@@ -47,6 +47,12 @@
     def right(n, b, h):
         return panels[:, :, :, n, b, h].reshape(half, width)
 
+    def wide(b):
+        return jnp.concatenate([left(h, b) for h in range(pieces)], axis=1)
+
+    def tall(n, b):
+        return jnp.concatenate([right(n, b, h) for h in range(pieces)], axis=0)
+
     def arrive(n, b):
         if b % many == 0:
             for copy in copies[n, b // many]:
@@ -55,8 +61,7 @@
     total = jnp.zeros((rows, width), F32)
     for b in range(blocks):
         arrive(0, b)
-        for h in range(pieces):
-            total += dot(left(h, b), right(0, b, h))
+        total += dot(wide(b), tall(0, b))
     column = (-total).astype(BF16)
     at = lax.broadcasted_iota(jnp.int32, (rows, rows), 0)
     of = lax.broadcasted_iota(jnp.int32, (rows, rows), 1)
@@ -73,30 +78,24 @@
     column_out[...] = column_natural.reshape(column_out.shape)
 
     arrive(1, 0)
-    top = [right(1, 0, h) for h in range(pieces)]
+    top = tall(1, 0)
     first = own_first[...].reshape(rows, width)
     second = own_second[...].reshape(rows, width)
     diagonal = pivot[...].reshape(strip * pieces, width)
     parent_sum = dot_rows(first, column_natural)
-    cross = jnp.zeros((rows, width), F32)
-    for h in range(pieces):
-        cross += dot(first[:, h * half : (h + 1) * half], top[h])
+    cross = dot(first, top)
     head_sum = (
         dot_rows(column_kept, second)
         - dot_rows(column_natural, cross.astype(BF16))
         + dot_rows(diagonal, second[: strip * pieces])
     ).astype(BF16)
-    child_sum = jnp.zeros((width, width), F32)
-    for h in range(pieces):
-        child_sum += dot_rows(top[h], head_sum[h * half : (h + 1) * half])
+    child_sum = dot_rows(top, head_sum)
 
     total = jnp.zeros((rows, width), F32)
     for b in range(1, blocks):
         arrive(1, b)
-        for h in range(pieces):
-            total += dot(left(h, kept[b - 1]), right(1, b, h))
-    for h in range(pieces):
-        total += dot(column[:, h * half : (h + 1) * half], top[h])
+        total += dot(wide(kept[b - 1]), tall(1, b))
+    total += dot(column, top)
     child = dot(in_child, (-total).astype(BF16)).astype(BF16)
     child_out[...] = child.reshape(child_out.shape)
     child_sum -= dot_rows(second, child)
@@ -243,13 +242,14 @@
             jax.ShapeDtypeStruct((pieces, strip, width), BF16),
         ),
         in_specs=[
-            pl.BlockSpec(arrived.shape, lambda i: (0, 0, 0, 0, 0)),
+            vmem,
             whole,
             whole,
             pl.BlockSpec(memory_space=pl.ANY),
         ],
         out_specs=(whole, pl.BlockSpec((1, pieces, strip, width), lambda i: (0, 0, 0, 0)), whole),
         input_output_aliases={3: 1},
+        compiler_params=pltpu.CompilerParams(vmem_limit_bytes=8 * 1024 * 1024),
         interpret=INTERPRET,
         name="final",
     )(arrived, pivot_parent[0], pivot_child[0], column_child)

time: 184 us -> 183 us (level)
  transfers between devices with their start and end apart: 12 -> 12, of which waited for: 7 -> 7; matrix products, arithmetic and copies ran while one was open for 1% -> 2% of each run, Pallas kernels for 3% -> 3%
where the time goes in v9:
time: 183 us; the launch traced here: 182 us
  waiting for transfers between devices  92.2 us (50%)
  starting transfers between devices  49 us (27%)
  blocking collectives  18.4 us (10%)
  Pallas kernels  13.7 us (7%)
  local copies, waits for them, and re-layouts  3.06 us (2%)
  matrix products  2.71 us (1%)
  other arithmetic  1.93 us (1%)
    ppermute x10, waiting for transfers between devices, moved(): return lax.ppermute(value, 'proc', pairs)  84.2 us
    ppermute x10, starting transfers between devices, moved(): return lax.ppermute(value, 'proc', pairs)  27.7 us
    all_to_all x1, blocking collectives, per_device(): lax.all_to_all(sums, 'proc', split_axis=0, concat_axis=0, tiled=True, axi...  18.4 us
    all_to_all x1, starting transfers between devices, per_device(): lax.all_to_all(spread.reshape(groups, tops, half), 'group', split_axis=0,...  12.7 us
    all_to_all x1, starting transfers between devices, per_device(): lax.all_to_all(outgoing.reshape(groups, blocks, slabs, half), 'group', sp...  8.59 us
    all_to_all x1, waiting for transfers between devices, per_device(): lax.all_to_all(spread.reshape(groups, tops, half), 'group', split_axis=0,...  7.97 us
    pallas_call x1, Pallas kernels, per_device(): pl.pallas_call(products_kernel, out_shape=(jax.ShapeDtypeStruct((blocks,...  7.21 us
    pallas_call x2, Pallas kernels, gathered(): pl.pallas_call(assemble_kernel, out_shape=jax.ShapeDtypeStruct((XS,) + ro...  5.8 us
  transfers between devices with their start and end apart: 12, of which 7 were waited for; matrix products, arithmetic and copies ran while one was open for 2% of the time, Pallas kernels for 3%

profile of v9, /device:TPU:256, one launch (start us, length us, event | category | flops | bytes accessed | tf_op | source)
XLA Modules:
  0.0 181.9 jit_solution(3991865085307838490)
XLA Ops:
  2.5 12.7 %all-to-all-start = ((bf16[32,16,256]{2,1,0:T(8,128)(2,1)}), bf16[32,16,256]{2,1,0:T(8,128)(2,1)S(1)}, u32[]{:S(2)}, u32[]{:S(2)}) async-start(bf16[32,16,256]{2,1,0:T(8,128)(2,1)} %bitcast.5), calls=%async_computation | async-start | bytes 524288 | tf_op jit(solution)/shard_map/all_to_all | solution.py:190
  17.7 8.0 %all-to-all-done = bf16[32,16,256]{2,1,0:T(8,128)(2,1)S(1)} async-done(((bf16[32,16,256]{2,1,0:T(8,128)(2,1)}), bf16[32,16,256]{2,1,0:T(8,128)(2,1)S(1)}, u32[]{:S(2)}, u32[]{:S(2)}) %all-to-all-start) | async-done | bytes 262176 | tf_op jit(solution)/shard_map/all_to_all | solution.py:190
  25.6 2.7 %fusion.1 = bf16[32,8,16,256]{3,2,1,0:T(8,128)(2,1)} fusion(bf16[512,256,1,1]{1,0,3,2:T(8,128)(2,1)S(1)} %bitcast.32, s32[32,8,16]{2,1,0:T(8,128)S(1)} %copy.19), kind=kOutput, calls=%fused_computation.2 | convolution fusion | flops 1075838976 | bytes 2375680 | tf_op jit(solution)/shard_map/dot_general | solution.py:198
  28.4 8.6 %all-to-all-start.1 = ((bf16[32,8,16,256]{3,2,1,0:T(8,128)(2,1)}), bf16[32,8,16,256]{3,2,1,0:T(8,128)(2,1)S(1)}, u32[]{:S(2)}, u32[]{:S(2)}) async-start(bf16[32,8,16,256]{3,2,1,0:T(8,128)(2,1)} %fusion.1), calls=%async_computation.1 | async-start | bytes 4194304 | tf_op jit(solution)/shard_map/all_to_all | solution.py:201
  37.0 2.3 %collective-permute-start.4 = (bf16[2,8,2,16,512]{4,3,2,1,0:T(8,128)(2,1)S(1)}, bf16[2,8,2,16,512]{4,3,2,1,0:T(8,128)(2,1)}, u32[]{:S(2)}, u32[]{:S(2)}) collective-permute-start(bf16[2,8,2,16,512]{4,3,2,1,0:T(8,128)(2,1)S(1)} %constant_dynamic-update-slice_fusion.refs_0_), channel_id=1, source_target_pairs={{0,8},{1,9},{2,10},{3,11},{4,12},{5,13},{6,14},{7,15},{8,0},{9,1},... | collective-permute-start | bytes 1572872 | tf_op jit(solution)/shard_map/ppermute | solution.py:128
  39.3 4.7 %collective-permute-start.1 = (bf16[2,8,2,16,512]{4,3,2,1,0:T(8,128)(2,1)S(1)}, bf16[2,8,2,16,512]{4,3,2,1,0:T(8,128)(2,1)}, u32[]{:S(2)}, u32[]{:S(2)}) collective-permute-start(bf16[2,8,2,16,512]{4,3,2,1,0:T(8,128)(2,1)S(1)} %constant_dynamic-update-slice_fusion.refs_0_), channel_id=1, source_target_pairs={{0,6},{1,7},{2,0},{3,1},{4,2},{5,3},{6,4},{7,5},{8,14},{9,15},{10,... | collective-permute-start | bytes 1572872 | tf_op jit(solution)/shard_map/ppermute | solution.py:128
  44.0 59.6 %collective-permute-done.4.refs_0_ = bf16[2,8,2,16,512]{4,3,2,1,0:T(8,128)(2,1)} collective-permute-done((bf16[2,8,2,16,512]{4,3,2,1,0:T(8,128)(2,1)S(1)}, bf16[2,8,2,16,512]{4,3,2,1,0:T(8,128)(2,1)}, u32[]{:S(2)}, u32[]{:S(2)}) %collective-permute-start.4) | collective-permute-done | bytes 524320 | tf_op jit(solution)/shard_map/ppermute | solution.py:128
  103.6 1.9 %collective-permute-start.5 = (bf16[2,8,2,16,512]{4,3,2,1,0:T(8,128)(2,1)}, bf16[2,8,2,16,512]{4,3,2,1,0:T(8,128)(2,1)}, u32[]{:S(2)}, u32[]{:S(2)}) collective-permute-start(bf16[2,8,2,16,512]{4,3,2,1,0:T(8,128)(2,1)} %collective-permute-done.4.refs_0_), channel_id=1, source_target_pairs={{0,2},{1,3},{2,4},{3,5},{4,6},{5,7},{6,0},{7,1},{8,10},{9,11},{10,... | collective-permute-start | bytes 1572872 | tf_op jit(solution)/shard_map/ppermute | solution.py:128
  105.5 5.3 %collective-permute-start = (bf16[2,8,2,16,512]{4,3,2,1,0:T(8,128)(2,1)S(1)}, bf16[2,8,2,16,512]{4,3,2,1,0:T(8,128)(2,1)}, u32[]{:S(2)}, u32[]{:S(2)}) collective-permute-start(bf16[2,8,2,16,512]{4,3,2,1,0:T(8,128)(2,1)S(1)} %constant_dynamic-update-slice_fusion.refs_0_), channel_id=1, source_target_pairs={{0,2},{1,3},{2,4},{3,5},{4,6},{5,7},{6,0},{7,1},{8,10},{9,11},{10,... | collective-permute-start | bytes 1572872 | tf_op jit(solution)/shard_map/ppermute | solution.py:128
  110.8 1.9 %collective-permute-start.2 = (bf16[2,8,2,16,512]{4,3,2,1,0:T(8,128)(2,1)}, bf16[2,8,2,16,512]{4,3,2,1,0:T(8,128)(2,1)}, u32[]{:S(2)}, u32[]{:S(2)}) collective-permute-start(bf16[2,8,2,16,512]{4,3,2,1,0:T(8,128)(2,1)} %collective-permute-done.1.refs_3_), channel_id=1, source_target_pairs={{0,6},{1,7},{2,0},{3,1},{4,2},{5,3},{6,4},{7,5},{8,14},{9,15},{10,... | collective-permute-start | bytes 1572872 | tf_op jit(solution)/shard_map/ppermute | solution.py:128
  112.7 3.8 %collective-permute-start.7 = (bf16[2,8,2,16,512]{4,3,2,1,0:T(8,128)(2,1)}, bf16[2,8,2,16,512]{4,3,2,1,0:T(8,128)(2,1)}, u32[]{:S(2)}, u32[]{:S(2)}) collective-permute-start(bf16[2,8,2,16,512]{4,3,2,1,0:T(8,128)(2,1)} %collective-permute-done.4.refs_0_), channel_id=1, source_target_pairs={{0,6},{1,7},{2,0},{3,1},{4,2},{5,3},{6,4},{7,5},{8,14},{9,15},{10,... | collective-permute-start | bytes 1572872 | tf_op jit(solution)/shard_map/ppermute | solution.py:128
  116.5 5.3 %collective-permute-done.5.refs_1_ = bf16[2,8,2,16,512]{4,3,2,1,0:T(8,128)(2,1)} collective-permute-done((bf16[2,8,2,16,512]{4,3,2,1,0:T(8,128)(2,1)}, bf16[2,8,2,16,512]{4,3,2,1,0:T(8,128)(2,1)}, u32[]{:S(2)}, u32[]{:S(2)}) %collective-permute-start.5) | collective-permute-done | bytes 524320 | tf_op jit(solution)/shard_map/ppermute | solution.py:128
  121.8 1.9 %collective-permute-start.6 = (bf16[2,8,2,16,512]{4,3,2,1,0:T(8,128)(2,1)}, bf16[2,8,2,16,512]{4,3,2,1,0:T(8,128)(2,1)}, u32[]{:S(2)}, u32[]{:S(2)}) collective-permute-start(bf16[2,8,2,16,512]{4,3,2,1,0:T(8,128)(2,1)} %collective-permute-done.5.refs_1_), channel_id=1, source_target_pairs={{0,2},{1,3},{2,4},{3,5},{4,6},{5,7},{6,0},{7,1},{8,10},{9,11},{10,... | collective-permute-start | bytes 1572872 | tf_op jit(solution)/shard_map/ppermute | solution.py:128
  123.7 9.3 %collective-permute-done.refs_1_ = bf16[2,8,2,16,512]{4,3,2,1,0:T(8,128)(2,1)} collective-permute-done((bf16[2,8,2,16,512]{4,3,2,1,0:T(8,128)(2,1)S(1)}, bf16[2,8,2,16,512]{4,3,2,1,0:T(8,128)(2,1)}, u32[]{:S(2)}, u32[]{:S(2)}) %collective-permute-start) | collective-permute-done | bytes 524320 | tf_op jit(solution)/shard_map/ppermute | solution.py:128
  133.0 2.8 %assemble.2.near = bf16[4,2,8,2,16,512]{5,4,3,2,1,0:T(8,128)(2,1)} custom-call(s32[1]{0:T(128)} %bitcast.10.place, bf16[2,8,2,16,512]{4,3,2,1,0:T(8,128)(2,1)S(1)} %constant_dynamic-update-slice_fusion.refs_0_, bf16[2,8,2,16,512]{4,3,2,1,0:T(8,128)(2,1)} %collective-permute-done.refs_1_, bf16[2,8,2,16,512]{4,3,2,1,0:T(8,128)(2,1)} %collective-permute-done.2.refs_2_, ...), custom_call_target="tpu_custom_call" | custom-call | tf_op jit(solution)/shard_map/assemble/pallas_call | solution.py:153
  135.8 2.0 %collective-permute-start.3 = (bf16[4,2,8,2,16,512]{5,4,3,2,1,0:T(8,128)(2,1)}, bf16[4,2,8,2,16,512]{5,4,3,2,1,0:T(8,128)(2,1)}, u32[]{:S(2)}, u32[]{:S(2)}) collective-permute-start(bf16[4,2,8,2,16,512]{5,4,3,2,1,0:T(8,128)(2,1)} %assemble.2.near), channel_id=1, source_target_pairs={{0,1},{1,0},{2,3},{3,2},{4,5},{5,4},{6,7},{7,6},{8,9},{9,8},{10,11... | collective-permute-start | bytes 6291464 | tf_op jit(solution)/shard_map/ppermute | solution.py:128
  137.9 3.8 %collective-permute-done.6.refs_2_ = bf16[2,8,2,16,512]{4,3,2,1,0:T(8,128)(2,1)} collective-permute-done((bf16[2,8,2,16,512]{4,3,2,1,0:T(8,128)(2,1)}, bf16[2,8,2,16,512]{4,3,2,1,0:T(8,128)(2,1)}, u32[]{:S(2)}, u32[]{:S(2)}) %collective-permute-start.6) | collective-permute-done | bytes 524320 | tf_op jit(solution)/shard_map/ppermute | solution.py:128
  141.7 3.0 %assemble.3.far = bf16[4,2,8,2,16,512]{5,4,3,2,1,0:T(8,128)(2,1)} custom-call(s32[1]{0:T(128)} %bitcast.10.place, bf16[2,8,2,16,512]{4,3,2,1,0:T(8,128)(2,1)} %collective-permute-done.4.refs_0_, bf16[2,8,2,16,512]{4,3,2,1,0:T(8,128)(2,1)} %collective-permute-done.5.refs_1_, bf16[2,8,2,16,512]{4,3,2,1,0:T(8,128)(2,1)} %collective-permute-done.6.refs_2_, ...), custom_call_target="tpu_custom_call" | custom-call | tf_op jit(solution)/shard_map/assemble/pallas_call | solution.py:153
  144.6 1.9 %collective-permute-start.8 = (bf16[4,2,8,2,16,512]{5,4,3,2,1,0:T(8,128)(2,1)}, bf16[4,2,8,2,16,512]{5,4,3,2,1,0:T(8,128)(2,1)}, u32[]{:S(2)}, u32[]{:S(2)}) collective-permute-start(bf16[4,2,8,2,16,512]{5,4,3,2,1,0:T(8,128)(2,1)} %assemble.3.far), channel_id=1, source_target_pairs={{0,1},{1,0},{2,3},{3,2},{4,5},{5,4},{6,7},{7,6},{8,9},{9,8},{10,11... | collective-permute-start | bytes 6291464 | tf_op jit(solution)/shard_map/ppermute | solution.py:128
  146.8 4.2 %collective-permute-done.8.far_other = bf16[4,2,8,2,16,512]{5,4,3,2,1,0:T(8,128)(2,1)} collective-permute-done((bf16[4,2,8,2,16,512]{5,4,3,2,1,0:T(8,128)(2,1)}, bf16[4,2,8,2,16,512]{5,4,3,2,1,0:T(8,128)(2,1)}, u32[]{:S(2)}, u32[]{:S(2)}) %collective-permute-start.8) | collective-permute-done | bytes 2097184 | tf_op jit(solution)/shard_map/ppermute | solution.py:128
  151.0 7.2 %products.1 = (bf16[8,2,16,512]{3,2,1,0:T(8,128)(2,1)}, bf16[8,2,16,512]{3,2,1,0:T(8,128)(2,1)}, bf16[8,3,2,16,512]{4,3,2,1,0:T(8,128)(2,1)S(1)}, bf16[8,3,2,16,512]{4,3,2,1,0:T(8,128)(2,1)S(1)}) custom-call(s32[9]{0:T(128)S(1)} %pad_add_fusion.kept, bf16[16,2,8,16,256]{4,3,2,1,0:T(8,128)(2,1)S(1)} %bitcast.24, ...), custom_call_target="tpu_custom_call" | custom-call | tf_op jit(solution)/shard_map/products/pallas_call | solution.py:212
  158.3 2.0 %collective-permute-start.9 = (bf16[8,3,2,16,512]{4,3,2,1,0:T(8,128)(2,1)S(1)}, bf16[8,3,2,16,512]{4,3,2,1,0:T(8,128)(2,1)S(1)}, u32[]{:S(2)}, u32[]{:S(2)}) collective-permute-start(bf16[8,3,2,16,512]{4,3,2,1,0:T(8,128)(2,1)S(1)} %get-tuple-element.13), channel_id=1, source_target_pairs={{0,1},{1,0},{2,3},{3,2},{4,5},{5,4},{6,7},{7,6},{8,9},{9,8},{10,11... | collective-permute-start | bytes 2359304 | tf_op jit(solution)/shard_map/ppermute | solution.py:128
  160.3 2.1 %collective-permute-done.9 = bf16[8,3,2,16,512]{4,3,2,1,0:T(8,128)(2,1)S(1)} collective-permute-done((bf16[8,3,2,16,512]{4,3,2,1,0:T(8,128)(2,1)S(1)}, bf16[8,3,2,16,512]{4,3,2,1,0:T(8,128)(2,1)S(1)}, u32[]{:S(2)}, u32[]{:S(2)}) %collective-permute-start.9) | collective-permute-done | bytes 786464 | tf_op jit(solution)/shard_map/ppermute | solution.py:128
  162.8 18.4 %all_to_all.15.arrived = bf16[8,3,2,16,512]{4,3,2,1,0:T(8,128)(2,1)S(1)} all-to-all(bf16[8,3,2,16,512]{4,3,2,1,0:T(8,128)(2,1)S(1)} %add_convert_fusion), channel_id=1, replica_groups={{0,2,4,6,8,10,12,14},{1,3,5,7,9,11,13,15},{16,18,20,22,24,26,28,30},{17..., dimensions={0} | all-to-all | bytes 1572864 | tf_op jit(solution)/shard_map/all_to_all | solution.py:232
  (30 shorter events, 5.7 us)
Async XLA Ops:
  0.6 145.9 %copy-start = (s32[32,7]{0,1:T(8,128)S(1)}, s32[32,7]{0,1:T(8,128)}, u32[]{:S(2)}) copy-start(s32[32,7]{0,1:T(8,128)} %param.11) | copy-start | bytes 2692
  2.5 23.1 %all-to-all-start = ((bf16[32,16,256]{2,1,0:T(8,128)(2,1)}), bf16[32,16,256]{2,1,0:T(8,128)(2,1)S(1)}, u32[]{:S(2)}, u32[]{:S(2)}) async-start(bf16[32,16,256]{2,1,0:T(8,128)(2,1)} %bitcast.5), calls=%async_computation | async-start | bytes 524288 | tf_op jit(solution)/shard_map/all_to_all | solution.py:190
  28.4 8.6 %copy-start.1 = (bf16[1,8,2,16,512]{4,3,2,1,0:T(8,128)(2,1)S(1)}, bf16[1,8,2,16,512]{4,3,2,1,0:T(8,128)(2,1)}, u32[]{:S(2)}) copy-start(bf16[1,8,2,16,512]{4,3,2,1,0:T(8,128)(2,1)} %param.12) | copy-start | bytes 786436
  28.4 8.6 %copy-start.2 = (bf16[1,8,2,16,512]{4,3,2,1,0:T(8,128)(2,1)S(1)}, bf16[1,8,2,16,512]{4,3,2,1,0:T(8,128)(2,1)}, u32[]{:S(2)}) copy-start(bf16[1,8,2,16,512]{4,3,2,1,0:T(8,128)(2,1)} %param.13) | copy-start | bytes 786436
  28.4 122.7 %all-to-all-start.1 = ((bf16[32,8,16,256]{3,2,1,0:T(8,128)(2,1)}), bf16[32,8,16,256]{3,2,1,0:T(8,128)(2,1)S(1)}, u32[]{:S(2)}, u32[]{:S(2)}) async-start(bf16[32,8,16,256]{3,2,1,0:T(8,128)(2,1)} %fusion.1), calls=%async_computation.1 | async-start | bytes 4194304 | tf_op jit(solution)/shard_map/all_to_all | solution.py:201
  37.0 66.5 %collective-permute-start.4 = (bf16[2,8,2,16,512]{4,3,2,1,0:T(8,128)(2,1)S(1)}, bf16[2,8,2,16,512]{4,3,2,1,0:T(8,128)(2,1)}, u32[]{:S(2)}, u32[]{:S(2)}) collective-permute-start(bf16[2,8,2,16,512]{4,3,2,1,0:T(8,128)(2,1)S(1)} %constant_dynamic-update-slice_fusion.refs_0_), channel_id=1, source_target_pairs={{0,8},{1,9},{2,10},{3,11},{4,12},{5,13},{6,14},{7,15},{8,0},{9,1},... | collective-permute-start | bytes 1572872 | tf_op jit(solution)/shard_map/ppermute | solution.py:128
  39.3 71.4 %collective-permute-start.1 = (bf16[2,8,2,16,512]{4,3,2,1,0:T(8,128)(2,1)S(1)}, bf16[2,8,2,16,512]{4,3,2,1,0:T(8,128)(2,1)}, u32[]{:S(2)}, u32[]{:S(2)}) collective-permute-start(bf16[2,8,2,16,512]{4,3,2,1,0:T(8,128)(2,1)S(1)} %constant_dynamic-update-slice_fusion.refs_0_), channel_id=1, source_target_pairs={{0,6},{1,7},{2,0},{3,1},{4,2},{5,3},{6,4},{7,5},{8,14},{9,15},{10,... | collective-permute-start | bytes 1572872 | tf_op jit(solution)/shard_map/ppermute | solution.py:128
  103.6 18.2 %collective-permute-start.5 = (bf16[2,8,2,16,512]{4,3,2,1,0:T(8,128)(2,1)}, bf16[2,8,2,16,512]{4,3,2,1,0:T(8,128)(2,1)}, u32[]{:S(2)}, u32[]{:S(2)}) collective-permute-start(bf16[2,8,2,16,512]{4,3,2,1,0:T(8,128)(2,1)} %collective-permute-done.4.refs_0_), channel_id=1, source_target_pairs={{0,2},{1,3},{2,4},{3,5},{4,6},{5,7},{6,0},{7,1},{8,10},{9,11},{10,... | collective-permute-start | bytes 1572872 | tf_op jit(solution)/shard_map/ppermute | solution.py:128
  105.5 27.5 %collective-permute-start = (bf16[2,8,2,16,512]{4,3,2,1,0:T(8,128)(2,1)S(1)}, bf16[2,8,2,16,512]{4,3,2,1,0:T(8,128)(2,1)}, u32[]{:S(2)}, u32[]{:S(2)}) collective-permute-start(bf16[2,8,2,16,512]{4,3,2,1,0:T(8,128)(2,1)S(1)} %constant_dynamic-update-slice_fusion.refs_0_), channel_id=1, source_target_pairs={{0,2},{1,3},{2,4},{3,5},{4,6},{5,7},{6,0},{7,1},{8,10},{9,11},{10,... | collective-permute-start | bytes 1572872 | tf_op jit(solution)/shard_map/ppermute | solution.py:128
  110.8 22.2 %collective-permute-start.2 = (bf16[2,8,2,16,512]{4,3,2,1,0:T(8,128)(2,1)}, bf16[2,8,2,16,512]{4,3,2,1,0:T(8,128)(2,1)}, u32[]{:S(2)}, u32[]{:S(2)}) collective-permute-start(bf16[2,8,2,16,512]{4,3,2,1,0:T(8,128)(2,1)} %collective-permute-done.1.refs_3_), channel_id=1, source_target_pairs={{0,6},{1,7},{2,0},{3,1},{4,2},{5,3},{6,4},{7,5},{8,14},{9,15},{10,... | collective-permute-start | bytes 1572872 | tf_op jit(solution)/shard_map/ppermute | solution.py:128
  112.7 25.2 %collective-permute-start.7 = (bf16[2,8,2,16,512]{4,3,2,1,0:T(8,128)(2,1)}, bf16[2,8,2,16,512]{4,3,2,1,0:T(8,128)(2,1)}, u32[]{:S(2)}, u32[]{:S(2)}) collective-permute-start(bf16[2,8,2,16,512]{4,3,2,1,0:T(8,128)(2,1)} %collective-permute-done.4.refs_0_), channel_id=1, source_target_pairs={{0,6},{1,7},{2,0},{3,1},{4,2},{5,3},{6,4},{7,5},{8,14},{9,15},{10,... | collective-permute-start | bytes 1572872 | tf_op jit(solution)/shard_map/ppermute | solution.py:128
  121.8 19.9 %collective-permute-start.6 = (bf16[2,8,2,16,512]{4,3,2,1,0:T(8,128)(2,1)}, bf16[2,8,2,16,512]{4,3,2,1,0:T(8,128)(2,1)}, u32[]{:S(2)}, u32[]{:S(2)}) collective-permute-start(bf16[2,8,2,16,512]{4,3,2,1,0:T(8,128)(2,1)} %collective-permute-done.5.refs_1_), channel_id=1, source_target_pairs={{0,2},{1,3},{2,4},{3,5},{4,6},{5,7},{6,0},{7,1},{8,10},{9,11},{10,... | collective-permute-start | bytes 1572872 | tf_op jit(solution)/shard_map/ppermute | solution.py:128
  135.8 15.2 %copy-start.3 = (bf16[1,2,16,512]{3,2,1,0:T(8,128)(2,1)S(1)}, bf16[1,2,16,512]{3,2,1,0:T(8,128)(2,1)}, u32[]{:S(2)}) copy-start(bf16[1,2,16,512]{3,2,1,0:T(8,128)(2,1)} %param.14) | copy-start | bytes 98308
  135.8 11.0 %collective-permute-start.3 = (bf16[4,2,8,2,16,512]{5,4,3,2,1,0:T(8,128)(2,1)}, bf16[4,2,8,2,16,512]{5,4,3,2,1,0:T(8,128)(2,1)}, u32[]{:S(2)}, u32[]{:S(2)}) collective-permute-start(bf16[4,2,8,2,16,512]{5,4,3,2,1,0:T(8,128)(2,1)} %assemble.2.near), channel_id=1, source_target_pairs={{0,1},{1,0},{2,3},{3,2},{4,5},{5,4},{6,7},{7,6},{8,9},{9,8},{10,11... | collective-permute-start | bytes 6291464 | tf_op jit(solution)/shard_map/ppermute | solution.py:128
  144.6 6.4 %collective-permute-start.8 = (bf16[4,2,8,2,16,512]{5,4,3,2,1,0:T(8,128)(2,1)}, bf16[4,2,8,2,16,512]{5,4,3,2,1,0:T(8,128)(2,1)}, u32[]{:S(2)}, u32[]{:S(2)}) collective-permute-start(bf16[4,2,8,2,16,512]{5,4,3,2,1,0:T(8,128)(2,1)} %assemble.3.far), channel_id=1, source_target_pairs={{0,1},{1,0},{2,3},{3,2},{4,5},{5,4},{6,7},{7,6},{8,9},{9,8},{10,11... | collective-permute-start | bytes 6291464 | tf_op jit(solution)/shard_map/ppermute | solution.py:128
  158.3 23.0 %copy-start.4 = (bf16[1,2,16,512]{3,2,1,0:T(8,128)(2,1)S(1)}, bf16[1,2,16,512]{3,2,1,0:T(8,128)(2,1)}, u32[]{:S(2)}) copy-start(bf16[1,2,16,512]{3,2,1,0:T(8,128)(2,1)} %param.15) | copy-start | bytes 98308
  158.3 4.2 %collective-permute-start.9 = (bf16[8,3,2,16,512]{4,3,2,1,0:T(8,128)(2,1)S(1)}, bf16[8,3,2,16,512]{4,3,2,1,0:T(8,128)(2,1)S(1)}, u32[]{:S(2)}, u32[]{:S(2)}) collective-permute-start(bf16[8,3,2,16,512]{4,3,2,1,0:T(8,128)(2,1)S(1)} %get-tuple-element.13), channel_id=1, source_target_pairs={{0,1},{1,0},{2,3},{3,2},{4,5},{5,4},{6,7},{7,6},{8,9},{9,8},{10,11... | collective-permute-start | bytes 2359304 | tf_op jit(solution)/shard_map/ppermute | solution.py:128

commit v10 on v9

--- a/solution.py
+++ b/solution.py
@@ -29,11 +29,12 @@
     rows = strip * slabs
     core, y = kept[blocks - 1], kept[blocks]
     sources = ((near, y, core), (near_other, y, 1 - core), (far, 1 - y, core), (far_other, 1 - y, 1 - core))
-    many = blocks // 2
+    starts = ((0, blocks // 2), (0, blocks - 2))
     copies = {}
     for n in range(2):
         for part in range(2):
-            span = pl.ds(part * many, many)
+            ends = starts[n][1:] + (blocks,)
+            span = pl.ds(starts[n][part], ends[part] - starts[n][part])
             copies[n, part] = [
                 pltpu.make_async_copy(source.at[:, n, span], panels.at[at_y, :, at_core, n, span], sems.at[n, part, k])
                 for k, (source, at_y, at_core) in enumerate(sources)
@@ -54,8 +55,8 @@
         return jnp.concatenate([right(n, b, h) for h in range(pieces)], axis=0)
 
     def arrive(n, b):
-        if b % many == 0:
-            for copy in copies[n, b // many]:
+        if b in starts[n]:
+            for copy in copies[n, starts[n].index(b)]:
                 copy.wait()
 
     total = jnp.zeros((rows, width), F32)

time: 183 us -> 183 us (level)
  no operation moved by 1% of the time
where the time goes in v10:
time: 183 us; the launch traced here: 182 us
  waiting for transfers between devices  92.2 us (50%)
  starting transfers between devices  49 us (27%)
  blocking collectives  18.4 us (10%)
  Pallas kernels  13.7 us (7%)
  local copies, waits for them, and re-layouts  3.06 us (2%)
  matrix products  2.71 us (1%)
  other arithmetic  1.93 us (1%)
    ppermute x10, waiting for transfers between devices, moved(): return lax.ppermute(value, 'proc', pairs)  84.2 us
    ppermute x10, starting transfers between devices, moved(): return lax.ppermute(value, 'proc', pairs)  27.7 us
    all_to_all x1, blocking collectives, per_device(): lax.all_to_all(sums, 'proc', split_axis=0, concat_axis=0, tiled=True, axi...  18.4 us
    all_to_all x1, starting transfers between devices, per_device(): lax.all_to_all(spread.reshape(groups, tops, half), 'group', split_axis=0,...  12.7 us
    all_to_all x1, starting transfers between devices, per_device(): lax.all_to_all(outgoing.reshape(groups, blocks, slabs, half), 'group', sp...  8.59 us
    all_to_all x1, waiting for transfers between devices, per_device(): lax.all_to_all(spread.reshape(groups, tops, half), 'group', split_axis=0,...  7.97 us
    pallas_call x1, Pallas kernels, per_device(): pl.pallas_call(products_kernel, out_shape=(jax.ShapeDtypeStruct((blocks,...  7.21 us
    pallas_call x2, Pallas kernels, gathered(): pl.pallas_call(assemble_kernel, out_shape=jax.ShapeDtypeStruct((XS,) + ro...  5.8 us
  transfers between devices with their start and end apart: 12, of which 7 were waited for; matrix products, arithmetic and copies ran while one was open for 2% of the time, Pallas kernels for 3%

profile of v10, /device:TPU:256, one launch (start us, length us, event | category | flops | bytes accessed | tf_op | source)
XLA Modules:
  0.0 181.9 jit_solution(11533112771435966091)
XLA Ops:
  2.5 12.7 %all-to-all-start = ((bf16[32,16,256]{2,1,0:T(8,128)(2,1)}), bf16[32,16,256]{2,1,0:T(8,128)(2,1)S(1)}, u32[]{:S(2)}, u32[]{:S(2)}) async-start(bf16[32,16,256]{2,1,0:T(8,128)(2,1)} %bitcast.5), calls=%async_computation | async-start | bytes 524288 | tf_op jit(solution)/shard_map/all_to_all | solution.py:191
  17.7 8.0 %all-to-all-done = bf16[32,16,256]{2,1,0:T(8,128)(2,1)S(1)} async-done(((bf16[32,16,256]{2,1,0:T(8,128)(2,1)}), bf16[32,16,256]{2,1,0:T(8,128)(2,1)S(1)}, u32[]{:S(2)}, u32[]{:S(2)}) %all-to-all-start) | async-done | bytes 262176 | tf_op jit(solution)/shard_map/all_to_all | solution.py:191
  25.6 2.7 %fusion.1 = bf16[32,8,16,256]{3,2,1,0:T(8,128)(2,1)} fusion(bf16[512,256,1,1]{1,0,3,2:T(8,128)(2,1)S(1)} %bitcast.32, s32[32,8,16]{2,1,0:T(8,128)S(1)} %copy.19), kind=kOutput, calls=%fused_computation.2 | convolution fusion | flops 1075838976 | bytes 2375680 | tf_op jit(solution)/shard_map/dot_general | solution.py:199
  28.4 8.6 %all-to-all-start.1 = ((bf16[32,8,16,256]{3,2,1,0:T(8,128)(2,1)}), bf16[32,8,16,256]{3,2,1,0:T(8,128)(2,1)S(1)}, u32[]{:S(2)}, u32[]{:S(2)}) async-start(bf16[32,8,16,256]{3,2,1,0:T(8,128)(2,1)} %fusion.1), calls=%async_computation.1 | async-start | bytes 4194304 | tf_op jit(solution)/shard_map/all_to_all | solution.py:202
  37.0 2.3 %collective-permute-start.4 = (bf16[2,8,2,16,512]{4,3,2,1,0:T(8,128)(2,1)S(1)}, bf16[2,8,2,16,512]{4,3,2,1,0:T(8,128)(2,1)}, u32[]{:S(2)}, u32[]{:S(2)}) collective-permute-start(bf16[2,8,2,16,512]{4,3,2,1,0:T(8,128)(2,1)S(1)} %constant_dynamic-update-slice_fusion.refs_0_), channel_id=1, source_target_pairs={{0,8},{1,9},{2,10},{3,11},{4,12},{5,13},{6,14},{7,15},{8,0},{9,1},... | collective-permute-start | bytes 1572872 | tf_op jit(solution)/shard_map/ppermute | solution.py:129
  39.3 4.7 %collective-permute-start.1 = (bf16[2,8,2,16,512]{4,3,2,1,0:T(8,128)(2,1)S(1)}, bf16[2,8,2,16,512]{4,3,2,1,0:T(8,128)(2,1)}, u32[]{:S(2)}, u32[]{:S(2)}) collective-permute-start(bf16[2,8,2,16,512]{4,3,2,1,0:T(8,128)(2,1)S(1)} %constant_dynamic-update-slice_fusion.refs_0_), channel_id=1, source_target_pairs={{0,6},{1,7},{2,0},{3,1},{4,2},{5,3},{6,4},{7,5},{8,14},{9,15},{10,... | collective-permute-start | bytes 1572872 | tf_op jit(solution)/shard_map/ppermute | solution.py:129
  44.0 59.6 %collective-permute-done.4.refs_0_ = bf16[2,8,2,16,512]{4,3,2,1,0:T(8,128)(2,1)} collective-permute-done((bf16[2,8,2,16,512]{4,3,2,1,0:T(8,128)(2,1)S(1)}, bf16[2,8,2,16,512]{4,3,2,1,0:T(8,128)(2,1)}, u32[]{:S(2)}, u32[]{:S(2)}) %collective-permute-start.4) | collective-permute-done | bytes 524320 | tf_op jit(solution)/shard_map/ppermute | solution.py:129
  103.6 1.9 %collective-permute-start.5 = (bf16[2,8,2,16,512]{4,3,2,1,0:T(8,128)(2,1)}, bf16[2,8,2,16,512]{4,3,2,1,0:T(8,128)(2,1)}, u32[]{:S(2)}, u32[]{:S(2)}) collective-permute-start(bf16[2,8,2,16,512]{4,3,2,1,0:T(8,128)(2,1)} %collective-permute-done.4.refs_0_), channel_id=1, source_target_pairs={{0,2},{1,3},{2,4},{3,5},{4,6},{5,7},{6,0},{7,1},{8,10},{9,11},{10,... | collective-permute-start | bytes 1572872 | tf_op jit(solution)/shard_map/ppermute | solution.py:129
  105.5 5.3 %collective-permute-start = (bf16[2,8,2,16,512]{4,3,2,1,0:T(8,128)(2,1)S(1)}, bf16[2,8,2,16,512]{4,3,2,1,0:T(8,128)(2,1)}, u32[]{:S(2)}, u32[]{:S(2)}) collective-permute-start(bf16[2,8,2,16,512]{4,3,2,1,0:T(8,128)(2,1)S(1)} %constant_dynamic-update-slice_fusion.refs_0_), channel_id=1, source_target_pairs={{0,2},{1,3},{2,4},{3,5},{4,6},{5,7},{6,0},{7,1},{8,10},{9,11},{10,... | collective-permute-start | bytes 1572872 | tf_op jit(solution)/shard_map/ppermute | solution.py:129
  110.8 1.9 %collective-permute-start.2 = (bf16[2,8,2,16,512]{4,3,2,1,0:T(8,128)(2,1)}, bf16[2,8,2,16,512]{4,3,2,1,0:T(8,128)(2,1)}, u32[]{:S(2)}, u32[]{:S(2)}) collective-permute-start(bf16[2,8,2,16,512]{4,3,2,1,0:T(8,128)(2,1)} %collective-permute-done.1.refs_3_), channel_id=1, source_target_pairs={{0,6},{1,7},{2,0},{3,1},{4,2},{5,3},{6,4},{7,5},{8,14},{9,15},{10,... | collective-permute-start | bytes 1572872 | tf_op jit(solution)/shard_map/ppermute | solution.py:129
  112.7 3.8 %collective-permute-start.7 = (bf16[2,8,2,16,512]{4,3,2,1,0:T(8,128)(2,1)}, bf16[2,8,2,16,512]{4,3,2,1,0:T(8,128)(2,1)}, u32[]{:S(2)}, u32[]{:S(2)}) collective-permute-start(bf16[2,8,2,16,512]{4,3,2,1,0:T(8,128)(2,1)} %collective-permute-done.4.refs_0_), channel_id=1, source_target_pairs={{0,6},{1,7},{2,0},{3,1},{4,2},{5,3},{6,4},{7,5},{8,14},{9,15},{10,... | collective-permute-start | bytes 1572872 | tf_op jit(solution)/shard_map/ppermute | solution.py:129
  116.5 5.3 %collective-permute-done.5.refs_1_ = bf16[2,8,2,16,512]{4,3,2,1,0:T(8,128)(2,1)} collective-permute-done((bf16[2,8,2,16,512]{4,3,2,1,0:T(8,128)(2,1)}, bf16[2,8,2,16,512]{4,3,2,1,0:T(8,128)(2,1)}, u32[]{:S(2)}, u32[]{:S(2)}) %collective-permute-start.5) | collective-permute-done | bytes 524320 | tf_op jit(solution)/shard_map/ppermute | solution.py:129
  121.8 1.9 %collective-permute-start.6 = (bf16[2,8,2,16,512]{4,3,2,1,0:T(8,128)(2,1)}, bf16[2,8,2,16,512]{4,3,2,1,0:T(8,128)(2,1)}, u32[]{:S(2)}, u32[]{:S(2)}) collective-permute-start(bf16[2,8,2,16,512]{4,3,2,1,0:T(8,128)(2,1)} %collective-permute-done.5.refs_1_), channel_id=1, source_target_pairs={{0,2},{1,3},{2,4},{3,5},{4,6},{5,7},{6,0},{7,1},{8,10},{9,11},{10,... | collective-permute-start | bytes 1572872 | tf_op jit(solution)/shard_map/ppermute | solution.py:129
  123.7 9.3 %collective-permute-done.refs_1_ = bf16[2,8,2,16,512]{4,3,2,1,0:T(8,128)(2,1)} collective-permute-done((bf16[2,8,2,16,512]{4,3,2,1,0:T(8,128)(2,1)S(1)}, bf16[2,8,2,16,512]{4,3,2,1,0:T(8,128)(2,1)}, u32[]{:S(2)}, u32[]{:S(2)}) %collective-permute-start) | collective-permute-done | bytes 524320 | tf_op jit(solution)/shard_map/ppermute | solution.py:129
  133.0 2.8 %assemble.2.near = bf16[4,2,8,2,16,512]{5,4,3,2,1,0:T(8,128)(2,1)} custom-call(s32[1]{0:T(128)} %bitcast.10.place, bf16[2,8,2,16,512]{4,3,2,1,0:T(8,128)(2,1)S(1)} %constant_dynamic-update-slice_fusion.refs_0_, bf16[2,8,2,16,512]{4,3,2,1,0:T(8,128)(2,1)} %collective-permute-done.refs_1_, bf16[2,8,2,16,512]{4,3,2,1,0:T(8,128)(2,1)} %collective-permute-done.2.refs_2_, ...), custom_call_target="tpu_custom_call" | custom-call | tf_op jit(solution)/shard_map/assemble/pallas_call | solution.py:154
  135.8 2.0 %collective-permute-start.3 = (bf16[4,2,8,2,16,512]{5,4,3,2,1,0:T(8,128)(2,1)}, bf16[4,2,8,2,16,512]{5,4,3,2,1,0:T(8,128)(2,1)}, u32[]{:S(2)}, u32[]{:S(2)}) collective-permute-start(bf16[4,2,8,2,16,512]{5,4,3,2,1,0:T(8,128)(2,1)} %assemble.2.near), channel_id=1, source_target_pairs={{0,1},{1,0},{2,3},{3,2},{4,5},{5,4},{6,7},{7,6},{8,9},{9,8},{10,11... | collective-permute-start | bytes 6291464 | tf_op jit(solution)/shard_map/ppermute | solution.py:129
  137.9 3.8 %collective-permute-done.6.refs_2_ = bf16[2,8,2,16,512]{4,3,2,1,0:T(8,128)(2,1)} collective-permute-done((bf16[2,8,2,16,512]{4,3,2,1,0:T(8,128)(2,1)}, bf16[2,8,2,16,512]{4,3,2,1,0:T(8,128)(2,1)}, u32[]{:S(2)}, u32[]{:S(2)}) %collective-permute-start.6) | collective-permute-done | bytes 524320 | tf_op jit(solution)/shard_map/ppermute | solution.py:129
  141.7 3.0 %assemble.3.far = bf16[4,2,8,2,16,512]{5,4,3,2,1,0:T(8,128)(2,1)} custom-call(s32[1]{0:T(128)} %bitcast.10.place, bf16[2,8,2,16,512]{4,3,2,1,0:T(8,128)(2,1)} %collective-permute-done.4.refs_0_, bf16[2,8,2,16,512]{4,3,2,1,0:T(8,128)(2,1)} %collective-permute-done.5.refs_1_, bf16[2,8,2,16,512]{4,3,2,1,0:T(8,128)(2,1)} %collective-permute-done.6.refs_2_, ...), custom_call_target="tpu_custom_call" | custom-call | tf_op jit(solution)/shard_map/assemble/pallas_call | solution.py:154
  144.6 1.9 %collective-permute-start.8 = (bf16[4,2,8,2,16,512]{5,4,3,2,1,0:T(8,128)(2,1)}, bf16[4,2,8,2,16,512]{5,4,3,2,1,0:T(8,128)(2,1)}, u32[]{:S(2)}, u32[]{:S(2)}) collective-permute-start(bf16[4,2,8,2,16,512]{5,4,3,2,1,0:T(8,128)(2,1)} %assemble.3.far), channel_id=1, source_target_pairs={{0,1},{1,0},{2,3},{3,2},{4,5},{5,4},{6,7},{7,6},{8,9},{9,8},{10,11... | collective-permute-start | bytes 6291464 | tf_op jit(solution)/shard_map/ppermute | solution.py:129
  146.8 4.2 %collective-permute-done.8.far_other = bf16[4,2,8,2,16,512]{5,4,3,2,1,0:T(8,128)(2,1)} collective-permute-done((bf16[4,2,8,2,16,512]{5,4,3,2,1,0:T(8,128)(2,1)}, bf16[4,2,8,2,16,512]{5,4,3,2,1,0:T(8,128)(2,1)}, u32[]{:S(2)}, u32[]{:S(2)}) %collective-permute-start.8) | collective-permute-done | bytes 2097184 | tf_op jit(solution)/shard_map/ppermute | solution.py:129
  151.0 7.2 %products.1 = (bf16[8,2,16,512]{3,2,1,0:T(8,128)(2,1)}, bf16[8,2,16,512]{3,2,1,0:T(8,128)(2,1)}, bf16[8,3,2,16,512]{4,3,2,1,0:T(8,128)(2,1)S(1)}, bf16[8,3,2,16,512]{4,3,2,1,0:T(8,128)(2,1)S(1)}) custom-call(s32[9]{0:T(128)S(1)} %pad_add_fusion.kept, bf16[16,2,8,16,256]{4,3,2,1,0:T(8,128)(2,1)S(1)} %bitcast.24, ...), custom_call_target="tpu_custom_call" | custom-call | tf_op jit(solution)/shard_map/products/pallas_call | solution.py:213
  158.3 2.0 %collective-permute-start.9 = (bf16[8,3,2,16,512]{4,3,2,1,0:T(8,128)(2,1)S(1)}, bf16[8,3,2,16,512]{4,3,2,1,0:T(8,128)(2,1)S(1)}, u32[]{:S(2)}, u32[]{:S(2)}) collective-permute-start(bf16[8,3,2,16,512]{4,3,2,1,0:T(8,128)(2,1)S(1)} %get-tuple-element.13), channel_id=1, source_target_pairs={{0,1},{1,0},{2,3},{3,2},{4,5},{5,4},{6,7},{7,6},{8,9},{9,8},{10,11... | collective-permute-start | bytes 2359304 | tf_op jit(solution)/shard_map/ppermute | solution.py:129
  160.3 2.1 %collective-permute-done.9 = bf16[8,3,2,16,512]{4,3,2,1,0:T(8,128)(2,1)S(1)} collective-permute-done((bf16[8,3,2,16,512]{4,3,2,1,0:T(8,128)(2,1)S(1)}, bf16[8,3,2,16,512]{4,3,2,1,0:T(8,128)(2,1)S(1)}, u32[]{:S(2)}, u32[]{:S(2)}) %collective-permute-start.9) | collective-permute-done | bytes 786464 | tf_op jit(solution)/shard_map/ppermute | solution.py:129
  162.8 18.4 %all_to_all.15.arrived = bf16[8,3,2,16,512]{4,3,2,1,0:T(8,128)(2,1)S(1)} all-to-all(bf16[8,3,2,16,512]{4,3,2,1,0:T(8,128)(2,1)S(1)} %add_convert_fusion), channel_id=1, replica_groups={{0,2,4,6,8,10,12,14},{1,3,5,7,9,11,13,15},{16,18,20,22,24,26,28,30},{17..., dimensions={0} | all-to-all | bytes 1572864 | tf_op jit(solution)/shard_map/all_to_all | solution.py:233
  (30 shorter events, 5.7 us)
Async XLA Ops:
  0.6 145.9 %copy-start = (s32[32,7]{0,1:T(8,128)S(1)}, s32[32,7]{0,1:T(8,128)}, u32[]{:S(2)}) copy-start(s32[32,7]{0,1:T(8,128)} %param.11) | copy-start | bytes 2692
  2.5 23.1 %all-to-all-start = ((bf16[32,16,256]{2,1,0:T(8,128)(2,1)}), bf16[32,16,256]{2,1,0:T(8,128)(2,1)S(1)}, u32[]{:S(2)}, u32[]{:S(2)}) async-start(bf16[32,16,256]{2,1,0:T(8,128)(2,1)} %bitcast.5), calls=%async_computation | async-start | bytes 524288 | tf_op jit(solution)/shard_map/all_to_all | solution.py:191
  28.4 8.6 %copy-start.1 = (bf16[1,8,2,16,512]{4,3,2,1,0:T(8,128)(2,1)S(1)}, bf16[1,8,2,16,512]{4,3,2,1,0:T(8,128)(2,1)}, u32[]{:S(2)}) copy-start(bf16[1,8,2,16,512]{4,3,2,1,0:T(8,128)(2,1)} %param.12) | copy-start | bytes 786436
  28.4 8.6 %copy-start.2 = (bf16[1,8,2,16,512]{4,3,2,1,0:T(8,128)(2,1)S(1)}, bf16[1,8,2,16,512]{4,3,2,1,0:T(8,128)(2,1)}, u32[]{:S(2)}) copy-start(bf16[1,8,2,16,512]{4,3,2,1,0:T(8,128)(2,1)} %param.13) | copy-start | bytes 786436
  28.4 122.7 %all-to-all-start.1 = ((bf16[32,8,16,256]{3,2,1,0:T(8,128)(2,1)}), bf16[32,8,16,256]{3,2,1,0:T(8,128)(2,1)S(1)}, u32[]{:S(2)}, u32[]{:S(2)}) async-start(bf16[32,8,16,256]{3,2,1,0:T(8,128)(2,1)} %fusion.1), calls=%async_computation.1 | async-start | bytes 4194304 | tf_op jit(solution)/shard_map/all_to_all | solution.py:202
  37.0 66.5 %collective-permute-start.4 = (bf16[2,8,2,16,512]{4,3,2,1,0:T(8,128)(2,1)S(1)}, bf16[2,8,2,16,512]{4,3,2,1,0:T(8,128)(2,1)}, u32[]{:S(2)}, u32[]{:S(2)}) collective-permute-start(bf16[2,8,2,16,512]{4,3,2,1,0:T(8,128)(2,1)S(1)} %constant_dynamic-update-slice_fusion.refs_0_), channel_id=1, source_target_pairs={{0,8},{1,9},{2,10},{3,11},{4,12},{5,13},{6,14},{7,15},{8,0},{9,1},... | collective-permute-start | bytes 1572872 | tf_op jit(solution)/shard_map/ppermute | solution.py:129
  39.3 71.4 %collective-permute-start.1 = (bf16[2,8,2,16,512]{4,3,2,1,0:T(8,128)(2,1)S(1)}, bf16[2,8,2,16,512]{4,3,2,1,0:T(8,128)(2,1)}, u32[]{:S(2)}, u32[]{:S(2)}) collective-permute-start(bf16[2,8,2,16,512]{4,3,2,1,0:T(8,128)(2,1)S(1)} %constant_dynamic-update-slice_fusion.refs_0_), channel_id=1, source_target_pairs={{0,6},{1,7},{2,0},{3,1},{4,2},{5,3},{6,4},{7,5},{8,14},{9,15},{10,... | collective-permute-start | bytes 1572872 | tf_op jit(solution)/shard_map/ppermute | solution.py:129
  103.6 18.2 %collective-permute-start.5 = (bf16[2,8,2,16,512]{4,3,2,1,0:T(8,128)(2,1)}, bf16[2,8,2,16,512]{4,3,2,1,0:T(8,128)(2,1)}, u32[]{:S(2)}, u32[]{:S(2)}) collective-permute-start(bf16[2,8,2,16,512]{4,3,2,1,0:T(8,128)(2,1)} %collective-permute-done.4.refs_0_), channel_id=1, source_target_pairs={{0,2},{1,3},{2,4},{3,5},{4,6},{5,7},{6,0},{7,1},{8,10},{9,11},{10,... | collective-permute-start | bytes 1572872 | tf_op jit(solution)/shard_map/ppermute | solution.py:129
  105.5 27.5 %collective-permute-start = (bf16[2,8,2,16,512]{4,3,2,1,0:T(8,128)(2,1)S(1)}, bf16[2,8,2,16,512]{4,3,2,1,0:T(8,128)(2,1)}, u32[]{:S(2)}, u32[]{:S(2)}) collective-permute-start(bf16[2,8,2,16,512]{4,3,2,1,0:T(8,128)(2,1)S(1)} %constant_dynamic-update-slice_fusion.refs_0_), channel_id=1, source_target_pairs={{0,2},{1,3},{2,4},{3,5},{4,6},{5,7},{6,0},{7,1},{8,10},{9,11},{10,... | collective-permute-start | bytes 1572872 | tf_op jit(solution)/shard_map/ppermute | solution.py:129
  110.8 22.2 %collective-permute-start.2 = (bf16[2,8,2,16,512]{4,3,2,1,0:T(8,128)(2,1)}, bf16[2,8,2,16,512]{4,3,2,1,0:T(8,128)(2,1)}, u32[]{:S(2)}, u32[]{:S(2)}) collective-permute-start(bf16[2,8,2,16,512]{4,3,2,1,0:T(8,128)(2,1)} %collective-permute-done.1.refs_3_), channel_id=1, source_target_pairs={{0,6},{1,7},{2,0},{3,1},{4,2},{5,3},{6,4},{7,5},{8,14},{9,15},{10,... | collective-permute-start | bytes 1572872 | tf_op jit(solution)/shard_map/ppermute | solution.py:129
  112.7 25.2 %collective-permute-start.7 = (bf16[2,8,2,16,512]{4,3,2,1,0:T(8,128)(2,1)}, bf16[2,8,2,16,512]{4,3,2,1,0:T(8,128)(2,1)}, u32[]{:S(2)}, u32[]{:S(2)}) collective-permute-start(bf16[2,8,2,16,512]{4,3,2,1,0:T(8,128)(2,1)} %collective-permute-done.4.refs_0_), channel_id=1, source_target_pairs={{0,6},{1,7},{2,0},{3,1},{4,2},{5,3},{6,4},{7,5},{8,14},{9,15},{10,... | collective-permute-start | bytes 1572872 | tf_op jit(solution)/shard_map/ppermute | solution.py:129
  121.8 19.9 %collective-permute-start.6 = (bf16[2,8,2,16,512]{4,3,2,1,0:T(8,128)(2,1)}, bf16[2,8,2,16,512]{4,3,2,1,0:T(8,128)(2,1)}, u32[]{:S(2)}, u32[]{:S(2)}) collective-permute-start(bf16[2,8,2,16,512]{4,3,2,1,0:T(8,128)(2,1)} %collective-permute-done.5.refs_1_), channel_id=1, source_target_pairs={{0,2},{1,3},{2,4},{3,5},{4,6},{5,7},{6,0},{7,1},{8,10},{9,11},{10,... | collective-permute-start | bytes 1572872 | tf_op jit(solution)/shard_map/ppermute | solution.py:129
  135.8 15.2 %copy-start.3 = (bf16[1,2,16,512]{3,2,1,0:T(8,128)(2,1)S(1)}, bf16[1,2,16,512]{3,2,1,0:T(8,128)(2,1)}, u32[]{:S(2)}) copy-start(bf16[1,2,16,512]{3,2,1,0:T(8,128)(2,1)} %param.14) | copy-start | bytes 98308
  135.8 11.0 %collective-permute-start.3 = (bf16[4,2,8,2,16,512]{5,4,3,2,1,0:T(8,128)(2,1)}, bf16[4,2,8,2,16,512]{5,4,3,2,1,0:T(8,128)(2,1)}, u32[]{:S(2)}, u32[]{:S(2)}) collective-permute-start(bf16[4,2,8,2,16,512]{5,4,3,2,1,0:T(8,128)(2,1)} %assemble.2.near), channel_id=1, source_target_pairs={{0,1},{1,0},{2,3},{3,2},{4,5},{5,4},{6,7},{7,6},{8,9},{9,8},{10,11... | collective-permute-start | bytes 6291464 | tf_op jit(solution)/shard_map/ppermute | solution.py:129
  144.6 6.4 %collective-permute-start.8 = (bf16[4,2,8,2,16,512]{5,4,3,2,1,0:T(8,128)(2,1)}, bf16[4,2,8,2,16,512]{5,4,3,2,1,0:T(8,128)(2,1)}, u32[]{:S(2)}, u32[]{:S(2)}) collective-permute-start(bf16[4,2,8,2,16,512]{5,4,3,2,1,0:T(8,128)(2,1)} %assemble.3.far), channel_id=1, source_target_pairs={{0,1},{1,0},{2,3},{3,2},{4,5},{5,4},{6,7},{7,6},{8,9},{9,8},{10,11... | collective-permute-start | bytes 6291464 | tf_op jit(solution)/shard_map/ppermute | solution.py:129
  158.3 23.0 %copy-start.4 = (bf16[1,2,16,512]{3,2,1,0:T(8,128)(2,1)S(1)}, bf16[1,2,16,512]{3,2,1,0:T(8,128)(2,1)}, u32[]{:S(2)}) copy-start(bf16[1,2,16,512]{3,2,1,0:T(8,128)(2,1)} %param.15) | copy-start | bytes 98308
  158.3 4.2 %collective-permute-start.9 = (bf16[8,3,2,16,512]{4,3,2,1,0:T(8,128)(2,1)S(1)}, bf16[8,3,2,16,512]{4,3,2,1,0:T(8,128)(2,1)S(1)}, u32[]{:S(2)}, u32[]{:S(2)}) collective-permute-start(bf16[8,3,2,16,512]{4,3,2,1,0:T(8,128)(2,1)S(1)} %get-tuple-element.13), channel_id=1, source_target_pairs={{0,1},{1,0},{2,3},{3,2},{4,5},{5,4},{6,7},{7,6},{8,9},{9,8},{10,11... | collective-permute-start | bytes 2359304 | tf_op jit(solution)/shard_map/ppermute | solution.py:129
